TPU v7x, 32 devices: a whole 2x2x4 slice. The times are simulated.
32 devices in a mesh: leaf: 32 (over z, y, x, core).
Axes of the slice: x: 2, y: 2, z: 4, core: 2. Of those that a mesh axis runs over, the one named last changes fastest.
Arguments:
- points: float32 [131072, 128], P('leaf')
- right_side: float32 [64, 131072], P(None, 'leaf'), may hold values from -6 to 6
- neighbours: int32 [256, 5], P('leaf'), may hold values from -1 to 255, as said below
- leaf_interp: float32 [256, 512, 256], P('leaf'), may hold values from -0.25 to 0.25
- leaf_skeleton: int32 [256, 256], P('leaf'), may hold values from 0 to 511, as said below
- node_skeleton: int32 [254, 256], replicated, may hold values from 0 to 511, as said below
- node_gain: float32 [510, 256], replicated, may hold values from 0.5 to 1.5
- transfer: float32 [7, 2, 256, 256], replicated, may hold values from -0.1875 to 0.1875
Outputs:
- solution: float32 [64, 131072], P(None, 'leaf')
- residual: float32 [64, 131072], P(None, 'leaf')
Inputs may be any that keep to these rules, and one draw needn't show every extreme that they name: `neighbours`: slot s of leaf j holds j + s - 2 or -1, and slot 2 holds j; leaf m stands in leaf j's list exactly when j stands in leaf m's. `leaf_skeleton`: the entries of a row are distinct. `node_skeleton`: the entries of a row are distinct.
All inputs are finite; a program needn't handle non-finite values.
Results may differ from a plain program's by a relative error of at most 0.0003.
Values sent between devices are 32-bit elements; how exact they have to be, the bound alone decides.
No kernel may reach another device: no remote copies, remote signals or barrier semaphores. Data moves between devices by JAX's collectives and lax.ppermute only.
A program may use at most 192 MiB of HBM per device.

v0:
```python
import jax
import jax.numpy as jnp
from jax import lax
from jax.sharding import PartitionSpec as P

ITERS = 2


highest = lax.Precision.HIGHEST
ridge = 1.0


def padded(cells, sides, width):
    for axis, dim in sides:
        count = lax.axis_size(axis)
        ends = count - 1
        head = lax.slice_in_dim(cells, 0, width, axis=dim)
        tail = lax.slice_in_dim(cells, cells.shape[dim] - width, cells.shape[dim], axis=dim)
        cells = jnp.concatenate(
            [
                lax.ppermute(tail, axis, [(i, (i + 1) % count) for i in range(ends)]),
                cells,
                lax.ppermute(head, axis, [((i + 1) % count, i) for i in range(ends)]),
            ],
            axis=dim,
        )
    return cells


def swapped(block, axis, stride):
    count = lax.axis_size(axis)
    route = []
    for low in range(count):
        high = low | 1 << stride
        if high != low and high < count:
            route += [(low, high), (high, low)]
    return lax.ppermute(block, axis, route)


def pair_kernel(first_set, second_set):
    inner = jnp.einsum("nqd,npd->nqp", first_set, second_set, precision=highest)
    first_norm = jnp.sum(first_set * first_set, axis=-1)
    second_norm = jnp.sum(second_set * second_set, axis=-1)
    return jnp.exp((2.0 * inner - first_norm[:, :, None] - second_norm[:, None, :]) * 0.5)


def symmetric(matrix):
    return 0.5 * (matrix + matrix.T)


def chol_apply(matrix, target):
    factor = jnp.linalg.cholesky(matrix)
    return jax.scipy.linalg.cho_solve((factor, True), target)


def body(
    points, right_side, neighbours, leaf_interp, leaf_skeleton, node_skeleton, node_gain, transfer
):
    leaf_count, slot_count = neighbours.shape
    reach = (slot_count - 1) // 2
    leaf_size = leaf_interp.shape[1]
    skel_size = leaf_interp.shape[2]
    coord_dim = points.shape[1]
    classes = right_side.shape[0]
    dev_count = lax.axis_size("leaf")
    dev_levels = dev_count.bit_length() - 1
    local_levels = leaf_count.bit_length() - 1
    levels = local_levels + dev_levels
    leaves = leaf_count * dev_count
    device_index = lax.axis_index("leaf")
    rows_here = leaf_count * leaf_size

    def gain_first(level):
        return 2 * leaves - 2 * (leaves >> level)

    def skel_first(level):
        return leaves - 2 * (leaves >> level)

    own_points = points.reshape(leaf_count, leaf_size, coord_dim)
    extended_points = padded(points, (("leaf", 0),), reach * leaf_size)
    near_mask = (neighbours >= 0).astype(jnp.float32)
    near_tiles = []
    for slot_id in range(slot_count):
        neighbour = extended_points[slot_id * leaf_size : slot_id * leaf_size + rows_here].reshape(
            leaf_count, leaf_size, coord_dim
        )
        near_tiles.append(pair_kernel(neighbour, own_points) * near_mask[:, slot_id, None, None])
    skel_points = jnp.take_along_axis(own_points, leaf_skeleton[:, :, None], axis=1)
    local_far = []
    for level in range(local_levels):
        node_count = leaf_count >> level
        paired = skel_points.reshape(node_count // 2, 2, skel_size, coord_dim)
        sibling = paired[:, ::-1].reshape(node_count, skel_size, coord_dim)
        local_far.append(pair_kernel(sibling, skel_points))
        picked = lax.dynamic_slice_in_dim(
            node_skeleton,
            skel_first(level + 1) + device_index * (node_count // 2),
            node_count // 2,
            0,
        )
        skel_points = jnp.take_along_axis(
            paired.reshape(node_count // 2, 2 * skel_size, coord_dim), picked[:, :, None], axis=1
        )
    own_skel = skel_points[0]
    device_far = []
    for level_bit in range(dev_levels):
        level = local_levels + level_bit
        partner = swapped(own_skel, "leaf", level_bit)
        device_far.append(pair_kernel(partner[None], own_skel[None])[0])
        if level + 1 < levels:
            is_right = device_index >> level_bit & 1
            left_part = jnp.where(is_right == 0, own_skel, partner)
            right_part = jnp.where(is_right == 0, partner, own_skel)
            picked = lax.dynamic_slice_in_dim(
                node_skeleton, skel_first(level + 1) + (device_index >> level_bit + 1), 1, 0
            )[0]
            own_skel = jnp.take(jnp.concatenate([left_part, right_part], axis=0), picked, axis=0)
    solution = jnp.zeros_like(right_side)
    residual = right_side
    direction = right_side
    res_norm = symmetric(lax.psum(jnp.dot(residual, residual.T, precision=highest), "leaf"))
    for step in range(ITERS):
        extended = padded(direction, (("leaf", 1),), reach * leaf_size)
        near = jnp.zeros((classes, leaf_count, leaf_size), jnp.float32)
        for operate_slot_id in range(slot_count):
            shifted = extended[
                :, operate_slot_id * leaf_size : operate_slot_id * leaf_size + rows_here
            ].reshape(classes, leaf_count, leaf_size)
            near = near + jnp.einsum(
                "cnq,nqp->cnp", shifted, near_tiles[operate_slot_id], precision=highest
            )
        by_leaf = direction.reshape(classes, leaf_count, leaf_size)
        weights = jnp.einsum("cnq,nqs->ncs", by_leaf, leaf_interp, precision=highest)
        local_sibling = []
        for operate_level in range(local_levels):
            operate_node_count = leaf_count >> operate_level
            operate_paired = weights.reshape(operate_node_count // 2, 2, classes, skel_size)
            local_sibling.append(
                operate_paired[:, ::-1].reshape(operate_node_count, classes, skel_size)
            )
            node_scale = lax.dynamic_slice_in_dim(
                node_gain,
                gain_first(operate_level) + device_index * operate_node_count,
                operate_node_count,
                0,
            )
            scaled = operate_paired * node_scale.reshape(operate_node_count // 2, 2, 1, skel_size)
            weights = jnp.einsum(
                "ncs,st->nct", scaled[:, 0], transfer[operate_level, 0], precision=highest
            )
            weights = weights + jnp.einsum(
                "ncs,st->nct", scaled[:, 1], transfer[operate_level, 1], precision=highest
            )
        own_node = weights[0]
        device_sibling = []
        all_nodes = lax.all_gather(own_node[None], "leaf", axis=0, tiled=True)
        for operate_level_bit in range(dev_levels):
            operate_level = local_levels + operate_level_bit
            operate_node_count = dev_count >> operate_level_bit
            device_sibling.append(
                lax.dynamic_index_in_dim(
                    all_nodes, device_index >> operate_level_bit ^ 1, 0, keepdims=False
                )
            )
            if operate_level + 1 < levels:
                node_scale = lax.slice_in_dim(
                    node_gain,
                    gain_first(operate_level),
                    gain_first(operate_level) + operate_node_count,
                    axis=0,
                )
                scaled = all_nodes.reshape(
                    operate_node_count // 2, 2, classes, skel_size
                ) * node_scale.reshape(operate_node_count // 2, 2, 1, skel_size)
                all_nodes = jnp.einsum(
                    "ncs,st->nct", scaled[:, 0], transfer[operate_level, 0], precision=highest
                )
                all_nodes = all_nodes + jnp.einsum(
                    "ncs,st->nct", scaled[:, 1], transfer[operate_level, 1], precision=highest
                )
        potential = jnp.dot(device_sibling[-1], device_far[-1], precision=highest)
        for operate_level_bit in range(dev_levels - 2, -1, -1):
            operate_level = local_levels + operate_level_bit
            operate_is_right = device_index >> operate_level_bit & 1
            down_map = jnp.where(
                operate_is_right == 0, transfer[operate_level, 0], transfer[operate_level, 1]
            )
            node_scale = lax.dynamic_index_in_dim(
                node_gain,
                gain_first(operate_level) + (device_index >> operate_level_bit),
                0,
                keepdims=False,
            )
            potential = jnp.dot(potential, down_map.T, precision=highest) * node_scale
            potential = potential + jnp.dot(
                device_sibling[operate_level_bit], device_far[operate_level_bit], precision=highest
            )
        potential = potential[None]
        for operate_level in range(local_levels - 1, -1, -1):
            operate_node_count = leaf_count >> operate_level
            children = jnp.stack(
                [
                    jnp.einsum(
                        "nct,st->ncs", potential, transfer[operate_level, 0], precision=highest
                    ),
                    jnp.einsum(
                        "nct,st->ncs", potential, transfer[operate_level, 1], precision=highest
                    ),
                ],
                axis=1,
            )
            node_scale = lax.dynamic_slice_in_dim(
                node_gain,
                gain_first(operate_level) + device_index * operate_node_count,
                operate_node_count,
                0,
            )
            children = (
                children.reshape(operate_node_count, classes, skel_size) * node_scale[:, None, :]
            )
            potential = children + jnp.einsum(
                "ncs,nst->nct",
                local_sibling[operate_level],
                local_far[operate_level],
                precision=highest,
            )
        far = jnp.einsum("ncs,nqs->cnq", potential, leaf_interp, precision=highest)
        image = (
            ridge * direction + near.reshape(classes, rows_here) + far.reshape(classes, rows_here)
        )
        curvature = symmetric(lax.psum(jnp.dot(direction, image.T, precision=highest), "leaf"))
        alpha_mat = chol_apply(curvature, res_norm)
        solution = solution + jnp.dot(alpha_mat.T, direction, precision=highest)
        residual = residual - jnp.dot(alpha_mat.T, image, precision=highest)
        if step + 1 < ITERS:
            new_norm = symmetric(lax.psum(jnp.dot(residual, residual.T, precision=highest), "leaf"))
            beta_mat = chol_apply(res_norm, new_norm)
            direction = residual + jnp.dot(beta_mat.T, direction, precision=highest)
            res_norm = new_norm
    return (solution, residual)


def solution(mesh):
    placed = (
        P("leaf", None),
        P(None, "leaf"),
        P("leaf", None),
        P("leaf", None, None),
        P("leaf", None),
        P(),
        P(),
        P(),
    )
    return jax.shard_map(
        body,
        mesh=mesh,
        in_specs=placed,
        out_specs=(P(None, "leaf"), P(None, "leaf")),
        check_vma=False,
    )
```

profile of v0, /device:TPU:0, one launch (start us, length us, event | category | flops | bytes accessed | tf_op | source)
XLA Modules:
  0.0 585.5 jit_solution(3936154865233572906)
XLA Ops:
  12.3 22.2 %gather_fusion.1 = f32[2048,128]{1,0:T(8,128)S(1)} fusion(f32[8,512,128]{2,1,0:T(8,128)} %bitcast.587, s32[2048]{0:T(1024)S(1)} %bitcast.593), kind=kCustom, calls=%fused_computation.5 | custom fusion | bytes 2113536 | tf_op jit(solution)/shard_map/jit(take_along_axis)/gather | solution.py:88
  35.0 11.5 %gather_fusion.2 = f32[1024,128]{1,0:T(8,128)} fusion(f32[4,512,128]{2,1,0:T(8,128)S(1)} %broadcast_select_fusion.1, s32[1024]{0:T(1024)S(1)} %bitcast.596), kind=kCustom, calls=%fused_computation.6 | custom fusion | bytes 1056768 | tf_op jit(solution)/shard_map/jit(take_along_axis)/gather | solution.py:101
  47.8 3.7 gather_fusion.3
  54.8 4.9 fusion.115
  74.8 2.7 collective-permute-start
  78.4 4.4 collective-permute-start.1
  98.2 2.5 broadcast_select_fusion
  100.8 2.3 rev.24
  104.7 8.9 %fusion.328 = f32[8,512,512]{2,1,0:T(8,128)} fusion(f32[8,512,128]{2,1,0:T(8,128)S(1)} %bitcast.588), kind=kOutput, calls=%fused_computation.579 | convolution fusion | flops 3221225472 | bytes 10485760 | tf_op jit(solution)/shard_map/nqd,npd->nqp/dot_general | solution.py:41
  121.5 2.5 multiply_reduce_fusion.5
  125.5 2.6 fusion.77
  128.1 3.5 fusion.63
  131.6 4.7 multiply_exponential_fusion
  152.6 3.4 collective-permute-start.5
  163.7 2.5 collective-permute-start.6
  177.8 2.1 fusion.93
  185.1 2.5 collective-permute-start.8
  192.4 8.9 %fusion.326 = f32[8,512,512]{2,1,0:T(8,128)} fusion(f32[8,512,128]{2,1,0:T(8,128)S(1)} %bitcast.630, f32[8,512,128]{2,1,0:T(8,128)S(1)} %bitcast.589), kind=kOutput, calls=%fused_computation.577 | convolution fusion | flops 3221225472 | bytes 12582912 | tf_op jit(solution)/shard_map/nqd,npd->nqp/dot_general | solution.py:41
  201.4 10.4 %fusion.327 = f32[8,512,512]{2,1,0:T(8,128)} fusion(f32[8,512,128]{2,1,0:T(8,128)} %bitcast.628, f32[8,512,128]{2,1,0:T(8,128)S(1)} %bitcast.590), kind=kOutput, calls=%fused_computation.578 | convolution fusion | flops 3221225472 | bytes 12582912 | tf_op jit(solution)/shard_map/nqd,npd->nqp/dot_general | solution.py:41
  214.7 8.8 %fusion.329 = f32[8,512,512]{2,1,0:T(8,128)} fusion(f32[8,512,128]{2,1,0:T(8,128)S(1)} %bitcast.631, f32[8,512,128]{2,1,0:T(8,128)S(1)} %bitcast.591), kind=kOutput, calls=%fused_computation.580 | convolution fusion | flops 3221225472 | bytes 12582912 | tf_op jit(solution)/shard_map/nqd,npd->nqp/dot_general | solution.py:41
  224.1 10.0 %fusion.1 = f32[8,512,64]{1,2,0:T(8,128)S(1)} fusion(f32[8,512,512]{2,1,0:T(8,128)} %fusion.326, f32[8]{0:T(128)S(1)} %copy-done.121, f32[8,512]{1,0:T(8,128)S(1)} %sub.233, f32[8,512]{1,0:T(8,128)S(1)} %sub.230, f32[8,8,8,512]{3,2,1,0:T(8,128)} %bitcast.659), kind=kOutput, calls=%fused_computation.14 | convolution fusion | flops 1621098496 | bytes 10518560 | tf_op jit(solution)/shard_map/cnq,nqp->cnp/dot_general | solution.py:129
  234.2 9.2 %fusion.330 = f32[8,512,512]{2,1,0:T(8,128)} fusion(f32[8,512,128]{2,1,0:T(8,128)S(1)} %bitcast.629, f32[8,512,128]{2,1,0:T(8,128)S(1)} %bitcast.592), kind=kOutput, calls=%fused_computation.581 | convolution fusion | flops 3221225472 | bytes 12582912 | tf_op jit(solution)/shard_map/nqd,npd->nqp/dot_general | solution.py:41
  243.5 9.9 %fusion.72 = f32[8,512,64]{1,2,0:T(8,128)S(1)} fusion(f32[8,512,64]{1,2,0:T(8,128)S(1)} %fusion.1, f32[8,512,512]{2,1,0:T(8,128)} %fusion.327, f32[8]{0:T(128)S(1)} %copy-done.119, f32[8,512]{1,0:T(8,128)S(1)} %sub.236, f32[8,512]{1,0:T(8,128)S(1)} %sub.233, f32[8,8,8,512]{3,2,1,0:T(8,128)S(1)} %bitcast.657), kind=kOutput, calls=%fused_computation.102 | convolution fusion | flops 1621360640 | bytes 11567136 | tf_op jit(solution)/shard_map/cnq,nqp->cnp/dot_general | solution.py:129
  253.5 8.0 %fusion.70 = f32[8,512,64]{1,2,0:T(8,128)S(1)} fusion(f32[8,512,64]{1,2,0:T(8,128)S(1)} %fusion.72, f32[8,512,512]{2,1,0:T(8,128)S(1)} %bitcast.617, f32[8]{0:T(128)S(1)} %copy-done.117, f32[8,512]{1,0:T(8,128)S(1)} %sub.233, f32[8,8,8,512]{3,2,1,0:T(8,128)S(1)} %bitcast.595), kind=kOutput, calls=%fused_computation.100 | convolution fusion | flops 1621360640 | bytes 11550752 | tf_op jit(solution)/shard_map/cnq,nqp->cnp/dot_general | solution.py:129
  261.6 8.0 %fusion.68 = f32[8,512,64]{1,2,0:T(8,128)S(1)} fusion(f32[8,512,64]{1,2,0:T(8,128)S(1)} %fusion.70, f32[8,512,512]{2,1,0:T(8,128)S(1)} %bitcast.623, f32[8]{0:T(128)S(1)} %copy-done.115, f32[8,512]{1,0:T(8,128)S(1)} %sub.243, f32[8,512]{1,0:T(8,128)S(1)} %sub.233, f32[8,8,8,512]{3,2,1,0:T(8,128)S(1)} %bitcast.660), kind=kOutput, calls=%fused_computation.98 | convolution fusion | flops 1621360640 | bytes 11567136 | tf_op jit(solution)/shard_map/cnq,nqp->cnp/dot_general | solution.py:129
  269.7 10.0 %fusion.65 = f32[8,8,8,512]{3,2,1,0:T(8,128)S(1)} fusion(f32[8,512,64]{1,2,0:T(8,128)S(1)} %fusion.68, f32[8,512,512]{2,1,0:T(8,128)} %fusion.330, f32[8]{0:T(128)S(1)} %copy-done.113, f32[8,512]{1,0:T(8,128)S(1)} %copy-done.90, f32[8,512]{1,0:T(8,128)} %copy-done.84, f32[8,8,8,512]{3,2,1,0:T(8,128)S(1)} %bitcast.658), kind=kOutput, calls=%fused_computation.95 | convolution fusion | flops 1621360640 | bytes 11567136 | tf_op jit(solution)/shard_map/cnq,nqp->cnp/dot_general | solution.py:129
  299.8 4.4 convolution_bitcast_fusion.1
  306.3 39.8 %all-reduce = (f32[64,64]{1,0:T(8,128)S(1)}, f32[64,64]{1,0:T(8,128)S(1)}) all-reduce(f32[64,64]{1,0:T(8,128)S(1)} %copy-done.59, f32[64,64]{1,0:T(8,128)S(1)} %convolution_bitcast_fusion.14), channel_id=1, replica_groups=mesh['leaf'=32] {'leaf'}, use_global_device_ids=true, to_apply=%region_24.27 | all-reduce | flops 8192 | bytes 65536 | tf_op jit(solution)/shard_map/psum | solution.py:121
  346.3 5.8 cholesky.70
  353.5 5.5 custom-call.16
  359.3 5.8 cholesky.59
  366.5 4.9 custom-call.15
  371.9 2.3 convolution_subtract_fusion.1
  375.1 40.3 %psum.30 = f32[64,64]{1,0:T(8,128)S(1)} all-reduce(f32[64,64]{1,0:T(8,128)S(1)} %fusion.333), channel_id=1, replica_groups=mesh['leaf'=32] {'leaf'}, use_global_device_ids=true, to_apply=%region_25.29 | all-reduce | flops 4096 | bytes 32768 | tf_op jit(solution)/shard_map/psum | solution.py:236
  418.2 2.7 fusion.104
  433.9 3.7 collective-permute-start.9
  440.8 2.8 fusion.332
  443.5 2.8 pad_maximum_fusion
  446.4 10.9 %fusion = f32[8,512,64]{1,2,0:T(8,128)} fusion(f32[8,512,512]{2,1,0:T(8,128)} %fusion.326, f32[8]{0:T(128)S(1)} %copy-done.122, f32[8,512]{1,0:T(8,128)S(1)} %copy-done.85, f32[8,512]{1,0:T(8,128)S(1)} %copy-done.89, f32[8,8,8,512]{3,2,1,0:T(8,128)S(1)} %bitcast.664), kind=kOutput, calls=%fused_computation.13 | convolution fusion | flops 1621098496 | bytes 10518560 | tf_op jit(solution)/shard_map/cnq,nqp->cnp/dot_general | solution.py:129
  457.3 9.7 %fusion.73 = f32[8,512,64]{1,2,0:T(8,128)} fusion(f32[8,512,64]{1,2,0:T(8,128)} %fusion, f32[8,512,512]{2,1,0:T(8,128)S(1)} %bitcast.621, f32[8]{0:T(128)S(1)} %copy-done.120, f32[8,512]{1,0:T(8,128)S(1)} %copy-done.87, f32[8,512]{1,0:T(8,128)S(1)} %copy-done.85, f32[8,8,8,512]{3,2,1,0:T(8,128)} %bitcast.663), kind=kOutput, calls=%fused_computation.103 | convolution fusion | flops 1621360640 | bytes 11567136 | tf_op jit(solution)/shard_map/cnq,nqp->cnp/dot_general | solution.py:129
  467.1 9.8 %fusion.71 = f32[8,512,64]{1,2,0:T(8,128)} fusion(f32[8,512,64]{1,2,0:T(8,128)} %fusion.73, f32[8,512,512]{2,1,0:T(8,128)S(1)} %bitcast.619, f32[8]{0:T(128)S(1)} %copy-done.118, f32[8,512]{1,0:T(8,128)S(1)} %copy-done.85, f32[8,8,8,512]{3,2,1,0:T(8,128)S(1)} %bitcast.598), kind=kOutput, calls=%fused_computation.101 | convolution fusion | flops 1621360640 | bytes 11550752 | tf_op jit(solution)/shard_map/cnq,nqp->cnp/dot_general | solution.py:129
  477.0 9.1 %fusion.69 = f32[8,512,64]{1,2,0:T(8,128)S(1)} fusion(f32[8,512,64]{1,2,0:T(8,128)} %fusion.71, f32[8,512,512]{2,1,0:T(8,128)S(1)} %bitcast.625, f32[8]{0:T(128)S(1)} %copy-done.116, f32[8,512]{1,0:T(8,128)S(1)} %copy-done.93, f32[8,512]{1,0:T(8,128)S(1)} %copy-done.85, f32[8,8,8,512]{3,2,1,0:T(8,128)S(1)} %bitcast.662), kind=kOutput, calls=%fused_computation.99 | convolution fusion | flops 1621360640 | bytes 11567136 | tf_op jit(solution)/shard_map/cnq,nqp->cnp/dot_general | solution.py:129
  486.1 8.2 %fusion.67 = f32[8,8,8,512]{3,2,1,0:T(8,128)S(1)} fusion(f32[8,512,64]{1,2,0:T(8,128)S(1)} %fusion.69, f32[8,512,512]{2,1,0:T(8,128)S(1)} %bitcast.627, f32[8]{0:T(128)S(1)} %copy-done.114, f32[8,512]{1,0:T(8,128)S(1)} %copy-done.91, f32[8,512]{1,0:T(8,128)S(1)} %copy-done.85, f32[8,8,8,512]{3,2,1,0:T(8,128)S(1)} %bitcast.661), kind=kOutput, calls=%fused_computation.97 | convolution fusion | flops 1621360640 | bytes 11567136 | tf_op jit(solution)/shard_map/cnq,nqp->cnp/dot_general | solution.py:129
  514.3 4.4 convolution_bitcast_fusion
  520.8 39.4 %psum.31 = f32[64,64]{1,0:T(8,128)S(1)} all-reduce(f32[64,64]{1,0:T(8,128)S(1)} %fusion.134), channel_id=1, replica_groups=mesh['leaf'=32] {'leaf'}, use_global_device_ids=true, to_apply=%region_26.30 | all-reduce | flops 4096 | bytes 32768 | tf_op jit(solution)/shard_map/psum | solution.py:231
  560.4 5.8 cholesky.81
  567.6 4.9 custom-call.17
  573.0 3.2 convolution_subtract_fusion
  (536 shorter events, 171.8 us)
Async XLA Ops:
  7.2 275.6 %all-gather.5.cloned.1.call-start = ((), (), s32[]{:S(2)}) async-start(), calls=%async_computation | async-start | bytes 2162688 | tf_op jit(solution)/shard_map/all_gather | solution.py:156
  8.6 112.9 %copy-start.77 = (pred[8,256]{1,0:T(8,128)(4,1)}, pred[8,256]{1,0:T(8,128)(4,1)S(1)}, u32[]{:S(2)}) copy-start(pred[8,256]{1,0:T(8,128)(4,1)S(1)} %compare_and_fusion) | copy-start | bytes 6148
  10.1 82.4 %copy-start.82 = (pred[4,256]{1,0:T(4,128)(4,1)}, pred[4,256]{1,0:T(4,128)(4,1)S(1)}, u32[]{:S(2)}) copy-start(pred[4,256]{1,0:T(4,128)(4,1)S(1)} %compare_and_fusion.1) | copy-start | bytes 3076
  11.5 23.1 %copy-start.108 = (pred[2,256]{1,0:T(4,128)(4,1)}, pred[2,256]{1,0:T(4,128)(4,1)S(1)}, u32[]{:S(2)}) copy-start(pred[2,256]{1,0:T(4,128)(4,1)S(1)} %compare_and_fusion.2) | copy-start | bytes 1540
  12.3 40.1 %copy-start.102 = (pred[256]{0:T(512)(128)(4,1)}, pred[256]{0:T(512)(128)(4,1)S(1)}, u32[]{:S(2)}) copy-start(pred[256]{0:T(512)(128)(4,1)S(1)} %compare_and_fusion.7) | copy-start | bytes 772
  34.6 11.9 %copy-start.7 = (f32[2048,128]{1,0:T(8,128)}, f32[2048,128]{1,0:T(8,128)S(1)}, u32[]{:S(2)}) copy-start(f32[2048,128]{1,0:T(8,128)S(1)} %gather_fusion.1) | copy-start | bytes 3145732
  53.1 94.7 %collective-permute-start.4 = (f32[256,128]{1,0:T(8,128)}, f32[256,128]{1,0:T(8,128)}, u32[]{:S(2)}, u32[]{:S(2)}) collective-permute-start(f32[256,128]{1,0:T(8,128)} %broadcast_select_fusion.9), channel_id=1, source_target_pairs={{0,1},{1,0},{2,3},{3,2},{4,5},{5,4},{6,7},{7,6},{8,9},{9,8},{10,11... | collective-permute-start | bytes 393224 | tf_op jit(solution)/shard_map/ppermute | solution.py:37
  59.7 14.0 %copy-start = (f32[4096,128]{1,0:T(8,128)S(1)}, f32[4096,128]{1,0:T(8,128)}, u32[]{:S(2)}) copy-start(f32[4096,128]{1,0:T(8,128)} %param.13) | copy-start | bytes 6291460
  63.3 26.6 %copy-start.34 = (f32[4,64,256]{2,1,0:T(8,128)}, f32[4,64,256]{2,1,0:T(8,128)S(1)}, u32[]{:S(2)}) copy-start(f32[4,64,256]{2,1,0:T(8,128)S(1)} %convolution_add_fusion.11) | copy-start | bytes 786436
  64.7 27.7 %copy-start.68 = (f32[4,256]{1,0:T(4,128)}, f32[4,256]{1,0:T(4,128)S(1)}, u32[]{:S(2)}) copy-start(f32[4,256]{1,0:T(4,128)S(1)} %get-tuple-element.58) | copy-start | bytes 12292
  73.7 423.6 %all-gather.7.cloned.1.call-start = ((), (), s32[]{:S(2)}) async-start(), calls=%async_computation.1 | async-start | bytes 2162688 | tf_op jit(solution)/shard_map/all_gather | solution.py:156
  74.8 112.8 %collective-permute-start = (f32[1024,128]{1,0:T(8,128)}, f32[1024,128]{1,0:T(8,128)}, u32[]{:S(2)}, u32[]{:S(2)}) collective-permute-start(f32[1024,128]{1,0:T(8,128)} %get-tuple-element.33), channel_id=1, source_target_pairs={{0,1},{1,2},{2,3},{3,4},{4,5},{5,6},{6,7},{7,8},{8,9},{9,10},{10,1... | collective-permute-start | bytes 1572872 | tf_op jit(solution)/shard_map/ppermute | solution.py:21
  78.4 87.7 %collective-permute-start.1 = (f32[64,1024]{1,0:T(8,128)}, f32[64,1024]{1,0:T(8,128)}, u32[]{:S(2)}, u32[]{:S(2)}) collective-permute-start(f32[64,1024]{1,0:T(8,128)} %get-tuple-element.50), channel_id=1, source_target_pairs={{0,1},{1,2},{2,3},{3,4},{4,5},{5,6},{6,7},{7,8},{8,9},{9,10},{10,1... | collective-permute-start | bytes 786440 | tf_op jit(solution)/shard_map/ppermute | solution.py:21
  82.8 129.0 %collective-permute-start.2 = (f32[1024,128]{1,0:T(8,128)}, f32[1024,128]{1,0:T(8,128)}, u32[]{:S(2)}, u32[]{:S(2)}) collective-permute-start(f32[1024,128]{1,0:T(8,128)} %get-tuple-element.32), channel_id=1, source_target_pairs={{1,0},{2,1},{3,2},{4,3},{5,4},{6,5},{7,6},{8,7},{9,8},{10,9},{11,1... | collective-permute-start | bytes 1572872 | tf_op jit(solution)/shard_map/ppermute | solution.py:23
  84.1 84.8 %collective-permute-start.3 = (f32[64,1024]{1,0:T(8,128)}, f32[64,1024]{1,0:T(8,128)}, u32[]{:S(2)}, u32[]{:S(2)}) collective-permute-start(f32[64,1024]{1,0:T(8,128)} %get-tuple-element.49), channel_id=1, source_target_pairs={{1,0},{2,1},{3,2},{4,3},{5,4},{6,5},{7,6},{8,7},{9,8},{10,9},{11,1... | collective-permute-start | bytes 786440 | tf_op jit(solution)/shard_map/ppermute | solution.py:23
  104.7 11.2 %copy-start.110 = (s32[256]{0:T(256)S(1)}, s32[256]{0:T(256)}, u32[]{:S(2)}) copy-start(s32[256]{0:T(256)} %compare_select_fusion.6) | copy-start | bytes 3076
  104.7 11.7 %copy-start.111 = (s32[256]{0:T(256)S(1)}, s32[256]{0:T(256)}, u32[]{:S(2)}) copy-start(s32[256]{0:T(256)} %compare_select_fusion.5) | copy-start | bytes 3076
  104.7 12.3 %copy-start.112 = (s32[256]{0:T(256)S(1)}, s32[256]{0:T(256)}, u32[]{:S(2)}) copy-start(s32[256]{0:T(256)} %compare_select_fusion.4) | copy-start | bytes 3076
  104.7 14.2 %copy-start.83 = (pred[4,256]{1,0:T(4,128)(4,1)S(1)}, pred[4,256]{1,0:T(4,128)(4,1)}, u32[]{:S(2)}) copy-start(pred[4,256]{1,0:T(4,128)(4,1)} %copy-done.82) | copy-start | bytes 3076
  125.5 10.8 %copy-start.72 = (f32[510,256]{1,0:T(8,128)S(1)}, f32[510,256]{1,0:T(8,128)}, u32[]{:S(2)}) copy-start(f32[510,256]{1,0:T(8,128)} %param.19) | copy-start | bytes 1566724
  128.1 11.7 %copy-start.35 = (f32[4,64,256]{2,1,0:T(8,128)S(1)}, f32[4,64,256]{2,1,0:T(8,128)}, u32[]{:S(2)}) copy-start(f32[4,64,256]{2,1,0:T(8,128)} %copy-done.34) | copy-start | bytes 786436
  131.5 12.2 %slice-start.12 = ((f32[510,256]{1,0:T(8,128)}), f32[16,256]{1,0:T(8,128)S(1)}, s32[]{:S(2)}) async-start(f32[510,256]{1,0:T(8,128)} %param.19), calls=%async_computation.14 | async-start | bytes 32768 | tf_op jit(solution)/shard_map/slice | solution.py:166
  152.6 7.1 %collective-permute-start.5 = (f32[256,128]{1,0:T(8,128)S(1)}, f32[256,128]{1,0:T(8,128)S(1)}, u32[]{:S(2)}, u32[]{:S(2)}) collective-permute-start(f32[256,128]{1,0:T(8,128)S(1)} %get-tuple-element.19), channel_id=1, source_target_pairs={{0,2},{2,0},{1,3},{3,1},{4,6},{6,4},{5,7},{7,5},{8,10},{10,8},{9,1... | collective-permute-start | bytes 393224 | tf_op jit(solution)/shard_map/ppermute | solution.py:37
  163.7 8.8 %collective-permute-start.6 = (f32[256,128]{1,0:T(8,128)S(1)}, f32[256,128]{1,0:T(8,128)S(1)}, u32[]{:S(2)}, u32[]{:S(2)}) collective-permute-start(f32[256,128]{1,0:T(8,128)S(1)} %get-tuple-element.21), channel_id=1, source_target_pairs={{0,4},{4,0},{1,5},{5,1},{2,6},{6,2},{3,7},{7,3},{8,12},{12,8},{9,1... | collective-permute-start | bytes 393224 | tf_op jit(solution)/shard_map/ppermute | solution.py:37
  176.3 5.0 collective-permute-start.7
  185.1 95.1 %collective-permute-start.8 = (f32[256,128]{1,0:T(8,128)S(1)}, f32[256,128]{1,0:T(8,128)}, u32[]{:S(2)}, u32[]{:S(2)}) collective-permute-start(f32[256,128]{1,0:T(8,128)S(1)} %get-tuple-element.25), channel_id=1, source_target_pairs={{0,16},{16,0},{1,17},{17,1},{2,18},{18,2},{3,19},{19,3},{4,20},{20... | collective-permute-start | bytes 393224 | tf_op jit(solution)/shard_map/ppermute | solution.py:37
  201.3 60.2 %copy-start.84 = (f32[8,512]{1,0:T(8,128)}, f32[8,512]{1,0:T(8,128)S(1)}, u32[]{:S(2)}) copy-start(f32[8,512]{1,0:T(8,128)S(1)} %sub.233) | copy-start | bytes 49156
  201.3 22.8 %copy-start.88 = (f32[8,512]{1,0:T(8,128)}, f32[8,512]{1,0:T(8,128)S(1)}, u32[]{:S(2)}) copy-start(f32[8,512]{1,0:T(8,128)S(1)} %sub.230) | copy-start | bytes 49156
  201.3 42.1 %copy-start.86 = (f32[8,512]{1,0:T(8,128)}, f32[8,512]{1,0:T(8,128)S(1)}, u32[]{:S(2)}) copy-start(f32[8,512]{1,0:T(8,128)S(1)} %sub.236) | copy-start | bytes 49156
  223.5 38.0 %copy-start.92 = (f32[8,512]{1,0:T(8,128)}, f32[8,512]{1,0:T(8,128)S(1)}, u32[]{:S(2)}) copy-start(f32[8,512]{1,0:T(8,128)S(1)} %sub.243) | copy-start | bytes 49156
  234.2 19.2 %slice-start = ((s8[8388608]{0:T(1024)(128)(4,1)}), s8[4194304]{0:T(1024)(128)(4,1)S(1)}, s32[]{:S(2)}) async-start(s8[8388608]{0:T(1024)(128)(4,1)} %bitcast.616), calls=%async_computation.2 | async-start | bytes 8388608
  243.5 18.1 %slice-start.6 = ((s8[8388608]{0:T(1024)(128)(4,1)}), s8[4194304]{0:T(1024)(128)(4,1)S(1)}, s32[]{:S(2)}) async-start(s8[8388608]{0:T(1024)(128)(4,1)} %bitcast.622), calls=%async_computation.8 | async-start | bytes 8388608
  269.7 11.7 %copy-start.105 = (f32[256]{0:T(256)S(1)}, f32[256]{0:T(256)}, u32[]{:S(2)}) copy-start(f32[256]{0:T(256)} %get-tuple-element.24) | copy-start | bytes 3076
  269.7 13.1 %copy-start.55 = (f32[16,2,256]{2,0,1:T(8,128)S(1)}, f32[16,2,256]{2,0,1:T(8,128)}, u32[]{:S(2)}) copy-start(f32[16,2,256]{2,0,1:T(8,128)} %copy.50) | copy-start | bytes 98308
  280.3 10.7 %copy-start.30 = (f32[256,256]{1,0:T(8,128)}, f32[256,256]{1,0:T(8,128)S(1)}, u32[]{:S(2)}) copy-start(f32[256,256]{1,0:T(8,128)S(1)} %fusion.91) | copy-start | bytes 786436
  359.2 56.4 %copy-start.63 = (f32[1,64,64]{1,2,0:T(8,128)S(1)}, f32[1,64,64]{1,2,0:T(8,128)}, u32[]{:S(2)}) copy-start(f32[1,64,64]{1,2,0:T(8,128)} %custom-call.16) | copy-start | bytes 49156
  432.6 11.0 %collective-permute-start.10 = (f32[64,1024]{1,0:T(8,128)}, f32[64,1024]{1,0:T(8,128)}, u32[]{:S(2)}, u32[]{:S(2)}) collective-permute-start(f32[64,1024]{1,0:T(8,128)} %get-tuple-element.47), channel_id=1, source_target_pairs={{1,0},{2,1},{3,2},{4,3},{5,4},{6,5},{7,6},{8,7},{9,8},{10,9},{11,1... | collective-permute-start | bytes 786440 | tf_op jit(solution)/shard_map/ppermute | solution.py:23
  433.9 9.7 %collective-permute-start.9 = (f32[64,1024]{1,0:T(8,128)}, f32[64,1024]{1,0:T(8,128)}, u32[]{:S(2)}, u32[]{:S(2)}) collective-permute-start(f32[64,1024]{1,0:T(8,128)} %get-tuple-element.48), channel_id=1, source_target_pairs={{0,1},{1,2},{2,3},{3,4},{4,5},{5,6},{6,7},{7,8},{8,9},{9,10},{10,1... | collective-permute-start | bytes 786440 | tf_op jit(solution)/shard_map/ppermute | solution.py:21
  443.5 13.7 %slice-start.4 = ((s8[8388608]{0:T(1024)(128)(4,1)}), s8[4194304]{0:T(1024)(128)(4,1)S(1)}, s32[]{:S(2)}) async-start(s8[8388608]{0:T(1024)(128)(4,1)} %bitcast.620), calls=%async_computation.6 | async-start | bytes 8388608
  446.3 10.9 %slice-start.5 = ((s8[8388608]{0:T(1024)(128)(4,1)}), s8[4194304]{0:T(1024)(128)(4,1)S(1)}, s32[]{:S(2)}) async-start(s8[8388608]{0:T(1024)(128)(4,1)} %bitcast.620), calls=%async_computation.7 | async-start | bytes 8388608
  446.3 10.9 %copy-start.87 = (f32[8,512]{1,0:T(8,128)S(1)}, f32[8,512]{1,0:T(8,128)}, u32[]{:S(2)}) copy-start(f32[8,512]{1,0:T(8,128)} %copy-done.86) | copy-start | bytes 49156
  446.3 10.9 %copy-start.120 = (f32[8]{0:T(128)S(1)}, f32[8]{0:T(128)}, u32[]{:S(2)}) copy-start(f32[8]{0:T(128)} %get-tuple-element.14) | copy-start | bytes 100
  446.4 20.7 %slice-start.2 = ((s8[8388608]{0:T(1024)(128)(4,1)}), s8[4194304]{0:T(1024)(128)(4,1)S(1)}, s32[]{:S(2)}) async-start(s8[8388608]{0:T(1024)(128)(4,1)} %bitcast.618), calls=%async_computation.4 | async-start | bytes 8388608
  457.3 19.6 %slice-start.8 = ((s8[8388608]{0:T(1024)(128)(4,1)}), s8[4194304]{0:T(1024)(128)(4,1)S(1)}, s32[]{:S(2)}) async-start(s8[8388608]{0:T(1024)(128)(4,1)} %bitcast.624), calls=%async_computation.10 | async-start | bytes 8388608
  467.1 19.0 %slice-start.10 = ((s8[8388608]{0:T(1024)(128)(4,1)}), s8[4194304]{0:T(1024)(128)(4,1)S(1)}, s32[]{:S(2)}) async-start(s8[8388608]{0:T(1024)(128)(4,1)} %bitcast.626), calls=%async_computation.12 | async-start | bytes 8388608
  486.1 11.2 %copy-start.56 = (f32[16,2,256]{2,0,1:T(8,128)S(1)}, f32[16,2,256]{2,0,1:T(8,128)}, u32[]{:S(2)}) copy-start(f32[16,2,256]{2,0,1:T(8,128)} %copy.50) | copy-start | bytes 98308
  518.7 53.8 %copy-start.53 = (f32[64,64]{1,0:T(8,128)S(1)}, f32[64,64]{1,0:T(8,128)}, u32[]{:S(2)}) copy-start(f32[64,64]{1,0:T(8,128)} %copy-done.52) | copy-start | bytes 49156
  518.7 53.8 %copy-start.58 = (f32[64,64]{0,1:T(8,128)S(1)}, f32[64,64]{0,1:T(8,128)}, u32[]{:S(2)}) copy-start(f32[64,64]{0,1:T(8,128)} %copy-done.57) | copy-start | bytes 49156
  (101 other events, 510.7 us)
Sparse Core Ops, SparseCore 0:
  73.8 61.2 all-gather.4
  440.9 56.4 all-gather.6
where the time goes:
time: 595 us; the launch traced here: 586 us
  matrix products  235 us (39%)
  blocking collectives  119 us (20%)
  other arithmetic  92.8 us (16%)
  local copies, waits for them, and re-layouts  91.1 us (15%)
  starting transfers between devices  25.4 us (4%)
  between operations  17.1 us (3%)
    dot_general x10, matrix products, body(): jnp.einsum('cnq,nqp->cnp', shifted, near_tiles[operate_slot_id], precisio...  93.8 us
    psum x2, blocking collectives, body(): lax.psum(jnp.dot(residual, residual.T, precision=highest), 'leaf')  80.1 us
    dot_general x13, matrix products, pair_kernel(): inner = jnp.einsum('nqd,npd->nqp', first_set, second_set, precision=highest)  64.1 us
    psum x1, blocking collectives, body(): lax.psum(jnp.dot(direction, image.T, precision=highest), 'leaf')  39.4 us
    gather x1, local copies, waits for them, and re-layouts, body(): jnp.take_along_axis(own_points, leaf_skeleton[:, :, None], axis=1)  22.2 us
    another operation x9, other arithmetic, chol_apply(): factor = jnp.linalg.cholesky(matrix)  19.7 us
    another operation x6, other arithmetic, chol_apply(): return jax.scipy.linalg.cho_solve((factor, True), target)  17.3 us
    gather x3, local copies, waits for them, and re-layouts, body(): jnp.take_along_axis(paired.reshape(node_count // 2, 2 * skel_size, coord_...  15.9 us
  transfers between devices with their start and end apart: 13, of which 3 were waited for; matrix products, arithmetic and copies ran while one was open for 44% of the time, Pallas kernels for 0%

commit v1 on v0

v1 whole, which is shorter than its diff:
```python
import math

import jax
import jax.numpy as jnp
from jax import lax
from jax.experimental import pallas as pl
from jax.experimental.pallas import tpu as pltpu
from jax.sharding import PartitionSpec as P

ITERS = 2
ridge = 1.0
F32 = jnp.float32
BF16 = jnp.bfloat16
COORD_SCALE = math.sqrt(math.log2(math.e))
MIB = 1024 * 1024


def nn(a, b):
    return lax.dot_general(a, b, (((1,), (0,)), ((), ())), preferred_element_type=F32)


def nt(a, b):
    return lax.dot_general(a, b, (((1,), (1,)), ((), ())), preferred_element_type=F32)


def split(x):
    hi = x.astype(BF16)
    return hi, (x - hi.astype(F32)).astype(BF16)


def stacked(x):
    return jnp.concatenate(split(x), axis=0)


def times(cat, b_hi, b_lo, mul=nn):
    rows = cat.shape[0] // 2
    both = mul(cat, b_hi)
    return both[:rows] + both[rows:] + mul(cat[:rows], b_lo)


def scaled_cat(x):
    return jnp.concatenate(split(x * COORD_SCALE), axis=1)


def half_norms(cat):
    dim = cat.shape[1] // 2
    whole = cat[:, :dim].astype(F32) + cat[:, dim:].astype(F32)
    column = 0.5 * jnp.sum(whole * whole, axis=1, keepdims=True)
    wide = jnp.broadcast_to(column, (column.shape[0], 128))
    return wide, wide.T[0:1, :]


def pair_tile(cat_a, cat_b, wide_a, row_b):
    dim = cat_b.shape[1] // 2
    b_hi, b_lo = cat_b[:, :dim], cat_b[:, dim:]
    inner = nt(
        jnp.concatenate([cat_a, cat_a], axis=1),
        jnp.concatenate([b_hi, b_hi, b_lo, b_lo], axis=1),
    )
    count = cat_b.shape[0] // 128
    return jnp.exp2(inner - jnp.concatenate([wide_a] * count, axis=1) - row_b)


def one_hot(column, width):
    rows = column.shape[0]
    spots = lax.broadcasted_iota(jnp.int32, (rows, width), 1).astype(F32)
    return jnp.where(spots == column, 1.0, 0.0).astype(BF16)


def columns(rows):
    return rows.astype(F32).T


def pack_skel(ref, first, skel):
    half = skel.shape[0] // 2
    ref[first : first + half, : skel.shape[1]] = skel[:half]
    ref[first : first + half, skel.shape[1] :] = skel[half:]


def unpack_skel(pack):
    half = pack.shape[1] // 2
    return jnp.concatenate([pack[:, :half], pack[:, half:]], axis=0)


def call(body, out_shape, name, vmem, **options):
    return pl.pallas_call(
        body,
        out_shape=out_shape,
        name=name,
        compiler_params=pltpu.CompilerParams(vmem_limit_bytes=vmem * MIB),
        **options,
    )


def struct(shape, dtype=F32):
    return jax.ShapeDtypeStruct(shape, dtype)


VM = pl.BlockSpec(memory_space=pltpu.VMEM)
SM = pl.BlockSpec(memory_space=pltpu.SMEM)


def climb_local(device, level, leaf_count, leaves, transfer_ref, gain_ref, local_ref):
    classes = level[0].shape[0]
    first, depth = 0, 0
    while len(level) > 1:
        count = len(level)
        gain_first = 2 * leaves - 2 * (leaves >> depth) + device * count
        scaled = []
        for i, weights in enumerate(level):
            local_ref[first + i] = weights
            scaled.append(weights * gain_ref[pl.ds(gain_first + i, 1), :])
        left = times(stacked(jnp.concatenate(scaled[0::2], axis=0)), *split(transfer_ref[depth, 0]))
        right = times(stacked(jnp.concatenate(scaled[1::2], axis=0)), *split(transfer_ref[depth, 1]))
        total = left + right
        first += count
        depth += 1
        level = [total[i * classes : (i + 1) * classes] for i in range(count // 2)]
    return level[0]


def leaf_weights(vector_ref, interp_ref, leaf_count, leaf_size):
    return [
        times(stacked(vector_ref[:, j * leaf_size : (j + 1) * leaf_size]), *split(interp_ref[j]))
        for j in range(leaf_count)
    ]


def front(device, points, vector, leaf_skeleton, node_skeleton, leaf_interp, transfer, node_gain, leaves):
    dim = points.shape[1]
    leaf_count, leaf_size, skel_size = leaf_interp.shape
    classes = vector.shape[0]
    pair_count = leaf_count - 1
    local_levels = leaf_count.bit_length() - 1

    def body(
        dev_ref, points_ref, vector_ref, leaf_ref, node_ref, interp_ref, transfer_ref, gain_ref,
        pack_ref, local_ref, hi_ref, lo_ref, rows_ref,
    ):
        device = dev_ref[0]
        rows_ref[...] = jnp.zeros_like(rows_ref)
        pair = 0
        for depth in range(1, local_levels + 1):
            count = leaf_count >> depth
            first = leaves - 2 * (leaves >> depth) + device * count
            for i in range(count):
                rows_ref[pair : pair + 1, :] = node_ref[pl.ds(first + i, 1), :]
                pair += 1
        leaf_columns, node_columns = columns(leaf_ref[...]), columns(rows_ref[...])
        level = []
        for j in range(leaf_count):
            cat = scaled_cat(points_ref[j * leaf_size : (j + 1) * leaf_size, :])
            level.append(nn(one_hot(leaf_columns[:, j : j + 1], leaf_size), cat).astype(BF16))
        pair = 0
        while len(level) > 1:
            above = []
            for p in range(len(level) // 2):
                left, right = level[2 * p], level[2 * p + 1]
                both = jnp.concatenate([left, right], axis=0)
                pick = one_hot(node_columns[:, pair : pair + 1], 2 * skel_size)
                above.append(nn(pick, both).astype(BF16))
                tile = pair_tile(left, right, half_norms(left)[0], half_norms(right)[1])
                hi_ref[pair], lo_ref[pair] = split(tile)
                pair += 1
            level = above
        whole = level[0]
        pack_skel(pack_ref, classes, whole[:, :dim].astype(F32) + whole[:, dim:].astype(F32))
        weights = leaf_weights(vector_ref, interp_ref, leaf_count, leaf_size)
        pack_ref[:classes] = climb_local(
            device, weights, leaf_count, leaves, transfer_ref, gain_ref, local_ref
        )

    local_maps = pl.BlockSpec((local_levels,) + transfer.shape[1:], lambda i: (0, 0, 0, 0))
    return call(
        body,
        (
            struct((classes + skel_size // 2, skel_size)),
            struct((2 * leaf_count - 2, classes, skel_size)),
            struct((pair_count, skel_size, skel_size), BF16),
            struct((pair_count, skel_size, skel_size), BF16),
        ),
        "front",
        28,
        grid=(1,),
        in_specs=[SM, VM, VM, VM, VM, VM, local_maps, VM],
        out_specs=(VM, VM, VM, VM),
        scratch_shapes=[pltpu.VMEM((leaf_count, skel_size), jnp.int32)],
    )(device, points, vector, leaf_skeleton, node_skeleton, leaf_interp, transfer, node_gain)


def upward(device, vector, gram, leaf_interp, transfer, node_gain, leaves):
    leaf_count, leaf_size, skel_size = leaf_interp.shape
    classes = vector.shape[0]
    local_levels = leaf_count.bit_length() - 1

    def body(dev_ref, vector_ref, gram_ref, interp_ref, transfer_ref, gain_ref, pack_ref, local_ref):
        weights = leaf_weights(vector_ref, interp_ref, leaf_count, leaf_size)
        pack_ref[:classes] = climb_local(
            dev_ref[0], weights, leaf_count, leaves, transfer_ref, gain_ref, local_ref
        )
        pack_ref[classes:] = gram_ref[...]

    local_maps = pl.BlockSpec((local_levels,) + transfer.shape[1:], lambda i: (0, 0, 0, 0))
    return call(
        body,
        (
            struct((classes + gram.shape[0], skel_size)),
            struct((2 * leaf_count - 2, classes, skel_size)),
        ),
        "upward",
        18,
        grid=(1,),
        in_specs=[SM, VM, VM, VM, local_maps, VM],
        out_specs=(VM, VM),
    )(device, vector, gram, leaf_interp, transfer, node_gain)


def apply_tile(mask, cat_a, cat_b, hi, lo, out_ref, a, b):
    out_ref[b] = out_ref[b] + mask * times(cat_a, hi, lo)
    if cat_b is not None:
        out_ref[a] = out_ref[a] + mask * times(cat_b, hi, lo, nt)


def near_build(points, vector, near_mask, leaf_count, reach):
    dim = points.shape[1]
    leaf_size = points.shape[0] // leaf_count
    classes = vector.shape[0]

    def body(points_ref, vector_ref, mask_ref, tile_ref, out_ref, cats, wides, rows, vecs):
        a = pl.program_id(0)

        @pl.when(a == 0)
        def _():
            out_ref[...] = jnp.zeros_like(out_ref)
            for j in range(leaf_count):
                cat = scaled_cat(points_ref[j * leaf_size : (j + 1) * leaf_size, :])
                cats[j] = cat
                wide, row = half_norms(cat)
                wides[j] = wide
                rows[j] = jnp.broadcast_to(row, (8, leaf_size))
                vecs[j] = stacked(vector_ref[:, j * leaf_size : (j + 1) * leaf_size])

        for step in range(reach + 1):

            @pl.when(a + step < leaf_count)
            def _():
                b = a + step
                tile = pair_tile(cats[a], cats[b], wides[a], rows[b][0:1, :])
                tile_ref[0, step, 0], tile_ref[0, step, 1] = split(tile)
                apply_tile(
                    mask_ref[a, reach + step], vecs[a], vecs[b] if step else None,
                    tile_ref[0, step, 0], tile_ref[0, step, 1], out_ref, a, b,
                )

    tile_block = pl.BlockSpec((1, reach + 1, 2, leaf_size, leaf_size), lambda a: (a, 0, 0, 0, 0))
    tiles = struct((leaf_count, reach + 1, 2, leaf_size, leaf_size), BF16)
    return call(
        body,
        (tiles, struct((leaf_count, classes, leaf_size))),
        "near_build",
        30,
        grid=(leaf_count,),
        in_specs=[
            pl.BlockSpec(points.shape, lambda a: (0, 0)),
            pl.BlockSpec(vector.shape, lambda a: (0, 0)),
            SM,
        ],
        out_specs=(
            tile_block,
            pl.BlockSpec((leaf_count, classes, leaf_size), lambda a: (0, 0, 0)),
        ),
        scratch_shapes=[
            pltpu.VMEM((leaf_count, leaf_size, 2 * dim), BF16),
            pltpu.VMEM((leaf_count, leaf_size, 128), F32),
            pltpu.VMEM((leaf_count, 8, leaf_size), F32),
            pltpu.VMEM((leaf_count, 2 * classes, leaf_size), BF16),
        ],
    )(points, vector, near_mask)


def near_apply(tiles, vector, near_mask):
    leaf_count, steps, _, leaf_size, _ = tiles.shape
    reach = steps - 1
    classes = vector.shape[0]

    def body(tile_ref, vector_ref, mask_ref, out_ref, vecs):
        a = pl.program_id(0)

        @pl.when(a == 0)
        def _():
            out_ref[...] = jnp.zeros_like(out_ref)
            for j in range(leaf_count):
                vecs[j] = stacked(vector_ref[:, j * leaf_size : (j + 1) * leaf_size])

        for step in range(steps):

            @pl.when(a + step < leaf_count)
            def _():
                b = a + step
                apply_tile(
                    mask_ref[a, reach + step], vecs[a], vecs[b] if step else None,
                    tile_ref[0, step, 0], tile_ref[0, step, 1], out_ref, a, b,
                )

    tile_block = pl.BlockSpec((1, steps, 2, leaf_size, leaf_size), lambda a: (a, 0, 0, 0, 0))
    return call(
        body,
        struct((leaf_count, classes, leaf_size)),
        "near_apply",
        20,
        grid=(leaf_count,),
        in_specs=[tile_block, pl.BlockSpec(vector.shape, lambda a: (0, 0)), SM],
        out_specs=pl.BlockSpec((leaf_count, classes, leaf_size), lambda a: (0, 0, 0)),
        scratch_shapes=[pltpu.VMEM((leaf_count, 2 * classes, leaf_size), BF16)],
    )(tiles, vector, near_mask)


def edges(leaf_count, reach):
    found = []
    for h in range(reach):
        for j in range(reach):
            offset = j - (h - reach)
            if offset <= reach:
                found.append((h, j, reach - offset))
    for h in range(reach):
        for j in range(leaf_count - reach, leaf_count):
            offset = leaf_count + h - j
            if offset <= reach:
                found.append((reach + h, j, reach + offset))
    return found


def edge_build(points, left_points, right_points, left_rows, right_rows, near_mask, leaf_count, reach):
    dim = points.shape[1]
    leaf_size = points.shape[0] // leaf_count
    classes = left_rows.shape[0]
    border = edges(leaf_count, reach)

    def body(head_ref, tail_ref, lp_ref, rp_ref, lv_ref, rv_ref, mask_ref, hi_ref, lo_ref, out_ref):
        out_ref[...] = jnp.zeros_like(out_ref)
        for t, (h, j, slot) in enumerate(border):
            hs, hv = (lp_ref, lv_ref) if h < reach else (rp_ref, rv_ref)
            spot = h % reach
            where = slice(spot * leaf_size, (spot + 1) * leaf_size)
            cat_h = scaled_cat(hs[where, :])
            own_ref, own = (head_ref, j) if j < reach else (tail_ref, j - (leaf_count - reach))
            cat_j = scaled_cat(own_ref[own * leaf_size : (own + 1) * leaf_size, :])
            tile = pair_tile(cat_h, cat_j, half_norms(cat_h)[0], half_norms(cat_j)[1])
            hi_ref[t], lo_ref[t] = split(tile)
            spot = j if j < reach else reach + j - (leaf_count - reach)
            apply_tile(mask_ref[j, slot], stacked(hv[:, where]), None, hi_ref[t], lo_ref[t], out_ref, 0, spot)

    block = (reach * leaf_size, dim)
    last = leaf_count // reach - 1
    tiles = struct((len(border), leaf_size, leaf_size), BF16)
    return call(
        body,
        (tiles, tiles, struct((2 * reach, classes, leaf_size))),
        "edge_build",
        20,
        grid=(1,),
        in_specs=[
            pl.BlockSpec(block, lambda i: (0, 0)),
            pl.BlockSpec(block, lambda i: (last, 0)),
            VM, VM, VM, VM, SM,
        ],
        out_specs=(VM, VM, VM),
    )(points, points, left_points, right_points, left_rows, right_rows, near_mask)


def edge_apply(hi_tiles, lo_tiles, left_rows, right_rows, near_mask, leaf_count, reach):
    leaf_size = hi_tiles.shape[1]
    classes = left_rows.shape[0]
    border = edges(leaf_count, reach)

    def body(hi_ref, lo_ref, lv_ref, rv_ref, mask_ref, out_ref):
        out_ref[...] = jnp.zeros_like(out_ref)
        for t, (h, j, slot) in enumerate(border):
            hv = lv_ref if h < reach else rv_ref
            where = slice((h % reach) * leaf_size, (h % reach + 1) * leaf_size)
            spot = j if j < reach else reach + j - (leaf_count - reach)
            apply_tile(mask_ref[j, slot], stacked(hv[:, where]), None, hi_ref[t], lo_ref[t], out_ref, 0, spot)

    return call(
        body,
        struct((2 * reach, classes, leaf_size)),
        "edge_apply",
        14,
        in_specs=[VM, VM, VM, VM, SM],
        out_specs=VM,
    )(hi_tiles, lo_tiles, left_rows, right_rows, near_mask)


def tree_stage(device, packs, node_gain, transfer, node_skeleton, classes, leaves, level, bit, with_skel, extra, climb):
    count = len(packs)
    skel_size = packs[0].shape[1]
    levels = count.bit_length() - 1
    skel_rows = skel_size // 2 if with_skel else 0
    out_rows = packs[0].shape[0]

    def body(*refs):
        dev_ref, pack_refs = refs[0], refs[1 : 1 + count]
        rest = list(refs[1 + count :])
        gains_ref, transfer_ref = rest.pop(0), rest.pop(0)
        node_ref = rest.pop(0) if with_skel else None
        sibling_ref = rest.pop(0)
        next_ref = rest.pop(0)
        hi_ref, lo_ref = (rest.pop(0), rest.pop(0)) if with_skel else (None, None)
        joined = rest.pop(0)
        device = dev_ref[0]
        place = lax.shift_right_logical(device, bit) & (count - 1)
        base = lax.shift_right_logical(device, bit + levels)
        if with_skel and (climb or levels > 1):
            rows_ref = rest.pop(0)
            rows_ref[...] = jnp.zeros_like(rows_ref)
            spot = 0
            for depth in range(1, levels + 1 if climb else levels):
                nodes = count >> depth
                row = leaves - 2 * (leaves >> (level + depth)) + base * nodes
                for i in range(nodes):
                    rows_ref[spot : spot + 1, :] = node_ref[pl.ds(row + i, 1), :]
                    spot += 1
            pick_columns = columns(rows_ref[...])
        for i in range(count):
            joined[place ^ i] = pack_refs[i][...]
        weights = [joined[i][:classes] for i in range(count)]
        skels = []
        if with_skel:
            skels = [
                jnp.concatenate(split(unpack_skel(joined[i][classes : classes + skel_rows])), axis=1)
                for i in range(count)
            ]
        pick_first = 0
        for depth in range(levels):
            own = lax.shift_right_logical(place, depth)
            other = own ^ 1
            chosen = weights[0]
            for i in range(1, len(weights)):
                chosen = jnp.where(other == i, weights[i], chosen)
            sibling_ref[depth] = chosen
            if with_skel:
                mine, theirs = skels[0], skels[0]
                for i in range(1, len(skels)):
                    mine = jnp.where(own == i, skels[i], mine)
                    theirs = jnp.where(other == i, skels[i], theirs)
                tile = pair_tile(theirs, mine, half_norms(theirs)[0], half_norms(mine)[1])
                hi_ref[depth], lo_ref[depth] = split(tile)
            if depth + 1 < levels or climb:
                row = 2 * leaves - 2 * (leaves >> (level + depth)) + base * len(weights)
                scaled = [w * gains_ref[pl.ds(row + i, 1), :] for i, w in enumerate(weights)]
                left = times(stacked(jnp.concatenate(scaled[0::2], axis=0)), *split(transfer_ref[depth, 0]))
                right = times(stacked(jnp.concatenate(scaled[1::2], axis=0)), *split(transfer_ref[depth, 1]))
                total = left + right
                weights = [total[i * classes : (i + 1) * classes] for i in range(len(weights) // 2)]
                if with_skel:
                    above = []
                    for p in range(len(skels) // 2):
                        both = jnp.concatenate([skels[2 * p], skels[2 * p + 1]], axis=0)
                        pick = one_hot(pick_columns[:, pick_first : pick_first + 1], 2 * skel_size)
                        above.append(nn(pick, both).astype(BF16))
                        pick_first += 1
                    skels = above
        if climb:
            next_ref[:classes] = weights[0]
            if with_skel:
                dim = skels[0].shape[1] // 2
                pack_skel(next_ref, classes, skels[0][:, :dim].astype(F32) + skels[0][:, dim:].astype(F32))
        else:
            next_ref[: classes + skel_rows] = jnp.zeros((classes + skel_rows, skel_size), F32)
        if extra:
            rows = slice(classes + skel_rows, out_rows)
            total = joined[0][rows]
            for i in range(1, count):
                total = total + joined[i][rows]
            next_ref[rows] = total

    out = [struct((levels, classes, skel_size)), struct((out_rows, skel_size))]
    if with_skel:
        out += [struct((levels, skel_size, skel_size), BF16)] * 2
    scratch = [pltpu.VMEM((count, out_rows, skel_size), F32)]
    ins = [device, *packs, node_gain, transfer]
    if with_skel:
        ins.append(node_skeleton)
        if climb or levels > 1:
            scratch.append(pltpu.VMEM((8, skel_size), jnp.int32))
    return call(
        body,
        tuple(out),
        "tree_stage",
        10,
        in_specs=[SM] + [VM] * (len(ins) - 1),
        out_specs=tuple([VM] * len(out)),
        scratch_shapes=scratch,
    )(*ins)


def downward(
    device, vector, near, edge, leaf_interp, transfer, local_weights, local_tiles, node_gain,
    siblings, device_tiles, reach, leaves, start,
):
    leaf_count, leaf_size, skel_size = leaf_interp.shape
    classes = vector.shape[0]
    local_levels = leaf_count.bit_length() - 1
    stages = len(siblings)

    def body(*refs):
        dev_ref, vector_ref, near_ref, edge_ref, interp_hbm, transfer_hbm = refs[:6]
        weights_ref, tiles_hi, tiles_lo, gain_ref = refs[6:10]
        sib_refs = refs[10 : 10 + stages]
        dev_refs = refs[10 + stages : 10 + 3 * stages]
        rest = list(refs[10 + 3 * stages :])
        device = dev_ref[0]

        def gain(level, node):
            return gain_ref[pl.ds(2 * leaves - 2 * (leaves >> level) + node, 1), :]

        image_ref = rest.pop(0)
        head_ref, tail_ref = (rest.pop(0), rest.pop(0)) if start else (None, None)
        gram_ref = rest.pop(0) if start else None
        interp_ref, maps_ref, interp_sem, maps_sem = rest
        load_maps = pltpu.make_async_copy(transfer_hbm, maps_ref, maps_sem)
        load_interp = pltpu.make_async_copy(interp_hbm, interp_ref, interp_sem)
        load_maps.start()
        load_interp.start()
        local = []
        for s in range(stages):
            for i in range(sib_refs[s].shape[0]):
                local.append(times(stacked(sib_refs[s][i]), dev_refs[2 * s][i], dev_refs[2 * s + 1][i]))
        load_maps.wait()
        top = len(local) - 1
        potential = local[top]
        for b in range(top - 1, -1, -1):
            node = lax.shift_right_logical(device, b)
            down = maps_ref[local_levels + b, node & 1]
            potential = times(stacked(potential), *split(down), nt) * gain(local_levels + b, node) + local[b]
        level = [potential]
        for depth in range(local_levels - 1, -1, -1):
            cat = stacked(jnp.concatenate(level, axis=0))
            sides = [times(cat, *split(maps_ref[depth, c]), nt) for c in range(2)]
            count = leaf_count >> depth
            first = 2 * leaf_count - 2 * count
            pair_first = leaf_count - count
            below = []
            for n in range(count):
                p, c = n // 2, n % 2
                cat_sibling = stacked(weights_ref[first + (n ^ 1)])
                hi, lo = tiles_hi[pair_first + p], tiles_lo[pair_first + p]
                direct = times(cat_sibling, hi, lo, nn if c else nt)
                carried = sides[c][p * classes : (p + 1) * classes]
                below.append(carried * gain(depth, device * count + n) + direct)
            level = below
        load_interp.wait()
        for j in range(leaf_count):
            where = slice(j * leaf_size, (j + 1) * leaf_size)
            total = ridge * vector_ref[:, where] + near_ref[j]
            if j < reach:
                total = total + edge_ref[j]
            if j >= leaf_count - reach:
                total = total + edge_ref[reach + j - (leaf_count - reach)]
            image_ref[:, where] = total + times(stacked(level[j]), *split(interp_ref[j]), nt)
        if start:
            width = reach * leaf_size
            head_ref[...] = image_ref[:, :width]
            tail_ref[...] = image_ref[:, (leaf_count - reach) * leaf_size :]
            whole = nt(stacked(vector_ref[...]), jnp.concatenate([stacked(vector_ref[...]), stacked(image_ref[...])], axis=0))
            half = whole[:classes] + whole[classes:]
            rows = classes // 2
            self_gram = half[:, :classes] + half[:, classes : 2 * classes]
            image_gram = half[:, 2 * classes : 3 * classes] + half[:, 3 * classes :]
            gram = jnp.concatenate([self_gram, image_gram], axis=1)
            gram_ref[:, : 2 * classes] = gram[:rows]
            gram_ref[:, 2 * classes :] = gram[rows:]

    out = [struct(vector.shape)]
    if start:
        out += [struct((classes, reach * leaf_size))] * 2
        out.append(struct((classes // 2, 4 * classes)))
    ins = [device, vector, near, edge, leaf_interp, transfer, local_weights, *local_tiles, node_gain]
    ins += list(siblings)
    for pair in device_tiles:
        ins += list(pair)
    anywhere = pl.BlockSpec(memory_space=pl.ANY)
    specs = [SM, VM, VM, VM, anywhere, anywhere] + [VM] * (len(ins) - 6)
    return call(
        body,
        tuple(out),
        "downward",
        30,
        in_specs=specs,
        out_specs=tuple([VM] * len(out)),
        scratch_shapes=[
            pltpu.VMEM(leaf_interp.shape, F32),
            pltpu.VMEM(transfer.shape, F32),
            pltpu.SemaphoreType.DMA,
            pltpu.SemaphoreType.DMA,
        ],
    )(*ins)


def mixed(matrix, rows):
    m_hi, m_lo = split(matrix)
    r_hi, r_lo = split(rows)
    return nn(
        jnp.concatenate([m_hi, m_lo, m_hi, m_lo], axis=1),
        jnp.concatenate([r_hi, r_hi, r_lo, r_lo], axis=0),
    )


def three(x):
    hi = x.astype(BF16)
    rest = x - hi.astype(F32)
    mid = rest.astype(BF16)
    return hi, mid, (rest - mid.astype(F32)).astype(BF16)


def exact_dot(a, b):
    a0, a1, a2 = three(a)
    b0, b1, b2 = three(b)
    return nn(
        jnp.concatenate([a2, a1, a0, a1, a0, a0], axis=1),
        jnp.concatenate([b0, b1, b2, b0, b1, b0], axis=0),
    )


def eliminate(systems, width=4):
    size, wide = systems[0].shape
    place = lax.broadcasted_iota(jnp.int32, (size, wide), 0)
    for first in range(0, size, width):
        block = [
            [jnp.broadcast_to(m[:, k : k + 1], (size, wide)) for k in range(first, first + width)]
            for m in systems
        ]
        for i in range(width):
            k = first + i
            pivot = place == k
            for n in range(len(systems)):
                cols = block[n]
                inverse = 1.0 / cols[i][k : k + 1, :]
                for j in range(i + 1, width):
                    scaled = cols[j][k : k + 1, :] * inverse
                    cols[j] = jnp.where(pivot, scaled, cols[j] - cols[i] * scaled)
                scaled = systems[n][k : k + 1, :] * inverse
                systems[n] = jnp.where(pivot, scaled, systems[n] - cols[i] * scaled)
    return systems


def first_step(gram, right_side, image, second):
    classes = right_side.shape[0]

    def body(gram_in, b_ref, image_ref, second_ref, res_ref, res_image_ref, gram_ref, small_ref):
        packed = gram_in[classes:, :]
        both = jnp.concatenate([packed[:, : 2 * classes], packed[:, 2 * classes :]], axis=0)
        turned = both.T
        base = 0.5 * (both[:, :classes] + turned[:classes])
        curvature = 0.5 * (both[:, classes:] + turned[classes:])
        square = (classes, classes)
        unit = jnp.where(
            lax.broadcasted_iota(jnp.int32, square, 0) == lax.broadcasted_iota(jnp.int32, square, 1), 1.0, 0.0
        )
        solved, inverse = eliminate(
            [jnp.concatenate([curvature, base], axis=1), jnp.concatenate([base, unit], axis=1)]
        )
        alpha_t = solved.T[classes:]
        small_ref[:classes] = jnp.concatenate([alpha_t, inverse[:, classes:]], axis=1)
        small_ref[classes:] = both
        res = b_ref[...] - mixed(alpha_t, image_ref[...])
        res_image = image_ref[...] - mixed(alpha_t, second_ref[...])
        res_ref[...] = res
        res_image_ref[...] = res_image
        res_cat, base_cat = stacked(res), stacked(b_ref[...])
        left = jnp.concatenate([res_cat, base_cat], axis=0)
        right = jnp.concatenate([res_cat, stacked(res_image), stacked(image_ref[...])], axis=0)
        whole = nt(left, right)

        def block(i, j):
            part = whole[2 * i * classes : 2 * (i + 1) * classes, 2 * j * classes : 2 * (j + 1) * classes]
            half = part[:classes] + part[classes:]
            return half[:, :classes] + half[:, classes:]

        gram_ref[...] = jnp.concatenate([block(0, 0), block(0, 1), block(0, 2), block(1, 1)], axis=1)

    return call(
        body,
        (
            struct(right_side.shape),
            struct(right_side.shape),
            struct((classes, 4 * classes)),
            struct((2 * classes, 2 * classes)),
        ),
        "first_step",
        28,
    )(gram, right_side, image, second)


def last_step(small, parts, right_side, image, res, res_image):
    classes = right_side.shape[0]
    count = len(parts)

    def body(small_ref, *refs):
        base_ref, image_ref, res_ref, res_image_ref, sol_ref, out_ref = refs[count:]
        grams = [ref[...] for ref in refs[:count]]
        while len(grams) > 1:
            grams = [a + b for a, b in zip(grams[0::2], grams[1::2])]
        grams = grams[0]
        alpha_t = small_ref[:classes, :classes]
        inverse = small_ref[:classes, classes:]
        image_gram = small_ref[classes:, classes:]
        new_gram = grams[:, :classes]
        new_gram = 0.5 * (new_gram + grams[:, : 2 * classes].T[:classes])
        beta = exact_dot(inverse, new_gram)
        beta_t = jnp.concatenate([beta, beta], axis=1).T[:classes]
        res_image_gram = grams[:, classes : 2 * classes]
        res_base = grams[:, 2 * classes : 3 * classes]
        base_res = grams[:, 3 * classes :]
        curvature = (
            res_image_gram
            + exact_dot(res_base, beta)
            + exact_dot(beta_t, base_res + exact_dot(image_gram, beta))
        )
        curvature = 0.5 * (curvature + jnp.concatenate([curvature, curvature], axis=1).T[:classes])
        (solved,) = eliminate([jnp.concatenate([curvature, new_gram], axis=1)])
        alpha2_t = solved.T[classes:]
        direction = res_ref[...] + mixed(beta_t, base_ref[...])
        moved = res_image_ref[...] + mixed(beta_t, image_ref[...])
        sol_ref[...] = mixed(alpha_t, base_ref[...]) + mixed(alpha2_t, direction)
        out_ref[...] = res_ref[...] - mixed(alpha2_t, moved)

    return call(body, (struct(right_side.shape), struct(right_side.shape)), "last_step", 28)(
        small, *parts, right_side, image, res, res_image
    )


def body(
    points, right_side, neighbours, leaf_interp, leaf_skeleton, node_skeleton, node_gain, transfer
):
    leaf_count, slot_count = neighbours.shape
    reach = (slot_count - 1) // 2
    leaf_size, skel_size = leaf_interp.shape[1:]
    classes = right_side.shape[0]
    dev_count = lax.axis_size("leaf")
    dev_levels = dev_count.bit_length() - 1
    local_levels = leaf_count.bit_length() - 1
    levels = local_levels + dev_levels
    leaves = leaf_count * dev_count
    device = lax.axis_index("leaf").astype(jnp.int32)[None]

    def exchange(head, tail):
        ends = dev_count - 1
        left = lax.ppermute(tail, "leaf", [(i, i + 1) for i in range(ends)])
        right = lax.ppermute(head, "leaf", [(i + 1, i) for i in range(ends)])
        return left, right

    def halo(rows, axis):
        width = reach * leaf_size
        size = rows.shape[axis]
        return exchange(
            lax.slice_in_dim(rows, 0, width, axis=axis), lax.slice_in_dim(rows, size - width, size, axis=axis)
        )

    def group(pack, first_bit, count):
        return [pack] + [
            lax.ppermute(pack, "leaf", [(d, d ^ (i << first_bit)) for d in range(dev_count)])
            for i in range(1, count)
        ]

    stages = [(bit, min(2, dev_levels - bit)) for bit in range(0, dev_levels, 2)]
    near_mask = (neighbours >= 0).astype(F32)

    def climb(pack, with_skel, extra, covers):
        siblings, tiles, results = [], [], []
        for stage, (bit, width) in enumerate(stages):
            level = local_levels + bit
            depth = min(width, levels - 1 - level) or 1
            first = min(level, levels - 1 - depth)
            packs = group(pack, bit, 1 << width)
            if stage < len(covers):
                done = covers[stage](pack)
                results.append(done)
                packs, _ = lax.optimization_barrier((packs, done[-1]))
            found = tree_stage(
                device, packs, node_gain, lax.slice_in_dim(transfer, first, first + depth, axis=0),
                node_skeleton, classes, leaves, level, bit, with_skel, extra, level + width < levels,
            )
            siblings.append(found[0])
            pack = found[1]
            if with_skel:
                tiles.append((found[2], found[3]))
        return siblings, tiles, pack, results

    def after(pack, *values):
        return lax.optimization_barrier((pack, values))[1]

    left_points, right_points = halo(points, 0)
    left_rows, right_rows = halo(right_side, 1)
    pack, weights, *local_tiles = front(
        device, points, right_side, leaf_skeleton, node_skeleton, leaf_interp, transfer, node_gain, leaves
    )

    def build_near(pack):
        (vector,) = after(pack, right_side)
        return near_build(points, vector, near_mask, leaf_count, reach)

    def build_edge(pack):
        left, right = after(pack, left_rows, right_rows)
        return edge_build(points, left_points, right_points, left, right, near_mask, leaf_count, reach)

    siblings, device_tiles, _, results = climb(pack, True, False, [build_near, build_edge])
    (near_tiles, near), (edge_hi, edge_lo, edge) = results
    image, head, tail, gram = downward(
        device, right_side, near, edge, leaf_interp, transfer, weights, local_tiles, node_gain,
        siblings, device_tiles, reach, leaves, True,
    )

    left_rows, right_rows = exchange(head, tail)
    pack, weights = upward(device, image, gram, leaf_interp, transfer, node_gain, leaves)

    def apply_near(pack):
        (vector,) = after(pack, image)
        return (near_apply(near_tiles, vector, near_mask),)

    def apply_edge(pack):
        left, right = after(pack, left_rows, right_rows)
        return (edge_apply(edge_hi, edge_lo, left, right, near_mask, leaf_count, reach),)

    siblings, _, pack, results = climb(pack, False, True, [apply_near, apply_edge])
    (near,), (edge,) = results
    (second,) = downward(
        device, image, near, edge, leaf_interp, transfer, weights, local_tiles, node_gain,
        siblings, device_tiles, reach, leaves, False,
    )

    res, res_image, grams, small = first_step(pack, right_side, image, second)
    for bit, width in stages[:-1]:
        parts = group(grams, bit, 1 << width)
        while len(parts) > 1:
            parts = [a + b for a, b in zip(parts[0::2], parts[1::2])]
        grams = parts[0]
    bit, width = stages[-1]
    parts = group(grams, bit, 1 << width)
    return last_step(small, parts, right_side, image, res, res_image)


def solution(mesh):
    placed = (
        P("leaf", None),
        P(None, "leaf"),
        P("leaf", None),
        P("leaf", None, None),
        P("leaf", None),
        P(),
        P(),
        P(),
    )
    return jax.shard_map(
        body,
        mesh=mesh,
        in_specs=placed,
        out_specs=(P(None, "leaf"), P(None, "leaf")),
        check_vma=False,
    )
```

time: 595 us -> 176 us (0.30); the launches traced: 586 us -> 176 us
  matrix products: 235 us -> 0 us
  blocking collectives: 119 us -> 0 us
  other arithmetic: 92.8 us -> 0.04 us
  Pallas kernels: 0 us -> 76.7 us
  local copies, waits for them, and re-layouts: 91.1 us -> 25.2 us
  starting transfers between devices: 25.4 us -> 49 us
  waiting for transfers between devices: 5.04 us -> 23.7 us
  between operations: 17.1 us -> 1.09 us
    dot_general x100 -> x0, matrix products: 233 us -> none  [the longest x10 93.8 us: body(): jnp.einsum('cnq,nqp->cnp', shifted, near_tiles[operate_slot_id], precisio...]
    psum x3 -> x0, blocking collectives: 119 us -> none  [the longest x2 80.1 us: body(): lax.psum(jnp.dot(residual, residual.T, precision=highest), 'leaf')]
    pallas_call x0 -> x16, Pallas kernels: none -> 76.7 us  [the longest x1 25.2 us: near_build(): call(body, (tiles, struct((leaf_count, classes, leaf_size))), 'near_build...]
    gather x8 -> x0, local copies, waits for them, and re-layouts: 44 us -> none  [the longest x1 22.2 us: body(): jnp.take_along_axis(own_points, leaf_skeleton[:, :, None], axis=1)]
    another operation x19 -> x0, other arithmetic: 37.1 us -> none  [the longest x9 19.7 us: chol_apply(): factor = jnp.linalg.cholesky(matrix)]
    ppermute x11 -> x27, starting transfers between devices: 25.3 us -> 49 us  [the longest x21 36.2 us: group(): lax.ppermute(pack, 'leaf', [(d, d ^ i << first_bit) for d in range(dev_co...]
    reduce_sum x13 -> x0, other arithmetic: 21.5 us -> none  [the longest x7 12.6 us: pair_kernel(): second_norm = jnp.sum(second_set * second_set, axis=-1)]
    ppermute x11 -> x27, waiting for transfers between devices: 3.09 us -> 23.7 us  [the longest x21 23.7 us: group(): lax.ppermute(pack, 'leaf', [(d, d ^ i << first_bit) for d in range(dev_co...]
  transfers between devices with their start and end apart: 13 -> 27, of which waited for: 3 -> 8; matrix products, arithmetic and copies ran while one was open for 44% -> 0% of each run, Pallas kernels for 0% -> 27%
where the time goes in v1:
time: 176 us
  Pallas kernels  76.7 us (44%)
  starting transfers between devices  49 us (28%)
  local copies, waits for them, and re-layouts  25.2 us (14%)
  waiting for transfers between devices  23.7 us (13%)
    ppermute x21, starting transfers between devices, group(): lax.ppermute(pack, 'leaf', [(d, d ^ i << first_bit) for d in range(dev_co...  36.2 us
    pallas_call x1, Pallas kernels, near_build(): call(body, (tiles, struct((leaf_count, classes, leaf_size))), 'near_build...  25.2 us
    unnamed x60, local copies, waits for them, and re-layouts  24.8 us
    ppermute x21, waiting for transfers between devices, group(): lax.ppermute(pack, 'leaf', [(d, d ^ i << first_bit) for d in range(dev_co...  23.7 us
    pallas_call x1, Pallas kernels, near_apply(): call(body, struct((leaf_count, classes, leaf_size)), 'near_apply', 20, gr...  11.5 us
    pallas_call x2, Pallas kernels, downward(): call(body, tuple(out), 'downward', 30, in_specs=specs, out_specs=tuple([V...  11.4 us
    ppermute x3, starting transfers between devices, exchange(): left = lax.ppermute(tail, 'leaf', [(i, i + 1) for i in range(ends)])  8.7 us
    pallas_call x1, Pallas kernels, last_step(): call(body, (struct(right_side.shape), struct(right_side.shape)), 'last_st...  5.93 us
  transfers between devices with their start and end apart: 27, of which 8 were waited for; matrix products, arithmetic and copies ran while one was open for 0% of the time, Pallas kernels for 27%

profile of v1, /device:TPU:0, one launch (start us, length us, event | category | flops | bytes accessed | tf_op | source)
XLA Modules:
  0.0 175.7 jit_solution(6531068718318505955)
XLA Ops:
  0.6 2.0 %copy-done = f32[7,2,256,256]{3,2,1,0:T(8,128)S(1)} copy-done((f32[7,2,256,256]{3,2,1,0:T(8,128)S(1)}, f32[7,2,256,256]{3,2,1,0:T(8,128)}, u32[]{:S(2)}) %copy-start) | copy-done | bytes 3670040
  2.7 2.2 %copy-done.2 = f32[8,512,256]{2,1,0:T(8,128)S(1)} copy-done((f32[8,512,256]{2,1,0:T(8,128)S(1)}, f32[8,512,256]{2,1,0:T(8,128)}, u32[]{:S(2)}) %copy-start.2) | copy-done | bytes 4194328
  4.9 1.0 copy-done.4
  5.9 1.6 copy-done.6
  7.5 1.2 copy-done.8
  8.7 0.9 copy-done.11
  10.4 4.0 %front.1 = (f32[192,256]{1,0:T(8,128)S(1)}, f32[14,64,256]{2,1,0:T(8,128)S(1)}, bf16[7,256,256]{2,1,0:T(8,128)(2,1)S(1)}, bf16[7,256,256]{2,1,0:T(8,128)(2,1)S(1)}) custom-call(s32[1]{0:T(128)} %bitcast.dev_ref.refs_0_, f32[4096,128]{1,0:T(8,128)S(1)} %copy-done.6, f32[64,4096]{1,0:T(8,128)S(1)} %copy-done.8, s32[8,256]{1,0:T(8,128)S(1)} %copy-done.28, ...), custom_call_target="tpu_custom_call" | custom-call | tf_op jit(solution)/shard_map/front/pallas_call | solution.py:174
  14.4 0.9 copy-done.20
  15.3 2.4 %collective-permute-start.4 = (f32[192,256]{1,0:T(8,128)S(1)}, f32[192,256]{1,0:T(8,128)S(1)}, u32[]{:S(2)}, u32[]{:S(2)}) collective-permute-start(f32[192,256]{1,0:T(8,128)S(1)} %get-tuple-element.63.refs_1_), channel_id=1, source_target_pairs={{0,3},{1,2},{2,1},{3,0},{4,7},{5,6},{6,5},{7,4},{8,11},{9,10},{10,... | collective-permute-start | bytes 589832 | tf_op jit(solution)/shard_map/ppermute | solution.py:762
  18.4 1.3 collective-permute-start.1
  19.7 3.1 %collective-permute-start = (f32[1024,128]{1,0:T(8,128)S(1)}, f32[1024,128]{1,0:T(8,128)S(1)}, u32[]{:S(2)}, u32[]{:S(2)}) collective-permute-start(f32[1024,128]{1,0:T(8,128)S(1)} %get-tuple-element.121), channel_id=1, source_target_pairs={{0,1},{1,2},{2,3},{3,4},{4,5},{5,6},{6,7},{7,8},{8,9},{9,10},{10,1... | collective-permute-start | bytes 1572872 | tf_op jit(solution)/shard_map/ppermute | solution.py:749
  22.9 25.2 %near_build.1 = (bf16[8,3,2,512,512]{4,3,2,1,0:T(8,128)(2,1)}, f32[8,64,512]{2,1,0:T(8,128)S(1)}) custom-call(f32[4096,128]{1,0:T(8,128)S(1)} %copy-done.7, f32[64,4096]{1,0:T(8,128)S(1)} %copy-done.8, f32[8,5]{1,0:T(8,128)S(1)} %compare_convert_fusion.mask_ref), custom_call_target="tpu_custom_call" | custom-call | tf_op jit(solution)/shard_map/near_build/pallas_call | solution.py:257
  48.1 1.3 collective-permute-start.6
  49.4 4.3 %collective-permute-start.5 = (f32[64,1024]{1,0:T(8,128)S(1)}, f32[64,1024]{1,0:T(8,128)S(1)}, u32[]{:S(2)}, u32[]{:S(2)}) collective-permute-start(f32[64,1024]{1,0:T(8,128)S(1)} %get-tuple-element.123), channel_id=1, source_target_pairs={{0,1},{1,2},{2,3},{3,4},{4,5},{5,6},{6,7},{7,8},{8,9},{9,10},{10,1... | collective-permute-start | bytes 786440 | tf_op jit(solution)/shard_map/ppermute | solution.py:749
  54.0 1.1 tree_stage.6
  55.1 4.5 %collective-permute-start.9 = (f32[192,256]{1,0:T(8,128)S(1)}, f32[192,256]{1,0:T(8,128)S(1)}, u32[]{:S(2)}, u32[]{:S(2)}) collective-permute-start(f32[192,256]{1,0:T(8,128)S(1)} %get-tuple-element.75.refs_1_), channel_id=1, source_target_pairs={{0,12},{1,13},{2,14},{3,15},{4,8},{5,9},{6,10},{7,11},{8,4},{9,5},... | collective-permute-start | bytes 589832 | tf_op jit(solution)/shard_map/ppermute | solution.py:762
  59.6 2.0 %collective-permute-start.8 = (f32[192,256]{1,0:T(8,128)S(1)}, f32[192,256]{1,0:T(8,128)S(1)}, u32[]{:S(2)}, u32[]{:S(2)}) collective-permute-start(f32[192,256]{1,0:T(8,128)S(1)} %get-tuple-element.75.refs_1_), channel_id=1, source_target_pairs={{0,8},{1,9},{2,10},{3,11},{4,12},{5,13},{6,14},{7,15},{8,0},{9,1},... | collective-permute-start | bytes 589832 | tf_op jit(solution)/shard_map/ppermute | solution.py:762
  61.6 3.3 %collective-permute-start.7 = (f32[192,256]{1,0:T(8,128)S(1)}, f32[192,256]{1,0:T(8,128)S(1)}, u32[]{:S(2)}, u32[]{:S(2)}) collective-permute-start(f32[192,256]{1,0:T(8,128)S(1)} %get-tuple-element.75.refs_1_), channel_id=1, source_target_pairs={{0,4},{1,5},{2,6},{3,7},{4,0},{5,1},{6,2},{7,3},{8,12},{9,13},{10,... | collective-permute-start | bytes 589832 | tf_op jit(solution)/shard_map/ppermute | solution.py:762
  65.0 5.1 %edge_build.1 = (bf16[6,512,512]{2,1,0:T(8,128)(2,1)S(1)}, bf16[6,512,512]{2,1,0:T(8,128)(2,1)S(1)}, f32[4,64,512]{2,1,0:T(8,128)S(1)}) custom-call(f32[4096,128]{1,0:T(8,128)S(1)} %copy-done.7, f32[4096,128]{1,0:T(8,128)S(1)} %copy-done.7, f32[1024,128]{1,0:T(8,128)S(1)} %collective-permute-done.lp_ref, f32[1024,128]{1,0:T(8,128)S(1)} %collective-permute-done.1.rp_ref, ...), custom_call_target="tpu_custom_call" | custom-call | tf_op jit(solution)/shard_map/edge_build/pallas_call | solution.py:356
  70.7 1.1 tree_stage.7
  71.8 4.1 %collective-permute-start.10 = (f32[192,256]{1,0:T(8,128)S(1)}, f32[192,256]{1,0:T(8,128)S(1)}, u32[]{:S(2)}, u32[]{:S(2)}) collective-permute-start(f32[192,256]{1,0:T(8,128)S(1)} %get-tuple-element.80.refs_1_), channel_id=1, source_target_pairs={{0,16},{1,17},{2,18},{3,19},{4,20},{5,21},{6,22},{7,23},{8,24},{9,... | collective-permute-start | bytes 589832 | tf_op jit(solution)/shard_map/ppermute | solution.py:762
  76.0 7.1 %collective-permute-done.10.refs_2_ = f32[192,256]{1,0:T(8,128)S(1)} collective-permute-done((f32[192,256]{1,0:T(8,128)S(1)}, f32[192,256]{1,0:T(8,128)S(1)}, u32[]{:S(2)}, u32[]{:S(2)}) %collective-permute-start.10) | collective-permute-done | bytes 196640 | tf_op jit(solution)/shard_map/ppermute | solution.py:762
  83.1 0.9 tree_stage.8
  84.1 6.5 %downward.2 = (f32[64,4096]{1,0:T(8,128)S(1)}, f32[64,1024]{1,0:T(8,128)}, f32[64,1024]{1,0:T(8,128)}, f32[32,256]{1,0:T(8,128)S(1)}) custom-call(s32[1]{0:T(128)} %bitcast.dev_ref.refs_0_, f32[64,4096]{1,0:T(8,128)S(1)} %copy-done.9, f32[8,64,512]{2,1,0:T(8,128)S(1)} %get-tuple-element.62.refs_2_, f32[4,64,512]{2,1,0:T(8,128)S(1)} %get-tuple-element.70.refs_3_, ...), custom_call_target="tpu_custom_call" | custom-call | tf_op jit(solution)/shard_map/downward/pallas_call | solution.py:584
  90.6 1.3 collective-permute-start.17
  92.0 1.5 collective-permute-start.18
  93.5 2.2 %upward.1 = (f32[96,256]{1,0:T(8,128)S(1)}, f32[14,64,256]{2,1,0:T(8,128)S(1)}) custom-call(s32[1]{0:T(128)} %bitcast.dev_ref.refs_0_, f32[64,4096]{1,0:T(8,128)S(1)} %get-tuple-element.92.vector_ref.refs_1_.image_ref.refs_3_, f32[32,256]{1,0:T(8,128)S(1)} %get-tuple-element.89.gram_ref, f32[8,512,256]{2,1,0:T(8,128)S(1)} %copy-done.3, ...), custom_call_target="tpu_custom_call" | custom-call | tf_op jit(solution)/shard_map/upward/pallas_call | solution.py:204
  96.6 4.3 %collective-permute-start.13 = (f32[96,256]{1,0:T(8,128)S(1)}, f32[96,256]{1,0:T(8,128)S(1)}, u32[]{:S(2)}, u32[]{:S(2)}) collective-permute-start(f32[96,256]{1,0:T(8,128)S(1)} %get-tuple-element.93.refs_1_), channel_id=1, source_target_pairs={{0,3},{1,2},{2,1},{3,0},{4,7},{5,6},{6,5},{7,4},{8,11},{9,10},{10,... | collective-permute-start | bytes 294920 | tf_op jit(solution)/shard_map/ppermute | solution.py:762
  100.8 1.6 collective-permute-start.12
  102.6 8.2 %copy-done.10 = bf16[8,3,2,512,512]{4,3,2,1,0:T(8,128)(2,1)S(1)} copy-done((bf16[8,3,2,512,512]{4,3,2,1,0:T(8,128)(2,1)S(1)}, bf16[8,3,2,512,512]{4,3,2,1,0:T(8,128)(2,1)}, u32[]{:S(2)}) %copy-start.10) | copy-done | bytes 25165848
  110.7 11.5 %near_apply.1.refs_2_ = f32[8,64,512]{2,1,0:T(8,128)S(1)} custom-call(bf16[8,3,2,512,512]{4,3,2,1,0:T(8,128)(2,1)S(1)} %copy-done.10, f32[64,4096]{1,0:T(8,128)S(1)} %get-tuple-element.92.vector_ref.refs_1_.image_ref.refs_3_, f32[8,5]{1,0:T(8,128)S(1)} %compare_convert_fusion.mask_ref), custom_call_target="tpu_custom_call" | custom-call | tf_op jit(solution)/shard_map/near_apply/pallas_call | solution.py:306
  124.9 2.0 %collective-permute-start.15 = (f32[96,256]{1,0:T(8,128)S(1)}, f32[96,256]{1,0:T(8,128)S(1)}, u32[]{:S(2)}, u32[]{:S(2)}) collective-permute-start(f32[96,256]{1,0:T(8,128)S(1)} %get-tuple-element.104.refs_1_), channel_id=1, source_target_pairs={{0,8},{1,9},{2,10},{3,11},{4,12},{5,13},{6,14},{7,15},{8,0},{9,1},... | collective-permute-start | bytes 294920 | tf_op jit(solution)/shard_map/ppermute | solution.py:762
  126.9 1.1 collective-permute-start.14
  128.6 1.9 %copy-done.13 = bf16[6,512,512]{2,1,0:T(8,128)(2,1)S(1)} copy-done((bf16[6,512,512]{2,1,0:T(8,128)(2,1)S(1)}, bf16[6,512,512]{2,1,0:T(8,128)(2,1)}, u32[]{:S(2)}) %copy-start.13) | copy-done | bytes 3145752
  130.5 0.9 copy-done.25
  131.5 1.8 %edge_apply.1.refs_3_ = f32[4,64,512]{2,1,0:T(8,128)S(1)} custom-call(bf16[6,512,512]{2,1,0:T(8,128)(2,1)S(1)} %get-tuple-element.98.hi_ref, bf16[6,512,512]{2,1,0:T(8,128)(2,1)S(1)} %copy-done.13, f32[64,1024]{1,0:T(8,128)S(1)} %collective-permute-done.17.lv_ref, f32[64,1024]{1,0:T(8,128)S(1)} %copy-done.25, f32[8,5]{1,0:T(8,128)S(1)} %compare_convert_fusion.mask_ref), custom_call_target="tpu_custom_call" | custom-call | tf_op jit(solution)/shard_map/edge_apply/pallas_call | solution.py:384
  133.9 2.5 %collective-permute-start.19 = (f32[96,256]{1,0:T(8,128)S(1)}, f32[96,256]{1,0:T(8,128)S(1)}, u32[]{:S(2)}, u32[]{:S(2)}) collective-permute-start(f32[96,256]{1,0:T(8,128)S(1)} %get-tuple-element.108.refs_1_), channel_id=1, source_target_pairs={{0,16},{1,17},{2,18},{3,19},{4,20},{5,21},{6,22},{7,23},{8,24},{9,... | collective-permute-start | bytes 294920 | tf_op jit(solution)/shard_map/ppermute | solution.py:762
  136.4 4.8 %collective-permute-done.19.refs_2_ = f32[96,256]{1,0:T(8,128)S(1)} collective-permute-done((f32[96,256]{1,0:T(8,128)S(1)}, f32[96,256]{1,0:T(8,128)S(1)}, u32[]{:S(2)}, u32[]{:S(2)}) %collective-permute-start.19) | collective-permute-done | bytes 98336 | tf_op jit(solution)/shard_map/ppermute | solution.py:762
  141.3 4.9 %downward.3.second_ref = f32[64,4096]{1,0:T(8,128)S(1)} custom-call(s32[1]{0:T(128)} %bitcast.dev_ref.refs_0_, f32[64,4096]{1,0:T(8,128)S(1)} %get-tuple-element.92.vector_ref.refs_1_.image_ref.refs_3_, f32[8,64,512]{2,1,0:T(8,128)S(1)} %near_apply.1.refs_2_, f32[4,64,512]{2,1,0:T(8,128)S(1)} %edge_apply.1.refs_3_, f32[8,512,256]{2,1,0:T(8,128)S(1)} %copy-done.3, ...), custom_call_target="tpu_custom_call" | custom-call | tf_op jit(solution)/shard_map/downward/pallas_call | solution.py:584
  146.2 5.3 %first_step.1 = (f32[64,4096]{1,0:T(8,128)S(1)}, f32[64,4096]{1,0:T(8,128)S(1)}, f32[64,256]{1,0:T(8,128)S(1)}, f32[128,128]{1,0:T(8,128)S(1)}) custom-call(f32[96,256]{1,0:T(8,128)S(1)} %get-tuple-element.109.gram_in, f32[64,4096]{1,0:T(8,128)S(1)} %copy-done.9, f32[64,4096]{1,0:T(8,128)S(1)} %get-tuple-element.92.vector_ref.refs_1_.image_ref.refs_3_, ...), custom_call_target="tpu_custom_call" | custom-call | tf_op jit(solution)/shard_map/first_step/pallas_call | solution.py:682
  153.4 2.4 %collective-permute-done.22 = f32[64,256]{1,0:T(8,128)S(1)} collective-permute-done((f32[64,256]{1,0:T(8,128)S(1)}, f32[64,256]{1,0:T(8,128)S(1)}, u32[]{:S(2)}, u32[]{:S(2)}) %collective-permute-start.22) | collective-permute-done | bytes 65568 | tf_op jit(solution)/shard_map/ppermute | solution.py:762
  155.9 1.4 collective-permute-done.21
  157.5 1.3 collective-permute-start.24
  158.9 2.0 %collective-permute-start.23 = (f32[64,256]{1,0:T(8,128)S(1)}, f32[64,256]{1,0:T(8,128)S(1)}, u32[]{:S(2)}, u32[]{:S(2)}) collective-permute-start(f32[64,256]{1,0:T(8,128)S(1)} %add_add_fusion.1), channel_id=1, source_target_pairs={{0,4},{1,5},{2,6},{3,7},{4,0},{5,1},{6,2},{7,3},{8,12},{9,13},{10,... | collective-permute-start | bytes 196616 | tf_op jit(solution)/shard_map/ppermute | solution.py:762
  160.9 2.2 %collective-permute-done.25 = f32[64,256]{1,0:T(8,128)S(1)} collective-permute-done((f32[64,256]{1,0:T(8,128)S(1)}, f32[64,256]{1,0:T(8,128)S(1)}, u32[]{:S(2)}, u32[]{:S(2)}) %collective-permute-start.25) | collective-permute-done | bytes 65568 | tf_op jit(solution)/shard_map/ppermute | solution.py:762
  163.8 1.5 collective-permute-start.26
  165.3 4.4 %collective-permute-done.26.refs_1_ = f32[64,256]{1,0:T(8,128)S(1)} collective-permute-done((f32[64,256]{1,0:T(8,128)S(1)}, f32[64,256]{1,0:T(8,128)S(1)}, u32[]{:S(2)}, u32[]{:S(2)}) %collective-permute-start.26) | collective-permute-done | bytes 65568 | tf_op jit(solution)/shard_map/ppermute | solution.py:762
  169.8 5.9 %last_step.1 = (f32[64,4096]{1,0:T(8,128)}, f32[64,4096]{1,0:T(8,128)}) custom-call(f32[128,128]{1,0:T(8,128)S(1)} %get-tuple-element.114.small_ref, f32[64,256]{1,0:T(8,128)S(1)} %add_add_fusion.refs_0_, f32[64,256]{1,0:T(8,128)S(1)} %collective-permute-done.26.refs_1_, f32[64,4096]{1,0:T(8,128)S(1)} %copy-done.9, ...), custom_call_target="tpu_custom_call" | custom-call | tf_op jit(solution)/shard_map/last_step/pallas_call | solution.py:728
  (89 shorter events, 10.2 us)
Async XLA Ops:
  0.6 2.0 %copy-start = (f32[7,2,256,256]{3,2,1,0:T(8,128)S(1)}, f32[7,2,256,256]{3,2,1,0:T(8,128)}, u32[]{:S(2)}) copy-start(f32[7,2,256,256]{3,2,1,0:T(8,128)} %refs_5_.13) | copy-start | bytes 11010052
  2.7 2.2 %copy-start.2 = (f32[8,512,256]{2,1,0:T(8,128)S(1)}, f32[8,512,256]{2,1,0:T(8,128)}, u32[]{:S(2)}) copy-start(f32[8,512,256]{2,1,0:T(8,128)} %refs_4_.3) | copy-start | bytes 12582916
  5.9 1.6 copy-start.6
  7.5 1.2 copy-start.8
  10.4 12.5 %copy-start.29 = (s32[8,5]{1,0:T(8,128)S(1)}, s32[8,5]{1,0:T(8,128)}, u32[]{:S(2)}) copy-start(s32[8,5]{1,0:T(8,128)} %param.10) | copy-start | bytes 484
  15.3 7.6 %copy-start.7 = (f32[4096,128]{1,0:T(8,128)S(1)}, f32[4096,128]{1,0:T(8,128)}, u32[]{:S(2)}) copy-start(f32[4096,128]{1,0:T(8,128)} %tail_ref.1) | copy-start | bytes 6291460
  15.3 32.8 %collective-permute-start.4 = (f32[192,256]{1,0:T(8,128)S(1)}, f32[192,256]{1,0:T(8,128)S(1)}, u32[]{:S(2)}, u32[]{:S(2)}) collective-permute-start(f32[192,256]{1,0:T(8,128)S(1)} %get-tuple-element.63.refs_1_), channel_id=1, source_target_pairs={{0,3},{1,2},{2,1},{3,0},{4,7},{5,6},{6,5},{7,4},{8,11},{9,10},{10,... | collective-permute-start | bytes 589832 | tf_op jit(solution)/shard_map/ppermute | solution.py:762
  17.7 31.7 %collective-permute-start.3 = (f32[192,256]{1,0:T(8,128)S(1)}, f32[192,256]{1,0:T(8,128)S(1)}, u32[]{:S(2)}, u32[]{:S(2)}) collective-permute-start(f32[192,256]{1,0:T(8,128)S(1)} %get-tuple-element.63.refs_1_), channel_id=1, source_target_pairs={{0,2},{1,3},{2,0},{3,1},{4,6},{5,7},{6,4},{7,5},{8,10},{9,11},{10,... | collective-permute-start | bytes 589832 | tf_op jit(solution)/shard_map/ppermute | solution.py:762
  18.2 35.7 %collective-permute-start.2 = (f32[192,256]{1,0:T(8,128)S(1)}, f32[192,256]{1,0:T(8,128)S(1)}, u32[]{:S(2)}, u32[]{:S(2)}) collective-permute-start(f32[192,256]{1,0:T(8,128)S(1)} %get-tuple-element.63.refs_1_), channel_id=1, source_target_pairs={{0,1},{1,0},{2,3},{3,2},{4,5},{5,4},{6,7},{7,6},{8,9},{9,8},{10,11... | collective-permute-start | bytes 589832 | tf_op jit(solution)/shard_map/ppermute | solution.py:762
  18.4 46.5 %collective-permute-start.1 = (f32[1024,128]{1,0:T(8,128)S(1)}, f32[1024,128]{1,0:T(8,128)S(1)}, u32[]{:S(2)}, u32[]{:S(2)}) collective-permute-start(f32[1024,128]{1,0:T(8,128)S(1)} %get-tuple-element.120), channel_id=1, source_target_pairs={{1,0},{2,1},{3,2},{4,3},{5,4},{6,5},{7,6},{8,7},{9,8},{10,9},{11,1... | collective-permute-start | bytes 1572872 | tf_op jit(solution)/shard_map/ppermute | solution.py:750
  19.7 45.2 %collective-permute-start = (f32[1024,128]{1,0:T(8,128)S(1)}, f32[1024,128]{1,0:T(8,128)S(1)}, u32[]{:S(2)}, u32[]{:S(2)}) collective-permute-start(f32[1024,128]{1,0:T(8,128)S(1)} %get-tuple-element.121), channel_id=1, source_target_pairs={{0,1},{1,2},{2,3},{3,4},{4,5},{5,6},{6,7},{7,8},{8,9},{9,10},{10,1... | collective-permute-start | bytes 1572872 | tf_op jit(solution)/shard_map/ppermute | solution.py:749
  48.1 11.5 %collective-permute-start.6 = (f32[64,1024]{1,0:T(8,128)S(1)}, f32[64,1024]{1,0:T(8,128)S(1)}, u32[]{:S(2)}, u32[]{:S(2)}) collective-permute-start(f32[64,1024]{1,0:T(8,128)S(1)} %get-tuple-element.122), channel_id=1, source_target_pairs={{1,0},{2,1},{3,2},{4,3},{5,4},{6,5},{7,6},{8,7},{9,8},{10,9},{11,1... | collective-permute-start | bytes 786440 | tf_op jit(solution)/shard_map/ppermute | solution.py:750
  49.4 12.2 %collective-permute-start.5 = (f32[64,1024]{1,0:T(8,128)S(1)}, f32[64,1024]{1,0:T(8,128)S(1)}, u32[]{:S(2)}, u32[]{:S(2)}) collective-permute-start(f32[64,1024]{1,0:T(8,128)S(1)} %get-tuple-element.123), channel_id=1, source_target_pairs={{0,1},{1,2},{2,3},{3,4},{4,5},{5,6},{6,7},{7,8},{8,9},{9,10},{10,1... | collective-permute-start | bytes 786440 | tf_op jit(solution)/shard_map/ppermute | solution.py:749
  55.1 28.9 %copy-start.14 = (bf16[2,256,256]{2,1,0:T(8,128)(2,1)}, bf16[2,256,256]{2,1,0:T(8,128)(2,1)S(1)}, u32[]{:S(2)}) copy-start(bf16[2,256,256]{2,1,0:T(8,128)(2,1)S(1)} %get-tuple-element.83.refs_14_) | copy-start | bytes 786436
  55.1 15.0 %collective-permute-start.9 = (f32[192,256]{1,0:T(8,128)S(1)}, f32[192,256]{1,0:T(8,128)S(1)}, u32[]{:S(2)}, u32[]{:S(2)}) collective-permute-start(f32[192,256]{1,0:T(8,128)S(1)} %get-tuple-element.75.refs_1_), channel_id=1, source_target_pairs={{0,12},{1,13},{2,14},{3,15},{4,8},{5,9},{6,10},{7,11},{8,4},{9,5},... | collective-permute-start | bytes 589832 | tf_op jit(solution)/shard_map/ppermute | solution.py:762
  59.6 11.0 %collective-permute-start.8 = (f32[192,256]{1,0:T(8,128)S(1)}, f32[192,256]{1,0:T(8,128)S(1)}, u32[]{:S(2)}, u32[]{:S(2)}) collective-permute-start(f32[192,256]{1,0:T(8,128)S(1)} %get-tuple-element.75.refs_1_), channel_id=1, source_target_pairs={{0,8},{1,9},{2,10},{3,11},{4,12},{5,13},{6,14},{7,15},{8,0},{9,1},... | collective-permute-start | bytes 589832 | tf_op jit(solution)/shard_map/ppermute | solution.py:762
  61.6 9.0 %collective-permute-start.7 = (f32[192,256]{1,0:T(8,128)S(1)}, f32[192,256]{1,0:T(8,128)S(1)}, u32[]{:S(2)}, u32[]{:S(2)}) collective-permute-start(f32[192,256]{1,0:T(8,128)S(1)} %get-tuple-element.75.refs_1_), channel_id=1, source_target_pairs={{0,4},{1,5},{2,6},{3,7},{4,0},{5,1},{6,2},{7,3},{8,12},{9,13},{10,... | collective-permute-start | bytes 589832 | tf_op jit(solution)/shard_map/ppermute | solution.py:762
  65.0 19.1 %copy-start.3 = (f32[8,512,256]{2,1,0:T(8,128)S(1)}, f32[8,512,256]{2,1,0:T(8,128)}, u32[]{:S(2)}) copy-start(f32[8,512,256]{2,1,0:T(8,128)} %refs_4_.3) | copy-start | bytes 12582916
  65.0 19.1 %copy-start.21 = (f32[14,64,256]{2,1,0:T(8,128)S(1)}, f32[14,64,256]{2,1,0:T(8,128)}, u32[]{:S(2)}) copy-start(f32[14,64,256]{2,1,0:T(8,128)} %copy-done.20) | copy-start | bytes 2752516
  70.1 13.9 %copy-start.12 = (bf16[6,512,512]{2,1,0:T(8,128)(2,1)}, bf16[6,512,512]{2,1,0:T(8,128)(2,1)S(1)}, u32[]{:S(2)}) copy-start(bf16[6,512,512]{2,1,0:T(8,128)(2,1)S(1)} %get-tuple-element.99.lo_ref) | copy-start | bytes 9437188
  70.1 13.9 %copy-start.1 = (f32[7,2,256,256]{3,2,1,0:T(8,128)S(1)}, f32[7,2,256,256]{3,2,1,0:T(8,128)}, u32[]{:S(2)}) copy-start(f32[7,2,256,256]{3,2,1,0:T(8,128)} %refs_5_.13) | copy-start | bytes 11010052
  70.1 13.9 %copy-start.9 = (f32[64,4096]{1,0:T(8,128)S(1)}, f32[64,4096]{1,0:T(8,128)}, u32[]{:S(2)}) copy-start(f32[64,4096]{1,0:T(8,128)} %refs_2_.1) | copy-start | bytes 3145732
  71.8 18.8 %copy-start.16 = (bf16[2,256,256]{2,1,0:T(8,128)(2,1)}, bf16[2,256,256]{2,1,0:T(8,128)(2,1)S(1)}, u32[]{:S(2)}) copy-start(bf16[2,256,256]{2,1,0:T(8,128)(2,1)S(1)} %get-tuple-element.84.refs_15_) | copy-start | bytes 786436
  71.8 18.8 %copy-start.18 = (bf16[2,256,256]{2,1,0:T(8,128)(2,1)}, bf16[2,256,256]{2,1,0:T(8,128)(2,1)S(1)}, u32[]{:S(2)}) copy-start(bf16[2,256,256]{2,1,0:T(8,128)(2,1)S(1)} %get-tuple-element.85.refs_16_) | copy-start | bytes 786436
  71.8 11.3 %collective-permute-start.10 = (f32[192,256]{1,0:T(8,128)S(1)}, f32[192,256]{1,0:T(8,128)S(1)}, u32[]{:S(2)}, u32[]{:S(2)}) collective-permute-start(f32[192,256]{1,0:T(8,128)S(1)} %get-tuple-element.80.refs_1_), channel_id=1, source_target_pairs={{0,16},{1,17},{2,18},{3,19},{4,20},{5,21},{6,22},{7,23},{8,24},{9,... | collective-permute-start | bytes 589832 | tf_op jit(solution)/shard_map/ppermute | solution.py:762
  90.6 37.3 %collective-permute-start.17 = (f32[64,1024]{1,0:T(8,128)}, f32[64,1024]{1,0:T(8,128)S(1)}, u32[]{:S(2)}, u32[]{:S(2)}) collective-permute-start(f32[64,1024]{1,0:T(8,128)} %get-tuple-element.100), channel_id=1, source_target_pairs={{0,1},{1,2},{2,3},{3,4},{4,5},{5,6},{6,7},{7,8},{8,9},{9,10},{10,1... | collective-permute-start | bytes 786440 | tf_op jit(solution)/shard_map/ppermute | solution.py:749
  92.0 36.0 %collective-permute-start.18 = (f32[64,1024]{1,0:T(8,128)}, f32[64,1024]{1,0:T(8,128)S(1)}, u32[]{:S(2)}, u32[]{:S(2)}) collective-permute-start(f32[64,1024]{1,0:T(8,128)} %get-tuple-element.101), channel_id=1, source_target_pairs={{1,0},{2,1},{3,2},{4,3},{5,4},{6,5},{7,6},{8,7},{9,8},{10,9},{11,1... | collective-permute-start | bytes 786440 | tf_op jit(solution)/shard_map/ppermute | solution.py:750
  96.6 25.7 %collective-permute-start.13 = (f32[96,256]{1,0:T(8,128)S(1)}, f32[96,256]{1,0:T(8,128)S(1)}, u32[]{:S(2)}, u32[]{:S(2)}) collective-permute-start(f32[96,256]{1,0:T(8,128)S(1)} %get-tuple-element.93.refs_1_), channel_id=1, source_target_pairs={{0,3},{1,2},{2,1},{3,0},{4,7},{5,6},{6,5},{7,4},{8,11},{9,10},{10,... | collective-permute-start | bytes 294920 | tf_op jit(solution)/shard_map/ppermute | solution.py:762
  100.8 21.4 %collective-permute-start.12 = (f32[96,256]{1,0:T(8,128)S(1)}, f32[96,256]{1,0:T(8,128)S(1)}, u32[]{:S(2)}, u32[]{:S(2)}) collective-permute-start(f32[96,256]{1,0:T(8,128)S(1)} %get-tuple-element.93.refs_1_), channel_id=1, source_target_pairs={{0,2},{1,3},{2,0},{3,1},{4,6},{5,7},{6,4},{7,5},{8,10},{9,11},{10,... | collective-permute-start | bytes 294920 | tf_op jit(solution)/shard_map/ppermute | solution.py:762
  102.5 19.8 %collective-permute-start.11 = (f32[96,256]{1,0:T(8,128)S(1)}, f32[96,256]{1,0:T(8,128)S(1)}, u32[]{:S(2)}, u32[]{:S(2)}) collective-permute-start(f32[96,256]{1,0:T(8,128)S(1)} %get-tuple-element.93.refs_1_), channel_id=1, source_target_pairs={{0,1},{1,0},{2,3},{3,2},{4,5},{5,4},{6,7},{7,6},{8,9},{9,8},{10,11... | collective-permute-start | bytes 294920 | tf_op jit(solution)/shard_map/ppermute | solution.py:762
  102.6 8.2 %copy-start.10 = (bf16[8,3,2,512,512]{4,3,2,1,0:T(8,128)(2,1)S(1)}, bf16[8,3,2,512,512]{4,3,2,1,0:T(8,128)(2,1)}, u32[]{:S(2)}) copy-start(bf16[8,3,2,512,512]{4,3,2,1,0:T(8,128)(2,1)} %get-tuple-element.91.tile_ref) | copy-start | bytes 75497472
  110.7 12.2 %copy-start.5 = (f32[510,256]{1,0:T(8,128)S(1)}, f32[510,256]{1,0:T(8,128)}, u32[]{:S(2)}) copy-start(f32[510,256]{1,0:T(8,128)} %refs_9_.3) | copy-start | bytes 1566724
  124.4 8.9 %collective-permute-start.16 = (f32[96,256]{1,0:T(8,128)S(1)}, f32[96,256]{1,0:T(8,128)S(1)}, u32[]{:S(2)}, u32[]{:S(2)}) collective-permute-start(f32[96,256]{1,0:T(8,128)S(1)} %get-tuple-element.104.refs_1_), channel_id=1, source_target_pairs={{0,12},{1,13},{2,14},{3,15},{4,8},{5,9},{6,10},{7,11},{8,4},{9,5},... | collective-permute-start | bytes 294920 | tf_op jit(solution)/shard_map/ppermute | solution.py:762
  124.9 8.4 %collective-permute-start.15 = (f32[96,256]{1,0:T(8,128)S(1)}, f32[96,256]{1,0:T(8,128)S(1)}, u32[]{:S(2)}, u32[]{:S(2)}) collective-permute-start(f32[96,256]{1,0:T(8,128)S(1)} %get-tuple-element.104.refs_1_), channel_id=1, source_target_pairs={{0,8},{1,9},{2,10},{3,11},{4,12},{5,13},{6,14},{7,15},{8,0},{9,1},... | collective-permute-start | bytes 294920 | tf_op jit(solution)/shard_map/ppermute | solution.py:762
  126.9 6.4 %collective-permute-start.14 = (f32[96,256]{1,0:T(8,128)S(1)}, f32[96,256]{1,0:T(8,128)S(1)}, u32[]{:S(2)}, u32[]{:S(2)}) collective-permute-start(f32[96,256]{1,0:T(8,128)S(1)} %get-tuple-element.104.refs_1_), channel_id=1, source_target_pairs={{0,4},{1,5},{2,6},{3,7},{4,0},{5,1},{6,2},{7,3},{8,12},{9,13},{10,... | collective-permute-start | bytes 294920 | tf_op jit(solution)/shard_map/ppermute | solution.py:762
  128.6 1.9 %copy-start.13 = (bf16[6,512,512]{2,1,0:T(8,128)(2,1)S(1)}, bf16[6,512,512]{2,1,0:T(8,128)(2,1)}, u32[]{:S(2)}) copy-start(bf16[6,512,512]{2,1,0:T(8,128)(2,1)} %copy-done.12) | copy-start | bytes 9437188
  131.5 9.8 %copy-start.15 = (bf16[2,256,256]{2,1,0:T(8,128)(2,1)S(1)}, bf16[2,256,256]{2,1,0:T(8,128)(2,1)}, u32[]{:S(2)}) copy-start(bf16[2,256,256]{2,1,0:T(8,128)(2,1)} %copy-done.14) | copy-start | bytes 786436
  131.5 9.8 %copy-start.17 = (bf16[2,256,256]{2,1,0:T(8,128)(2,1)S(1)}, bf16[2,256,256]{2,1,0:T(8,128)(2,1)}, u32[]{:S(2)}) copy-start(bf16[2,256,256]{2,1,0:T(8,128)(2,1)} %copy-done.16) | copy-start | bytes 786436
  131.5 9.8 %copy-start.19 = (bf16[2,256,256]{2,1,0:T(8,128)(2,1)S(1)}, bf16[2,256,256]{2,1,0:T(8,128)(2,1)}, u32[]{:S(2)}) copy-start(bf16[2,256,256]{2,1,0:T(8,128)(2,1)} %copy-done.18) | copy-start | bytes 786436
  131.5 9.8 %copy-start.23 = (f32[14,64,256]{2,1,0:T(8,128)S(1)}, f32[14,64,256]{2,1,0:T(8,128)}, u32[]{:S(2)}) copy-start(f32[14,64,256]{2,1,0:T(8,128)} %copy-done.22) | copy-start | bytes 2752516
  133.9 7.3 %collective-permute-start.19 = (f32[96,256]{1,0:T(8,128)S(1)}, f32[96,256]{1,0:T(8,128)S(1)}, u32[]{:S(2)}, u32[]{:S(2)}) collective-permute-start(f32[96,256]{1,0:T(8,128)S(1)} %get-tuple-element.108.refs_1_), channel_id=1, source_target_pairs={{0,16},{1,17},{2,18},{3,19},{4,20},{5,21},{6,22},{7,23},{8,24},{9,... | collective-permute-start | bytes 294920 | tf_op jit(solution)/shard_map/ppermute | solution.py:762
  151.5 4.4 %collective-permute-start.22 = (f32[64,256]{1,0:T(8,128)S(1)}, f32[64,256]{1,0:T(8,128)S(1)}, u32[]{:S(2)}, u32[]{:S(2)}) collective-permute-start(f32[64,256]{1,0:T(8,128)S(1)} %get-tuple-element.115), channel_id=1, source_target_pairs={{0,3},{1,2},{2,1},{3,0},{4,7},{5,6},{6,5},{7,4},{8,11},{9,10},{10,... | collective-permute-start | bytes 196616 | tf_op jit(solution)/shard_map/ppermute | solution.py:762
  152.3 5.0 %collective-permute-start.21 = (f32[64,256]{1,0:T(8,128)S(1)}, f32[64,256]{1,0:T(8,128)S(1)}, u32[]{:S(2)}, u32[]{:S(2)}) collective-permute-start(f32[64,256]{1,0:T(8,128)S(1)} %get-tuple-element.115), channel_id=1, source_target_pairs={{0,2},{1,3},{2,0},{3,1},{4,6},{5,7},{6,4},{7,5},{8,10},{9,11},{10,... | collective-permute-start | bytes 196616 | tf_op jit(solution)/shard_map/ppermute | solution.py:762
  153.0 4.3 %collective-permute-start.20 = (f32[64,256]{1,0:T(8,128)S(1)}, f32[64,256]{1,0:T(8,128)S(1)}, u32[]{:S(2)}, u32[]{:S(2)}) collective-permute-start(f32[64,256]{1,0:T(8,128)S(1)} %get-tuple-element.115), channel_id=1, source_target_pairs={{0,1},{1,0},{2,3},{3,2},{4,5},{5,4},{6,7},{7,6},{8,9},{9,8},{10,11... | collective-permute-start | bytes 196616 | tf_op jit(solution)/shard_map/ppermute | solution.py:762
  157.3 5.8 %collective-permute-start.25 = (f32[64,256]{1,0:T(8,128)S(1)}, f32[64,256]{1,0:T(8,128)S(1)}, u32[]{:S(2)}, u32[]{:S(2)}) collective-permute-start(f32[64,256]{1,0:T(8,128)S(1)} %add_add_fusion.1), channel_id=1, source_target_pairs={{0,12},{1,13},{2,14},{3,15},{4,8},{5,9},{6,10},{7,11},{8,4},{9,5},... | collective-permute-start | bytes 196616 | tf_op jit(solution)/shard_map/ppermute | solution.py:762
  157.5 5.5 %collective-permute-start.24 = (f32[64,256]{1,0:T(8,128)S(1)}, f32[64,256]{1,0:T(8,128)S(1)}, u32[]{:S(2)}, u32[]{:S(2)}) collective-permute-start(f32[64,256]{1,0:T(8,128)S(1)} %add_add_fusion.1), channel_id=1, source_target_pairs={{0,8},{1,9},{2,10},{3,11},{4,12},{5,13},{6,14},{7,15},{8,0},{9,1},... | collective-permute-start | bytes 196616 | tf_op jit(solution)/shard_map/ppermute | solution.py:762
  158.9 4.9 %collective-permute-start.23 = (f32[64,256]{1,0:T(8,128)S(1)}, f32[64,256]{1,0:T(8,128)S(1)}, u32[]{:S(2)}, u32[]{:S(2)}) collective-permute-start(f32[64,256]{1,0:T(8,128)S(1)} %add_add_fusion.1), channel_id=1, source_target_pairs={{0,4},{1,5},{2,6},{3,7},{4,0},{5,1},{6,2},{7,3},{8,12},{9,13},{10,... | collective-permute-start | bytes 196616 | tf_op jit(solution)/shard_map/ppermute | solution.py:762
  163.8 6.0 %collective-permute-start.26 = (f32[64,256]{1,0:T(8,128)S(1)}, f32[64,256]{1,0:T(8,128)S(1)}, u32[]{:S(2)}, u32[]{:S(2)}) collective-permute-start(f32[64,256]{1,0:T(8,128)S(1)} %add_add_fusion.refs_0_), channel_id=1, source_target_pairs={{0,16},{1,17},{2,18},{3,19},{4,20},{5,21},{6,22},{7,23},{8,24},{9,... | collective-permute-start | bytes 196616 | tf_op jit(solution)/shard_map/ppermute | solution.py:762
  (9 other events, 7.7 us)

commit v2 on v1

--- a/solution.py
+++ b/solution.py
@@ -92,12 +92,17 @@
     )
 
 
+def in_hbm(x):
+    return pltpu.with_memory_space_constraint(x, pltpu.HBM)
+
+
 def struct(shape, dtype=F32):
     return jax.ShapeDtypeStruct(shape, dtype)
 
 
 VM = pl.BlockSpec(memory_space=pltpu.VMEM)
 SM = pl.BlockSpec(memory_space=pltpu.SMEM)
+HBM = pl.BlockSpec(memory_space=pltpu.HBM)
 
 
 def climb_local(device, level, leaf_count, leaves, transfer_ref, gain_ref, local_ref):
@@ -119,25 +124,47 @@
     return level[0]
 
 
-def leaf_weights(vector_ref, interp_ref, leaf_count, leaf_size):
-    return [
-        times(stacked(vector_ref[:, j * leaf_size : (j + 1) * leaf_size]), *split(interp_ref[j]))
-        for j in range(leaf_count)
-    ]
-
-
-def front(device, points, vector, leaf_skeleton, node_skeleton, leaf_interp, transfer, node_gain, leaves):
+def leaf_weights(vector_ref, interp_ref, leaf_count, leaf_size, loads):
+    found = []
+    for j in range(leaf_count):
+        if loads is not None:
+            loads[j].wait()
+        found.append(times(stacked(vector_ref[:, j * leaf_size : (j + 1) * leaf_size]), *split(interp_ref[j])))
+    return found
+
+
+def front(device, points, vector, leaf_skeleton, node_skeleton, leaf_interp, transfer, node_gain, leaves, reach):
     dim = points.shape[1]
     leaf_count, leaf_size, skel_size = leaf_interp.shape
     classes = vector.shape[0]
     pair_count = leaf_count - 1
+    width = reach * leaf_size
     local_levels = leaf_count.bit_length() - 1
 
     def body(
-        dev_ref, points_ref, vector_ref, leaf_ref, node_ref, interp_ref, transfer_ref, gain_ref,
-        pack_ref, local_ref, hi_ref, lo_ref, rows_ref,
+        dev_ref, points_hbm, vector_hbm, leaf_ref, node_hbm, interp_hbm, transfer_hbm, gain_hbm,
+        pack_ref, local_ref, hi_ref, lo_ref, head_ref, tail_ref,
+        rows_ref, points_ref, vector_ref, interp_ref, transfer_ref, points_sem, vector_sem, interp_sem, transfer_sem,
+        node_ref, gain_ref, node_sem, gain_sem,
     ):
+        load_nodes = pltpu.make_async_copy(node_hbm, node_ref, node_sem)
+        load_gains = pltpu.make_async_copy(gain_hbm, gain_ref, gain_sem)
+        loads = [
+            pltpu.make_async_copy(
+                points_hbm.at[pl.ds(j * leaf_size, leaf_size)], points_ref.at[pl.ds(j * leaf_size, leaf_size)],
+                points_sem.at[j],
+            )
+            for j in range(leaf_count)
+        ]
+        load_vector = pltpu.make_async_copy(vector_hbm, vector_ref, vector_sem)
+        load_maps = pltpu.make_async_copy(transfer_hbm.at[pl.ds(0, local_levels)], transfer_ref, transfer_sem)
+        interp_loads = [
+            pltpu.make_async_copy(interp_hbm.at[j], interp_ref.at[j], interp_sem.at[j]) for j in range(leaf_count)
+        ]
+        for copy in [*loads, load_nodes, load_vector, *interp_loads, load_maps, load_gains]:
+            copy.start()
         device = dev_ref[0]
+        load_nodes.wait()
         rows_ref[...] = jnp.zeros_like(rows_ref)
         pair = 0
         for depth in range(1, local_levels + 1):
@@ -149,6 +176,7 @@
         leaf_columns, node_columns = columns(leaf_ref[...]), columns(rows_ref[...])
         level = []
         for j in range(leaf_count):
+            loads[j].wait()
             cat = scaled_cat(points_ref[j * leaf_size : (j + 1) * leaf_size, :])
             level.append(nn(one_hot(leaf_columns[:, j : j + 1], leaf_size), cat).astype(BF16))
         pair = 0
@@ -165,12 +193,20 @@
             level = above
         whole = level[0]
         pack_skel(pack_ref, classes, whole[:, :dim].astype(F32) + whole[:, dim:].astype(F32))
-        weights = leaf_weights(vector_ref, interp_ref, leaf_count, leaf_size)
+        load_vector.wait()
+        for ref, start in ((head_ref, 0), (tail_ref, (leaf_count - reach) * leaf_size)):
+            ref[:width, :] = points_ref[start : start + width, :]
+            for i in range(width // 128):
+                ref[width + i * classes : width + (i + 1) * classes, :] = vector_ref[
+                    :, start + i * 128 : start + (i + 1) * 128
+                ]
+        weights = leaf_weights(vector_ref, interp_ref, leaf_count, leaf_size, interp_loads)
+        load_maps.wait()
+        load_gains.wait()
         pack_ref[:classes] = climb_local(
             device, weights, leaf_count, leaves, transfer_ref, gain_ref, local_ref
         )
 
-    local_maps = pl.BlockSpec((local_levels,) + transfer.shape[1:], lambda i: (0, 0, 0, 0))
     return call(
         body,
         (
@@ -178,14 +214,32 @@
             struct((2 * leaf_count - 2, classes, skel_size)),
             struct((pair_count, skel_size, skel_size), BF16),
             struct((pair_count, skel_size, skel_size), BF16),
+            struct((width + width // 128 * classes, 128)),
+            struct((width + width // 128 * classes, 128)),
         ),
         "front",
         28,
-        grid=(1,),
-        in_specs=[SM, VM, VM, VM, VM, VM, local_maps, VM],
-        out_specs=(VM, VM, VM, VM),
-        scratch_shapes=[pltpu.VMEM((leaf_count, skel_size), jnp.int32)],
-    )(device, points, vector, leaf_skeleton, node_skeleton, leaf_interp, transfer, node_gain)
+        in_specs=[SM, HBM, HBM, VM, HBM, HBM, HBM, HBM],
+        out_specs=(VM,) * 6,
+        scratch_shapes=[
+            pltpu.VMEM((leaf_count, skel_size), jnp.int32),
+            pltpu.VMEM(points.shape, F32),
+            pltpu.VMEM(vector.shape, F32),
+            pltpu.VMEM(leaf_interp.shape, F32),
+            pltpu.VMEM((local_levels,) + transfer.shape[1:], F32),
+            pltpu.SemaphoreType.DMA((leaf_count,)),
+            pltpu.SemaphoreType.DMA,
+            pltpu.SemaphoreType.DMA((leaf_count,)),
+            pltpu.SemaphoreType.DMA,
+            pltpu.VMEM(node_skeleton.shape, jnp.int32),
+            pltpu.VMEM(node_gain.shape, F32),
+            pltpu.SemaphoreType.DMA,
+            pltpu.SemaphoreType.DMA,
+        ],
+    )(
+        device, in_hbm(points), in_hbm(vector), leaf_skeleton, in_hbm(node_skeleton), in_hbm(leaf_interp),
+        in_hbm(transfer), in_hbm(node_gain),
+    )
 
 
 def upward(device, vector, gram, leaf_interp, transfer, node_gain, leaves):
@@ -194,13 +248,12 @@
     local_levels = leaf_count.bit_length() - 1
 
     def body(dev_ref, vector_ref, gram_ref, interp_ref, transfer_ref, gain_ref, pack_ref, local_ref):
-        weights = leaf_weights(vector_ref, interp_ref, leaf_count, leaf_size)
+        weights = leaf_weights(vector_ref, interp_ref, leaf_count, leaf_size, None)
         pack_ref[:classes] = climb_local(
             dev_ref[0], weights, leaf_count, leaves, transfer_ref, gain_ref, local_ref
         )
         pack_ref[classes:] = gram_ref[...]
 
-    local_maps = pl.BlockSpec((local_levels,) + transfer.shape[1:], lambda i: (0, 0, 0, 0))
     return call(
         body,
         (
@@ -209,30 +262,49 @@
         ),
         "upward",
         18,
-        grid=(1,),
-        in_specs=[SM, VM, VM, VM, local_maps, VM],
+        in_specs=[SM, VM, VM, VM, VM, VM],
         out_specs=(VM, VM),
     )(device, vector, gram, leaf_interp, transfer, node_gain)
 
 
-def apply_tile(mask, cat_a, cat_b, hi, lo, out_ref, a, b):
-    out_ref[b] = out_ref[b] + mask * times(cat_a, hi, lo)
-    if cat_b is not None:
-        out_ref[a] = out_ref[a] + mask * times(cat_b, hi, lo, nt)
-
-
-def near_build(points, vector, near_mask, leaf_count, reach):
+def apply_tile(mask, cat, hi, lo, out_ref, place):
+    out_ref[place] = out_ref[place] + mask * times(cat, hi, lo)
+
+
+def near_pairs(t, leaf_count):
+    final = t == leaf_count - 2
+    third = (jnp.where(final, t + 1, t), jnp.where(final, t + 1, t + 2), jnp.where(final, 0.0, 1.0))
+    return [(t, t, None), (t, t + 1, 1.0), third]
+
+
+def near_products(pairs, mask_ref, vecs, tile_ref, out_ref, reach):
+    added = []
+    for e, (a, b, both) in enumerate(pairs):
+        mask = mask_ref[a, reach + b - a]
+        hi, lo = tile_ref[0, e, 0], tile_ref[0, e, 1]
+        added.append((b, mask * times(vecs[a], hi, lo)))
+        if both is not None:
+            added.append((a, (mask * both) * times(vecs[b], hi, lo, nt)))
+    own = added[0][1] + added[2][1]
+    out_ref[pairs[0][0]] = out_ref[pairs[0][0]] + own
+    for place, value in [added[1], *added[3:]]:
+        out_ref[place] = out_ref[place] + value
+
+
+def near_build(points, vector, near_mask, base, first, count, leaf_count, reach):
     dim = points.shape[1]
     leaf_size = points.shape[0] // leaf_count
     classes = vector.shape[0]
-
-    def body(points_ref, vector_ref, mask_ref, tile_ref, out_ref, cats, wides, rows, vecs):
-        a = pl.program_id(0)
-
-        @pl.when(a == 0)
+    used = range(first, min(first + count + 2, leaf_count))
+
+    def body(points_ref, vector_ref, mask_ref, *refs):
+        base_ref = refs[0] if base is not None else None
+        tile_ref, out_ref, cats, wides, rows, vecs = refs[-6:]
+
+        @pl.when(pl.program_id(0) == 0)
         def _():
-            out_ref[...] = jnp.zeros_like(out_ref)
-            for j in range(leaf_count):
+            out_ref[...] = jnp.zeros_like(out_ref) if base_ref is None else base_ref[...]
+            for j in used:
                 cat = scaled_cat(points_ref[j * leaf_size : (j + 1) * leaf_size, :])
                 cats[j] = cat
                 wide, row = half_norms(cat)
@@ -240,155 +312,201 @@
                 rows[j] = jnp.broadcast_to(row, (8, leaf_size))
                 vecs[j] = stacked(vector_ref[:, j * leaf_size : (j + 1) * leaf_size])
 
-        for step in range(reach + 1):
-
-            @pl.when(a + step < leaf_count)
-            def _():
-                b = a + step
-                tile = pair_tile(cats[a], cats[b], wides[a], rows[b][0:1, :])
-                tile_ref[0, step, 0], tile_ref[0, step, 1] = split(tile)
-                apply_tile(
-                    mask_ref[a, reach + step], vecs[a], vecs[b] if step else None,
-                    tile_ref[0, step, 0], tile_ref[0, step, 1], out_ref, a, b,
-                )
-
-    tile_block = pl.BlockSpec((1, reach + 1, 2, leaf_size, leaf_size), lambda a: (a, 0, 0, 0, 0))
-    tiles = struct((leaf_count, reach + 1, 2, leaf_size, leaf_size), BF16)
+        pairs = near_pairs(pl.program_id(0) + first, leaf_count)
+        for e, (a, b, _) in enumerate(pairs):
+            tile = pair_tile(cats[a], cats[b], wides[a], rows[b][0:1, :])
+            tile_ref[0, e, 0], tile_ref[0, e, 1] = split(tile)
+        near_products(pairs, mask_ref, vecs, tile_ref, out_ref, reach)
+
+    shape = (leaf_count, classes, leaf_size)
+    whole = pl.BlockSpec(shape, lambda a: (0, 0, 0))
     return call(
         body,
-        (tiles, struct((leaf_count, classes, leaf_size))),
+        (pltpu.HBM((count, 3, 2, leaf_size, leaf_size), BF16), struct(shape)),
         "near_build",
-        30,
-        grid=(leaf_count,),
+        34,
+        grid=(count,),
         in_specs=[
             pl.BlockSpec(points.shape, lambda a: (0, 0)),
             pl.BlockSpec(vector.shape, lambda a: (0, 0)),
             SM,
-        ],
-        out_specs=(
-            tile_block,
-            pl.BlockSpec((leaf_count, classes, leaf_size), lambda a: (0, 0, 0)),
-        ),
+        ] + ([] if base is None else [whole]),
+        out_specs=(pl.BlockSpec((1, 3, 2, leaf_size, leaf_size), lambda a: (a, 0, 0, 0, 0)), whole),
         scratch_shapes=[
             pltpu.VMEM((leaf_count, leaf_size, 2 * dim), BF16),
             pltpu.VMEM((leaf_count, leaf_size, 128), F32),
             pltpu.VMEM((leaf_count, 8, leaf_size), F32),
             pltpu.VMEM((leaf_count, 2 * classes, leaf_size), BF16),
         ],
-    )(points, vector, near_mask)
-
-
-def near_apply(tiles, vector, near_mask):
-    leaf_count, steps, _, leaf_size, _ = tiles.shape
-    reach = steps - 1
+    )(points, vector, near_mask, *([] if base is None else [base]))
+
+
+def near_apply(tiles, vector, near_mask, base, first, leaf_count, reach):
+    count, leaf_size = tiles.shape[0], tiles.shape[-1]
     classes = vector.shape[0]
 
-    def body(tile_ref, vector_ref, mask_ref, out_ref, vecs):
-        a = pl.program_id(0)
-
-        @pl.when(a == 0)
-        def _():
-            out_ref[...] = jnp.zeros_like(out_ref)
-            for j in range(leaf_count):
-                vecs[j] = stacked(vector_ref[:, j * leaf_size : (j + 1) * leaf_size])
-
-        for step in range(steps):
-
-            @pl.when(a + step < leaf_count)
+    def body(tile_hbm, vector_ref, mask_ref, *refs):
+        base_ref = refs[0] if base is not None else None
+        out_ref, vecs, tile_ref, sems = refs[-4:]
+        def loads(t):
+            return [pltpu.make_async_copy(tile_hbm.at[t, e], tile_ref.at[t, e], sems.at[t, e]) for e in range(3)]
+
+        for copy in loads(0):
+            copy.start()
+        out_ref[...] = jnp.zeros_like(out_ref) if base_ref is None else base_ref[...]
+        for j in range(first, min(first + count + 2, leaf_count)):
+            vecs[j] = stacked(vector_ref[:, j * leaf_size : (j + 1) * leaf_size])
+
+        @pl.loop(0, count)
+        def _(t):
+            for copy in loads(t):
+                copy.wait()
+
+            @pl.when(t + 1 < count)
             def _():
-                b = a + step
-                apply_tile(
-                    mask_ref[a, reach + step], vecs[a], vecs[b] if step else None,
-                    tile_ref[0, step, 0], tile_ref[0, step, 1], out_ref, a, b,
-                )
-
-    tile_block = pl.BlockSpec((1, steps, 2, leaf_size, leaf_size), lambda a: (a, 0, 0, 0, 0))
+                for copy in loads(t + 1):
+                    copy.start()
+
+            near_products(near_pairs(first + t, leaf_count), mask_ref, vecs, tile_ref.at[pl.ds(t, 1)], out_ref, reach)
+
     return call(
         body,
         struct((leaf_count, classes, leaf_size)),
         "near_apply",
         20,
-        grid=(leaf_count,),
-        in_specs=[tile_block, pl.BlockSpec(vector.shape, lambda a: (0, 0)), SM],
-        out_specs=pl.BlockSpec((leaf_count, classes, leaf_size), lambda a: (0, 0, 0)),
-        scratch_shapes=[pltpu.VMEM((leaf_count, 2 * classes, leaf_size), BF16)],
-    )(tiles, vector, near_mask)
+        in_specs=[HBM, VM, SM] + ([] if base is None else [VM]),
+        out_specs=VM,
+        scratch_shapes=[
+            pltpu.VMEM((leaf_count, 2 * classes, leaf_size), BF16),
+            pltpu.VMEM(tiles.shape, BF16),
+            pltpu.SemaphoreType.DMA((count, 3)),
+        ],
+    )(in_hbm(tiles), vector, near_mask, *([] if base is None else [base]))
 
 
 def edges(leaf_count, reach):
     found = []
-    for h in range(reach):
-        for j in range(reach):
-            offset = j - (h - reach)
-            if offset <= reach:
-                found.append((h, j, reach - offset))
-    for h in range(reach):
-        for j in range(leaf_count - reach, leaf_count):
-            offset = leaf_count + h - j
-            if offset <= reach:
-                found.append((reach + h, j, reach + offset))
-    return found
-
-
-def edge_build(points, left_points, right_points, left_rows, right_rows, near_mask, leaf_count, reach):
+    for side in range(2):
+        for h in range(reach):
+            for j in range(reach):
+                own = j if side == 0 else leaf_count - reach + j
+                offset = h - reach - own if side == 0 else leaf_count + h - own
+                if -reach <= offset <= reach:
+                    found.append((side, h, j, own, reach + offset))
+    return jnp.array(found, jnp.int32)
+
+
+def edge_build(points, left, right, near_mask, classes, leaf_count, reach):
     dim = points.shape[1]
     leaf_size = points.shape[0] // leaf_count
+    lanes = leaf_size // 128
+    width = reach * leaf_size
+    border = edges(leaf_count, reach)
+    count = border.shape[0]
+
+    def body(own_hbm, left_hbm, right_hbm, mask_ref, border_ref, tile_hbm, out_ref, tile_ref, halo_ref, own_ref, sems, out_sems):
+        tail = pl.ds((leaf_count - reach) * leaf_size, width)
+        loads = [
+            pltpu.make_async_copy(src, dst, sems.at[i])
+            for i, (src, dst) in enumerate(
+                [
+                    (left_hbm, halo_ref.at[0]), (right_hbm, halo_ref.at[1]),
+                    (own_hbm.at[pl.ds(0, width)], own_ref.at[0]), (own_hbm.at[tail], own_ref.at[1]),
+                ]
+            )
+        ]
+        for copy in loads:
+            copy.start()
+        out_ref[...] = jnp.zeros_like(out_ref)
+        for copy in loads:
+            copy.wait()
+
+        def cat_of(ref, i, spot):
+            return scaled_cat(ref[i, pl.ds(pl.multiple_of(spot * leaf_size, leaf_size), leaf_size), :])
+
+        def rows_of(i, spot):
+            firsts = [pl.multiple_of(width + (spot * lanes + n) * classes, classes) for n in range(lanes)]
+            return jnp.concatenate([halo_ref[i, pl.ds(f, classes), :] for f in firsts], axis=1)
+
+        def store(t):
+            return pltpu.make_async_copy(tile_ref.at[t], tile_hbm.at[t], out_sems.at[t])
+
+        @pl.loop(0, count)
+        def _(t):
+            side, h, j, own, slot = [border_ref[t, i] for i in range(5)]
+            cat_h, cat_j = cat_of(halo_ref, side, h), cat_of(own_ref, side, j)
+            tile = pair_tile(cat_h, cat_j, half_norms(cat_h)[0], half_norms(cat_j)[1])
+            tile_ref[t, 0], tile_ref[t, 1] = split(tile)
+            store(t).start()
+            apply_tile(
+                mask_ref[own, slot], stacked(rows_of(side, h)), tile_ref[t, 0], tile_ref[t, 1], out_ref,
+                side * reach + j,
+            )
+
+        @pl.loop(0, count)
+        def _(t):
+            store(t).wait()
+
+    shape = (count, 2, leaf_size, leaf_size)
+    return call(
+        body,
+        (pltpu.HBM(shape, BF16), struct((2 * reach, classes, leaf_size))),
+        "edge_build",
+        22,
+        in_specs=[HBM, HBM, HBM, SM, SM],
+        out_specs=(HBM, VM),
+        scratch_shapes=[
+            pltpu.VMEM(shape, BF16),
+            pltpu.VMEM((2,) + left.shape, F32),
+            pltpu.VMEM((2, width, dim), F32),
+            pltpu.SemaphoreType.DMA((4,)),
+            pltpu.SemaphoreType.DMA((count,)),
+        ],
+    )(in_hbm(points), in_hbm(left), in_hbm(right), near_mask, border)
+
+
+def edge_apply(tiles, left_rows, right_rows, near_mask, leaf_count, reach):
+    count, leaf_size = tiles.shape[0], tiles.shape[-1]
     classes = left_rows.shape[0]
-    border = edges(leaf_count, reach)
-
-    def body(head_ref, tail_ref, lp_ref, rp_ref, lv_ref, rv_ref, mask_ref, hi_ref, lo_ref, out_ref):
+
+    def body(tile_hbm, lv_ref, rv_ref, mask_ref, border_ref, out_ref, tile_ref, vecs, sems):
+        def load(t):
+            return pltpu.make_async_copy(tile_hbm.at[t], tile_ref.at[t], sems.at[t])
+
+        for t in range(min(3, count)):
+            load(t).start()
         out_ref[...] = jnp.zeros_like(out_ref)
-        for t, (h, j, slot) in enumerate(border):
-            hs, hv = (lp_ref, lv_ref) if h < reach else (rp_ref, rv_ref)
-            spot = h % reach
-            where = slice(spot * leaf_size, (spot + 1) * leaf_size)
-            cat_h = scaled_cat(hs[where, :])
-            own_ref, own = (head_ref, j) if j < reach else (tail_ref, j - (leaf_count - reach))
-            cat_j = scaled_cat(own_ref[own * leaf_size : (own + 1) * leaf_size, :])
-            tile = pair_tile(cat_h, cat_j, half_norms(cat_h)[0], half_norms(cat_j)[1])
-            hi_ref[t], lo_ref[t] = split(tile)
-            spot = j if j < reach else reach + j - (leaf_count - reach)
-            apply_tile(mask_ref[j, slot], stacked(hv[:, where]), None, hi_ref[t], lo_ref[t], out_ref, 0, spot)
-
-    block = (reach * leaf_size, dim)
-    last = leaf_count // reach - 1
-    tiles = struct((len(border), leaf_size, leaf_size), BF16)
-    return call(
-        body,
-        (tiles, tiles, struct((2 * reach, classes, leaf_size))),
-        "edge_build",
-        20,
-        grid=(1,),
-        in_specs=[
-            pl.BlockSpec(block, lambda i: (0, 0)),
-            pl.BlockSpec(block, lambda i: (last, 0)),
-            VM, VM, VM, VM, SM,
-        ],
-        out_specs=(VM, VM, VM),
-    )(points, points, left_points, right_points, left_rows, right_rows, near_mask)
-
-
-def edge_apply(hi_tiles, lo_tiles, left_rows, right_rows, near_mask, leaf_count, reach):
-    leaf_size = hi_tiles.shape[1]
-    classes = left_rows.shape[0]
-    border = edges(leaf_count, reach)
-
-    def body(hi_ref, lo_ref, lv_ref, rv_ref, mask_ref, out_ref):
-        out_ref[...] = jnp.zeros_like(out_ref)
-        for t, (h, j, slot) in enumerate(border):
-            hv = lv_ref if h < reach else rv_ref
-            where = slice((h % reach) * leaf_size, (h % reach + 1) * leaf_size)
-            spot = j if j < reach else reach + j - (leaf_count - reach)
-            apply_tile(mask_ref[j, slot], stacked(hv[:, where]), None, hi_ref[t], lo_ref[t], out_ref, 0, spot)
+        for h in range(reach):
+            where = slice(h * leaf_size, (h + 1) * leaf_size)
+            vecs[0, h] = stacked(lv_ref[:, where])
+            vecs[1, h] = stacked(rv_ref[:, where])
+
+        @pl.loop(0, count)
+        def _(t):
+            side, h, j, own, slot = [border_ref[t, i] for i in range(5)]
+            load(t).wait()
+
+            @pl.when(t + 3 < count)
+            def _():
+                load(t + 3).start()
+
+            apply_tile(
+                mask_ref[own, slot], vecs[side, h], tile_ref[t, 0], tile_ref[t, 1], out_ref, side * reach + j
+            )
 
     return call(
         body,
         struct((2 * reach, classes, leaf_size)),
         "edge_apply",
         14,
-        in_specs=[VM, VM, VM, VM, SM],
+        in_specs=[HBM, VM, VM, SM, SM],
         out_specs=VM,
-    )(hi_tiles, lo_tiles, left_rows, right_rows, near_mask)
+        scratch_shapes=[
+            pltpu.VMEM(tiles.shape, BF16),
+            pltpu.VMEM((2, reach, 2 * classes, leaf_size), BF16),
+            pltpu.SemaphoreType.DMA((count,)),
+        ],
+    )(in_hbm(tiles), left_rows, right_rows, near_mask, edges(leaf_count, reach))
 
 
 def tree_stage(device, packs, node_gain, transfer, node_skeleton, classes, leaves, level, bit, with_skel, extra, climb):
@@ -504,7 +622,7 @@
     stages = len(siblings)
 
     def body(*refs):
-        dev_ref, vector_ref, near_ref, edge_ref, interp_hbm, transfer_hbm = refs[:6]
+        dev_ref, vector_ref, near_ref, edge_ref, interp_ref, maps_ref = refs[:6]
         weights_ref, tiles_hi, tiles_lo, gain_ref = refs[6:10]
         sib_refs = refs[10 : 10 + stages]
         dev_refs = refs[10 + stages : 10 + 3 * stages]
@@ -517,16 +635,10 @@
         image_ref = rest.pop(0)
         head_ref, tail_ref = (rest.pop(0), rest.pop(0)) if start else (None, None)
         gram_ref = rest.pop(0) if start else None
-        interp_ref, maps_ref, interp_sem, maps_sem = rest
-        load_maps = pltpu.make_async_copy(transfer_hbm, maps_ref, maps_sem)
-        load_interp = pltpu.make_async_copy(interp_hbm, interp_ref, interp_sem)
-        load_maps.start()
-        load_interp.start()
         local = []
         for s in range(stages):
             for i in range(sib_refs[s].shape[0]):
                 local.append(times(stacked(sib_refs[s][i]), dev_refs[2 * s][i], dev_refs[2 * s + 1][i]))
-        load_maps.wait()
         top = len(local) - 1
         potential = local[top]
         for b in range(top - 1, -1, -1):
@@ -549,7 +661,6 @@
                 carried = sides[c][p * classes : (p + 1) * classes]
                 below.append(carried * gain(depth, device * count + n) + direct)
             level = below
-        load_interp.wait()
         for j in range(leaf_count):
             where = slice(j * leaf_size, (j + 1) * leaf_size)
             total = ridge * vector_ref[:, where] + near_ref[j]
@@ -579,8 +690,7 @@
     ins += list(siblings)
     for pair in device_tiles:
         ins += list(pair)
-    anywhere = pl.BlockSpec(memory_space=pl.ANY)
-    specs = [SM, VM, VM, VM, anywhere, anywhere] + [VM] * (len(ins) - 6)
+    specs = [SM] + [VM] * (len(ins) - 1)
     return call(
         body,
         tuple(out),
@@ -588,12 +698,6 @@
         30,
         in_specs=specs,
         out_specs=tuple([VM] * len(out)),
-        scratch_shapes=[
-            pltpu.VMEM(leaf_interp.shape, F32),
-            pltpu.VMEM(transfer.shape, F32),
-            pltpu.SemaphoreType.DMA,
-            pltpu.SemaphoreType.DMA,
-        ],
     )(*ins)
 
 
@@ -750,13 +854,6 @@
         right = lax.ppermute(head, "leaf", [(i + 1, i) for i in range(ends)])
         return left, right
 
-    def halo(rows, axis):
-        width = reach * leaf_size
-        size = rows.shape[axis]
-        return exchange(
-            lax.slice_in_dim(rows, 0, width, axis=axis), lax.slice_in_dim(rows, size - width, size, axis=axis)
-        )
-
     def group(pack, first_bit, count):
         return [pack] + [
             lax.ppermute(pack, "leaf", [(d, d ^ (i << first_bit)) for d in range(dev_count)])
@@ -790,40 +887,59 @@
     def after(pack, *values):
         return lax.optimization_barrier((pack, values))[1]
 
-    left_points, right_points = halo(points, 0)
-    left_rows, right_rows = halo(right_side, 1)
-    pack, weights, *local_tiles = front(
-        device, points, right_side, leaf_skeleton, node_skeleton, leaf_interp, transfer, node_gain, leaves
-    )
-
-    def build_near(pack):
-        (vector,) = after(pack, right_side)
-        return near_build(points, vector, near_mask, leaf_count, reach)
-
-    def build_edge(pack):
-        left, right = after(pack, left_rows, right_rows)
-        return edge_build(points, left_points, right_points, left, right, near_mask, leaf_count, reach)
-
-    siblings, device_tiles, _, results = climb(pack, True, False, [build_near, build_edge])
-    (near_tiles, near), (edge_hi, edge_lo, edge) = results
+    assert reach == 2
+    steps = leaf_count - 1
+    cuts = [0, -(-steps * 3 // 7), -(-steps * 5 // 7), steps]
+
+    pack, weights, *local_tiles, head, tail = front(
+        device, points, right_side, leaf_skeleton, node_skeleton, leaf_interp, transfer, node_gain, leaves, reach
+    )
+    left, right = exchange(head, tail)
+    near_tiles, total = [], [None]
+
+    def build(part):
+        def run(pack):
+            (vector,) = after(pack, right_side)
+            tiles, total[0] = near_build(
+                points, vector, near_mask, total[0], cuts[part], cuts[part + 1] - cuts[part], leaf_count, reach
+            )
+            near_tiles.append(tiles)
+            return total[0],
+
+        return run
+
+    def build_last(pack):
+        build(2)(pack)
+        left_pack, right_pack, _ = after(pack, left, right, total[0])
+        return edge_build(points, left_pack, right_pack, near_mask, classes, leaf_count, reach)
+
+    siblings, device_tiles, _, results = climb(pack, True, False, [build(0), build(1), build_last])
+    near = total[0]
+    edge_tiles, edge = results[2]
     image, head, tail, gram = downward(
         device, right_side, near, edge, leaf_interp, transfer, weights, local_tiles, node_gain,
         siblings, device_tiles, reach, leaves, True,
     )
 
-    left_rows, right_rows = exchange(head, tail)
     pack, weights = upward(device, image, gram, leaf_interp, transfer, node_gain, leaves)
-
-    def apply_near(pack):
-        (vector,) = after(pack, image)
-        return (near_apply(near_tiles, vector, near_mask),)
-
-    def apply_edge(pack):
-        left, right = after(pack, left_rows, right_rows)
-        return (edge_apply(edge_hi, edge_lo, left, right, near_mask, leaf_count, reach),)
-
-    siblings, _, pack, results = climb(pack, False, True, [apply_near, apply_edge])
-    (near,), (edge,) = results
+    left_rows, right_rows = exchange(*after(pack, head, tail))
+    total = [None]
+
+    def apply(part):
+        def run(pack):
+            (vector,) = after(pack, image)
+            total[0] = near_apply(near_tiles[part], vector, near_mask, total[0], cuts[part], leaf_count, reach)
+            return total[0],
+
+        return run
+
+    def apply_last(pack):
+        apply(2)(pack)
+        left, right, _ = after(pack, left_rows, right_rows, total[0])
+        return (edge_apply(edge_tiles, left, right, near_mask, leaf_count, reach),)
+
+    siblings, _, pack, results = climb(pack, False, True, [apply(0), apply(1), apply_last])
+    near, (edge,) = total[0], results[2]
     (second,) = downward(
         device, image, near, edge, leaf_interp, transfer, weights, local_tiles, node_gain,
         siblings, device_tiles, reach, leaves, False,

time: 176 us -> 149 us (0.85)
  local copies, waits for them, and re-layouts: 25.2 us -> 2.18 us
  Pallas kernels: 76.7 us -> 92.2 us
  waiting for transfers between devices: 23.7 us -> 13.6 us
  starting transfers between devices: 49 us -> 39.3 us
    unnamed x60 -> x22, local copies, waits for them, and re-layouts: 24.8 us -> 2 us
    ppermute x21, waiting for transfers between devices: 23.7 us -> 13.6 us  [group(): lax.ppermute(pack, 'leaf', [(d, d ^ i << first_bit) for d in range(dev_co...]
    pallas_call x3 -> x7, Pallas kernels: 41.8 us -> 50.4 us  [the longest x3 23.3 us: near_build(): call(body, (pltpu.HBM((count, 3, 2, leaf_size, leaf_size), BF16), struct(...]
    pallas_call x1, Pallas kernels: 3.96 us -> 10.4 us  [front(): call(body, (struct((classes + skel_size // 2, skel_size)), struct((2 * le...]
    ppermute x3 -> x2, starting transfers between devices: 8.7 us -> 4.32 us  [exchange(): left = lax.ppermute(tail, 'leaf', [(i, i + 1) for i in range(ends)])]
    ppermute x21, starting transfers between devices: 36.2 us -> 32.3 us  [group(): lax.ppermute(pack, 'leaf', [(d, d ^ i << first_bit) for d in range(dev_co...]
    pallas_call x1, Pallas kernels: 1.76 us -> 4.48 us  [edge_apply(): call(body, struct((2 * reach, classes, leaf_size)), 'edge_apply', 14, in_...]
    pallas_call x2, Pallas kernels: 11.4 us -> 9.13 us  [downward(): call(body, tuple(out), 'downward', 30, in_specs=specs, out_specs=tuple([V...]
  transfers between devices with their start and end apart: 27 -> 25, of which waited for: 8 -> 7; matrix products, arithmetic and copies ran while one was open for 0% -> 0% of each run, Pallas kernels for 27% -> 39%
where the time goes in v2:
time: 149 us; the launch traced here: 148 us
  Pallas kernels  92.2 us (62%)
  starting transfers between devices  39.3 us (26%)
  waiting for transfers between devices  13.6 us (9%)
  local copies, waits for them, and re-layouts  2.18 us (1%)
    ppermute x21, starting transfers between devices, group(): lax.ppermute(pack, 'leaf', [(d, d ^ i << first_bit) for d in range(dev_co...  32.3 us
    pallas_call x3, Pallas kernels, near_build(): call(body, (pltpu.HBM((count, 3, 2, leaf_size, leaf_size), BF16), struct(...  23.3 us
    pallas_call x3, Pallas kernels, near_apply(): call(body, struct((leaf_count, classes, leaf_size)), 'near_apply', 20, in...  18.9 us
    ppermute x21, waiting for transfers between devices, group(): lax.ppermute(pack, 'leaf', [(d, d ^ i << first_bit) for d in range(dev_co...  13.6 us
    pallas_call x1, Pallas kernels, front(): call(body, (struct((classes + skel_size // 2, skel_size)), struct((2 * le...  10.4 us
    pallas_call x2, Pallas kernels, downward(): call(body, tuple(out), 'downward', 30, in_specs=specs, out_specs=tuple([V...  9.13 us
    pallas_call x1, Pallas kernels, edge_build(): call(body, (pltpu.HBM(shape, BF16), struct((2 * reach, classes, leaf_size...  8.23 us
    pallas_call x1, Pallas kernels, last_step(): call(body, (struct(right_side.shape), struct(right_side.shape)), 'last_st...  5.91 us
  transfers between devices with their start and end apart: 25, of which 7 were waited for; matrix products, arithmetic and copies ran while one was open for 0% of the time, Pallas kernels for 39%

profile of v2, /device:TPU:0, one launch (start us, length us, event | category | flops | bytes accessed | tf_op | source)
XLA Modules:
  0.0 148.4 jit_solution(7671523918358216731)
XLA Ops:
  0.7 0.8 copy-done.7
  1.5 10.4 %front.1 = (f32[192,256]{1,0:T(8,128)S(1)}, f32[14,64,256]{2,1,0:T(8,128)S(1)}, bf16[7,256,256]{2,1,0:T(8,128)(2,1)S(1)}, bf16[7,256,256]{2,1,0:T(8,128)(2,1)S(1...) custom-call(s32[1]{0:T(128)} %bitcast.dev_ref.refs_0_, f32[4096,128]{1,0:T(8,128)} %own_hbm.1, f32[64,4096]{1,0:T(8,128)} %refs_2_.1, ...), custom_call_target="tpu_custom_call" | custom-call | tf_op jit(solution)/shard_map/front/pallas_call | solution.py:210
  12.0 0.6 collective-permute-start
  12.5 2.6 %collective-permute-start.1 = (f32[192,256]{1,0:T(8,128)S(1)}, f32[192,256]{1,0:T(8,128)S(1)}, u32[]{:S(2)}, u32[]{:S(2)}) collective-permute-start(f32[192,256]{1,0:T(8,128)S(1)} %get-tuple-element.78.refs_1_), channel_id=1, source_target_pairs={{0,2},{1,3},{2,0},{3,1},{4,6},{5,7},{6,4},{7,5},{8,10},{9,11},{10,... | collective-permute-start | bytes 589832 | tf_op jit(solution)/shard_map/ppermute | solution.py:859
  15.1 2.1 %collective-permute-start.6 = (f32[1536,128]{1,0:T(8,128)S(1)}, f32[1536,128]{1,0:T(8,128)S(1)}, u32[]{:S(2)}, u32[]{:S(2)}) collective-permute-start(f32[1536,128]{1,0:T(8,128)S(1)} %get-tuple-element.92), channel_id=1, source_target_pairs={{0,1},{1,2},{2,3},{3,4},{4,5},{5,6},{6,7},{7,8},{8,9},{9,10},{10,1... | collective-permute-start | bytes 2359304 | tf_op jit(solution)/shard_map/ppermute | solution.py:853
  17.2 1.5 collective-permute-start.7
  18.7 9.5 %near_build.3 = (bf16[3,3,2,512,512]{4,3,2,1,0:T(8,128)(2,1)}, f32[8,64,512]{2,1,0:T(8,128)S(1)}) custom-call(f32[4096,128]{1,0:T(8,128)S(1)} %copy-done.2, f32[64,4096]{1,0:T(8,128)S(1)} %copy-done.4, f32[8,5]{1,0:T(8,128)S(1)} %compare_convert_fusion.mask_ref), custom_call_target="tpu_custom_call" | custom-call | tf_op jit(solution)/shard_map/near_build/pallas_call | solution.py:323
  28.4 1.1 tree_stage.6
  29.5 4.9 %collective-permute-start.3 = (f32[192,256]{1,0:T(8,128)S(1)}, f32[192,256]{1,0:T(8,128)S(1)}, u32[]{:S(2)}, u32[]{:S(2)}) collective-permute-start(f32[192,256]{1,0:T(8,128)S(1)} %get-tuple-element.85.refs_1_), channel_id=1, source_target_pairs={{0,4},{1,5},{2,6},{3,7},{4,0},{5,1},{6,2},{7,3},{8,12},{9,13},{10,... | collective-permute-start | bytes 589832 | tf_op jit(solution)/shard_map/ppermute | solution.py:859
  34.4 2.8 %collective-permute-start.4 = (f32[192,256]{1,0:T(8,128)S(1)}, f32[192,256]{1,0:T(8,128)S(1)}, u32[]{:S(2)}, u32[]{:S(2)}) collective-permute-start(f32[192,256]{1,0:T(8,128)S(1)} %get-tuple-element.85.refs_1_), channel_id=1, source_target_pairs={{0,8},{1,9},{2,10},{3,11},{4,12},{5,13},{6,14},{7,15},{8,0},{9,1},... | collective-permute-start | bytes 589832 | tf_op jit(solution)/shard_map/ppermute | solution.py:859
  37.2 6.9 %near_build.4 = (bf16[2,3,2,512,512]{4,3,2,1,0:T(8,128)(2,1)}, f32[8,64,512]{2,1,0:T(8,128)S(1)}) custom-call(f32[4096,128]{1,0:T(8,128)S(1)} %copy-done.2, f32[64,4096]{1,0:T(8,128)S(1)} %copy-done.4, f32[8,5]{1,0:T(8,128)S(1)} %compare_convert_fusion.mask_ref, f32[8,64,512]{2,1,0:T(8,128)S(1)} %get-tuple-element.77.refs_0_), custom_call_target="tpu_custom_call" | custom-call | tf_op jit(solution)/shard_map/near_build/pallas_call | solution.py:323
  44.2 2.5 %collective-permute-done.5.refs_4_ = f32[192,256]{1,0:T(8,128)S(1)} collective-permute-done((f32[192,256]{1,0:T(8,128)S(1)}, f32[192,256]{1,0:T(8,128)S(1)}, u32[]{:S(2)}, u32[]{:S(2)}) %collective-permute-start.5) | collective-permute-done | bytes 196640 | tf_op jit(solution)/shard_map/ppermute | solution.py:859
  46.7 1.1 tree_stage.7
  47.8 2.8 %collective-permute-start.8 = (f32[192,256]{1,0:T(8,128)S(1)}, f32[192,256]{1,0:T(8,128)S(1)}, u32[]{:S(2)}, u32[]{:S(2)}) collective-permute-start(f32[192,256]{1,0:T(8,128)S(1)} %get-tuple-element.102.refs_1_), channel_id=1, source_target_pairs={{0,16},{1,17},{2,18},{3,19},{4,20},{5,21},{6,22},{7,23},{8,24},{9,... | collective-permute-start | bytes 589832 | tf_op jit(solution)/shard_map/ppermute | solution.py:859
  50.6 6.9 %near_build.5 = (bf16[2,3,2,512,512]{4,3,2,1,0:T(8,128)(2,1)}, f32[8,64,512]{2,1,0:T(8,128)S(1)}) custom-call(f32[4096,128]{1,0:T(8,128)S(1)} %copy-done.2, f32[64,4096]{1,0:T(8,128)S(1)} %copy-done.4, f32[8,5]{1,0:T(8,128)S(1)} %compare_convert_fusion.mask_ref, f32[8,64,512]{2,1,0:T(8,128)S(1)} %get-tuple-element.84.refs_0_), custom_call_target="tpu_custom_call" | custom-call | tf_op jit(solution)/shard_map/near_build/pallas_call | solution.py:323
  57.6 0.9 copy-done.8
  58.4 0.3 copy-done.9
  58.7 8.2 %edge_build.1 = (bf16[6,2,512,512]{3,2,1,0:T(8,128)(2,1)}, f32[4,64,512]{2,1,0:T(8,128)S(1)}) custom-call(f32[4096,128]{1,0:T(8,128)} %own_hbm.1, f32[1536,128]{1,0:T(8,128)} %copy-done.8, f32[1536,128]{1,0:T(8,128)} %copy-done.9, f32[8,5]{1,0:T(8,128)S(1)} %compare_convert_fusion.mask_ref, s32[6,5]{1,0:T(8,128)S(1)} %copy-done.6), custom_call_target="tpu_custom_call" | custom-call | tf_op jit(solution)/shard_map/edge_build/pallas_call | solution.py:451
  66.9 0.9 tree_stage.8
  67.9 5.2 %downward.2 = (f32[64,4096]{1,0:T(8,128)S(1)}, f32[64,1024]{1,0:T(8,128)S(1)}, f32[64,1024]{1,0:T(8,128)S(1)}, f32[32,256]{1,0:T(8,128)S(1)}) custom-call(s32[1]{0:T(128)} %bitcast.dev_ref.refs_0_, f32[64,4096]{1,0:T(8,128)S(1)} %copy-done.4, f32[8,64,512]{2,1,0:T(8,128)S(1)} %get-tuple-element.91.refs_2_, f32[4,64,512]{2,1,0:T(8,128)S(1)} %get-tuple-element.96.refs_3_, ...), custom_call_target="tpu_custom_call" | custom-call | tf_op jit(solution)/shard_map/downward/pallas_call | solution.py:694
  73.1 2.2 %upward.1 = (f32[96,256]{1,0:T(8,128)S(1)}, f32[14,64,256]{2,1,0:T(8,128)S(1)}) custom-call(s32[1]{0:T(128)} %bitcast.dev_ref.refs_0_, f32[64,4096]{1,0:T(8,128)S(1)} %get-tuple-element.134.vector_ref.refs_1_.image_ref.refs_3_, f32[32,256]{1,0:T(8,128)S(1)} %get-tuple-element.112.gram_ref, f32[8,512,256]{2,1,0:T(8,128)S(1)} %copy-done.1, ...), custom_call_target="tpu_custom_call" | custom-call | tf_op jit(solution)/shard_map/upward/pallas_call | solution.py:257
  75.3 2.2 %collective-permute-start.10 = (f32[96,256]{1,0:T(8,128)S(1)}, f32[96,256]{1,0:T(8,128)S(1)}, u32[]{:S(2)}, u32[]{:S(2)}) collective-permute-start(f32[96,256]{1,0:T(8,128)S(1)} %get-tuple-element.116.refs_1_), channel_id=1, source_target_pairs={{0,2},{1,3},{2,0},{3,1},{4,6},{5,7},{6,4},{7,5},{8,10},{9,11},{10,... | collective-permute-start | bytes 294920 | tf_op jit(solution)/shard_map/ppermute | solution.py:859
  77.5 0.2 collective-permute-start.9
  77.7 2.2 %collective-permute-start.16 = (f32[64,1024]{1,0:T(8,128)S(1)}, f32[64,1024]{1,0:T(8,128)S(1)}, u32[]{:S(2)}, u32[]{:S(2)}) collective-permute-start(f32[64,1024]{1,0:T(8,128)S(1)} %get-tuple-element.131), channel_id=1, source_target_pairs={{0,1},{1,2},{2,3},{3,4},{4,5},{5,6},{6,7},{7,8},{8,9},{9,10},{10,1... | collective-permute-start | bytes 786440 | tf_op jit(solution)/shard_map/ppermute | solution.py:853
  79.9 1.3 collective-permute-start.17
  81.2 7.5 %near_apply.3.refs_0_ = f32[8,64,512]{2,1,0:T(8,128)S(1)} custom-call(bf16[3,3,2,512,512]{4,3,2,1,0:T(8,128)(2,1)} %get-tuple-element.114.tile_hbm, f32[64,4096]{1,0:T(8,128)S(1)} %get-tuple-element.134.vector_ref.refs_1_.image_ref.refs_3_, f32[8,5]{1,0:T(8,128)S(1)} %compare_convert_fusion.mask_ref), custom_call_target="tpu_custom_call" | custom-call | tf_op jit(solution)/shard_map/near_apply/pallas_call | solution.py:372
  88.8 0.6 tree_stage.9
  89.4 5.3 %collective-permute-start.12 = (f32[96,256]{1,0:T(8,128)S(1)}, f32[96,256]{1,0:T(8,128)S(1)}, u32[]{:S(2)}, u32[]{:S(2)}) collective-permute-start(f32[96,256]{1,0:T(8,128)S(1)} %get-tuple-element.123.refs_1_), channel_id=1, source_target_pairs={{0,4},{1,5},{2,6},{3,7},{4,0},{5,1},{6,2},{7,3},{8,12},{9,13},{10,... | collective-permute-start | bytes 294920 | tf_op jit(solution)/shard_map/ppermute | solution.py:859
  94.6 1.6 %collective-permute-start.13 = (f32[96,256]{1,0:T(8,128)S(1)}, f32[96,256]{1,0:T(8,128)S(1)}, u32[]{:S(2)}, u32[]{:S(2)}) collective-permute-start(f32[96,256]{1,0:T(8,128)S(1)} %get-tuple-element.123.refs_1_), channel_id=1, source_target_pairs={{0,8},{1,9},{2,10},{3,11},{4,12},{5,13},{6,14},{7,15},{8,0},{9,1},... | collective-permute-start | bytes 294920 | tf_op jit(solution)/shard_map/ppermute | solution.py:859
  96.3 5.7 %near_apply.4.refs_0_ = f32[8,64,512]{2,1,0:T(8,128)S(1)} custom-call(bf16[2,3,2,512,512]{4,3,2,1,0:T(8,128)(2,1)} %get-tuple-element.121.tile_hbm, f32[64,4096]{1,0:T(8,128)S(1)} %get-tuple-element.134.vector_ref.refs_1_.image_ref.refs_3_, f32[8,5]{1,0:T(8,128)S(1)} %compare_convert_fusion.mask_ref, f32[8,64,512]{2,1,0:T(8,128)S(1)} %near_apply.3.refs_0_), custom_call_target="tpu_custom_call" | custom-call | tf_op jit(solution)/shard_map/near_apply/pallas_call | solution.py:372
  102.0 0.6 tree_stage.10
  102.6 1.2 collective-permute-start.15
  103.8 5.7 %near_apply.5.refs_2_ = f32[8,64,512]{2,1,0:T(8,128)S(1)} custom-call(bf16[2,3,2,512,512]{4,3,2,1,0:T(8,128)(2,1)} %get-tuple-element.133.tile_hbm, f32[64,4096]{1,0:T(8,128)S(1)} %get-tuple-element.134.vector_ref.refs_1_.image_ref.refs_3_, f32[8,5]{1,0:T(8,128)S(1)} %compare_convert_fusion.mask_ref, f32[8,64,512]{2,1,0:T(8,128)S(1)} %near_apply.4.refs_0_), custom_call_target="tpu_custom_call" | custom-call | tf_op jit(solution)/shard_map/near_apply/pallas_call | solution.py:372
  109.5 4.5 %edge_apply.1.refs_3_ = f32[4,64,512]{2,1,0:T(8,128)S(1)} custom-call(bf16[6,2,512,512]{3,2,1,0:T(8,128)(2,1)} %get-tuple-element.128.tile_hbm, f32[64,1024]{1,0:T(8,128)S(1)} %collective-permute-done.16.lv_ref, f32[64,1024]{1,0:T(8,128)S(1)} %collective-permute-done.17.rv_ref, f32[8,5]{1,0:T(8,128)S(1)} %compare_convert_fusion.mask_ref, s32[6,5]{1,0:T(8,128)S(1)} %copy-done.6), custom_call_target="tpu_custom_call" | custom-call | tf_op jit(solution)/shard_map/edge_apply/pallas_call | solution.py:497
  114.0 3.9 %downward.3.second_ref = f32[64,4096]{1,0:T(8,128)S(1)} custom-call(s32[1]{0:T(128)} %bitcast.dev_ref.refs_0_, f32[64,4096]{1,0:T(8,128)S(1)} %get-tuple-element.134.vector_ref.refs_1_.image_ref.refs_3_, f32[8,64,512]{2,1,0:T(8,128)S(1)} %near_apply.5.refs_2_, f32[4,64,512]{2,1,0:T(8,128)S(1)} %edge_apply.1.refs_3_, f32[8,512,256]{2,1,0:T(8,128)S(1)} %copy-done.1, ...), custom_call_target="tpu_custom_call" | custom-call | tf_op jit(solution)/shard_map/downward/pallas_call | solution.py:694
  117.9 5.3 %first_step.1 = (f32[64,4096]{1,0:T(8,128)S(1)}, f32[64,4096]{1,0:T(8,128)S(1)}, f32[64,256]{1,0:T(8,128)S(1)}, f32[128,128]{1,0:T(8,128)S(1)}) custom-call(f32[96,256]{1,0:T(8,128)S(1)} %get-tuple-element.139.gram_in, f32[64,4096]{1,0:T(8,128)S(1)} %copy-done.4, f32[64,4096]{1,0:T(8,128)S(1)} %get-tuple-element.134.vector_ref.refs_1_.image_ref.refs_3_, ...), custom_call_target="tpu_custom_call" | custom-call | tf_op jit(solution)/shard_map/first_step/pallas_call | solution.py:786
  123.4 1.8 %collective-permute-start.20 = (f32[64,256]{1,0:T(8,128)S(1)}, f32[64,256]{1,0:T(8,128)S(1)}, u32[]{:S(2)}, u32[]{:S(2)}) collective-permute-start(f32[64,256]{1,0:T(8,128)S(1)} %get-tuple-element.145), channel_id=1, source_target_pairs={{0,3},{1,2},{2,1},{3,0},{4,7},{5,6},{6,5},{7,4},{8,11},{9,10},{10,... | collective-permute-start | bytes 196616 | tf_op jit(solution)/shard_map/ppermute | solution.py:859
  125.2 3.2 %collective-permute-done.19 = f32[64,256]{1,0:T(8,128)S(1)} collective-permute-done((f32[64,256]{1,0:T(8,128)S(1)}, f32[64,256]{1,0:T(8,128)S(1)}, u32[]{:S(2)}, u32[]{:S(2)}) %collective-permute-start.19) | collective-permute-done | bytes 65568 | tf_op jit(solution)/shard_map/ppermute | solution.py:859
  128.3 0.3 collective-permute-done.20
  128.7 0.8 collective-permute-start.21
  129.5 1.9 %collective-permute-start.22 = (f32[64,256]{1,0:T(8,128)S(1)}, f32[64,256]{1,0:T(8,128)S(1)}, u32[]{:S(2)}, u32[]{:S(2)}) collective-permute-start(f32[64,256]{1,0:T(8,128)S(1)} %add_add_fusion.1), channel_id=1, source_target_pairs={{0,8},{1,9},{2,10},{3,11},{4,12},{5,13},{6,14},{7,15},{8,0},{9,1},... | collective-permute-start | bytes 196616 | tf_op jit(solution)/shard_map/ppermute | solution.py:859
  131.4 0.9 collective-permute-start.23
  132.2 0.9 collective-permute-done.21
  133.1 0.6 collective-permute-done.22
  133.7 2.8 %collective-permute-done.23 = f32[64,256]{1,0:T(8,128)S(1)} collective-permute-done((f32[64,256]{1,0:T(8,128)S(1)}, f32[64,256]{1,0:T(8,128)S(1)}, u32[]{:S(2)}, u32[]{:S(2)}) %collective-permute-start.23) | collective-permute-done | bytes 65568 | tf_op jit(solution)/shard_map/ppermute | solution.py:859
  136.6 2.7 %collective-permute-start.24 = (f32[64,256]{1,0:T(8,128)S(1)}, f32[64,256]{1,0:T(8,128)S(1)}, u32[]{:S(2)}, u32[]{:S(2)}) collective-permute-start(f32[64,256]{1,0:T(8,128)S(1)} %add_add_fusion.refs_0_), channel_id=1, source_target_pairs={{0,16},{1,17},{2,18},{3,19},{4,20},{5,21},{6,22},{7,23},{8,24},{9,... | collective-permute-start | bytes 196616 | tf_op jit(solution)/shard_map/ppermute | solution.py:859
  139.2 3.2 %collective-permute-done.24.refs_1_ = f32[64,256]{1,0:T(8,128)S(1)} collective-permute-done((f32[64,256]{1,0:T(8,128)S(1)}, f32[64,256]{1,0:T(8,128)S(1)}, u32[]{:S(2)}, u32[]{:S(2)}) %collective-permute-start.24) | collective-permute-done | bytes 65568 | tf_op jit(solution)/shard_map/ppermute | solution.py:859
  142.4 5.9 %last_step.1 = (f32[64,4096]{1,0:T(8,128)}, f32[64,4096]{1,0:T(8,128)}) custom-call(f32[128,128]{1,0:T(8,128)S(1)} %get-tuple-element.144.small_ref, f32[64,256]{1,0:T(8,128)S(1)} %add_add_fusion.refs_0_, f32[64,256]{1,0:T(8,128)S(1)} %collective-permute-done.24.refs_1_, f32[64,4096]{1,0:T(8,128)S(1)} %copy-done.4, ...), custom_call_target="tpu_custom_call" | custom-call | tf_op jit(solution)/shard_map/last_step/pallas_call | solution.py:832
  (49 shorter events, 0.6 us)
Async XLA Ops:
  0.6 18.1 %copy-start.2 = (f32[4096,128]{1,0:T(8,128)S(1)}, f32[4096,128]{1,0:T(8,128)}, u32[]{:S(2)}) copy-start(f32[4096,128]{1,0:T(8,128)} %own_hbm.1) | copy-start | bytes 6291460
  0.6 18.1 %copy-start.4 = (f32[64,4096]{1,0:T(8,128)S(1)}, f32[64,4096]{1,0:T(8,128)}, u32[]{:S(2)}) copy-start(f32[64,4096]{1,0:T(8,128)} %refs_2_.1) | copy-start | bytes 3145732
  0.7 0.8 copy-start.7
  1.5 17.2 %copy-start.10 = (s32[8,5]{1,0:T(8,128)S(1)}, s32[8,5]{1,0:T(8,128)}, u32[]{:S(2)}) copy-start(s32[8,5]{1,0:T(8,128)} %param.12) | copy-start | bytes 484
  1.5 26.7 %copy-start = (f32[7,2,256,256]{3,2,1,0:T(8,128)S(1)}, f32[7,2,256,256]{3,2,1,0:T(8,128)}, u32[]{:S(2)}) copy-start(f32[7,2,256,256]{3,2,1,0:T(8,128)} %refs_5_.13) | copy-start | bytes 11010052
  11.9 16.5 %copy-start.3 = (f32[510,256]{1,0:T(8,128)S(1)}, f32[510,256]{1,0:T(8,128)}, u32[]{:S(2)}) copy-start(f32[510,256]{1,0:T(8,128)} %refs_9_.3) | copy-start | bytes 1566724
  11.9 16.5 %copy-start.5 = (s32[254,256]{1,0:T(8,128)S(1)}, s32[254,256]{1,0:T(8,128)}, u32[]{:S(2)}) copy-start(s32[254,256]{1,0:T(8,128)} %refs_5_.9) | copy-start | bytes 780292
  12.0 16.4 %collective-permute-start = (f32[192,256]{1,0:T(8,128)S(1)}, f32[192,256]{1,0:T(8,128)S(1)}, u32[]{:S(2)}, u32[]{:S(2)}) collective-permute-start(f32[192,256]{1,0:T(8,128)S(1)} %get-tuple-element.78.refs_1_), channel_id=1, source_target_pairs={{0,1},{1,0},{2,3},{3,2},{4,5},{5,4},{6,7},{7,6},{8,9},{9,8},{10,11... | collective-permute-start | bytes 589832 | tf_op jit(solution)/shard_map/ppermute | solution.py:859
  12.5 15.9 %collective-permute-start.1 = (f32[192,256]{1,0:T(8,128)S(1)}, f32[192,256]{1,0:T(8,128)S(1)}, u32[]{:S(2)}, u32[]{:S(2)}) collective-permute-start(f32[192,256]{1,0:T(8,128)S(1)} %get-tuple-element.78.refs_1_), channel_id=1, source_target_pairs={{0,2},{1,3},{2,0},{3,1},{4,6},{5,7},{6,4},{7,5},{8,10},{9,11},{10,... | collective-permute-start | bytes 589832 | tf_op jit(solution)/shard_map/ppermute | solution.py:859
  15.1 13.3 %collective-permute-start.2 = (f32[192,256]{1,0:T(8,128)S(1)}, f32[192,256]{1,0:T(8,128)S(1)}, u32[]{:S(2)}, u32[]{:S(2)}) collective-permute-start(f32[192,256]{1,0:T(8,128)S(1)} %get-tuple-element.78.refs_1_), channel_id=1, source_target_pairs={{0,3},{1,2},{2,1},{3,0},{4,7},{5,6},{6,5},{7,4},{8,11},{9,10},{10,... | collective-permute-start | bytes 589832 | tf_op jit(solution)/shard_map/ppermute | solution.py:859
  15.1 42.4 %collective-permute-start.6 = (f32[1536,128]{1,0:T(8,128)S(1)}, f32[1536,128]{1,0:T(8,128)S(1)}, u32[]{:S(2)}, u32[]{:S(2)}) collective-permute-start(f32[1536,128]{1,0:T(8,128)S(1)} %get-tuple-element.92), channel_id=1, source_target_pairs={{0,1},{1,2},{2,3},{3,4},{4,5},{5,6},{6,7},{7,8},{8,9},{9,10},{10,1... | collective-permute-start | bytes 2359304 | tf_op jit(solution)/shard_map/ppermute | solution.py:853
  17.2 40.3 %collective-permute-start.7 = (f32[1536,128]{1,0:T(8,128)S(1)}, f32[1536,128]{1,0:T(8,128)S(1)}, u32[]{:S(2)}, u32[]{:S(2)}) collective-permute-start(f32[1536,128]{1,0:T(8,128)S(1)} %get-tuple-element.93), channel_id=1, source_target_pairs={{1,0},{2,1},{3,2},{4,3},{5,4},{6,5},{7,6},{8,7},{9,8},{10,9},{11,1... | collective-permute-start | bytes 2359304 | tf_op jit(solution)/shard_map/ppermute | solution.py:854
  29.5 29.1 %copy-start.6 = (s32[6,5]{1,0:T(8,128)S(1)}, s32[6,5]{1,0:T(8,128)}, u32[]{:S(2)}) copy-start(s32[6,5]{1,0:T(8,128)} %constant.8.clone.border_ref) | copy-start | bytes 364
  29.5 14.6 %collective-permute-start.3 = (f32[192,256]{1,0:T(8,128)S(1)}, f32[192,256]{1,0:T(8,128)S(1)}, u32[]{:S(2)}, u32[]{:S(2)}) collective-permute-start(f32[192,256]{1,0:T(8,128)S(1)} %get-tuple-element.85.refs_1_), channel_id=1, source_target_pairs={{0,4},{1,5},{2,6},{3,7},{4,0},{5,1},{6,2},{7,3},{8,12},{9,13},{10,... | collective-permute-start | bytes 589832 | tf_op jit(solution)/shard_map/ppermute | solution.py:859
  34.4 9.7 %collective-permute-start.4 = (f32[192,256]{1,0:T(8,128)S(1)}, f32[192,256]{1,0:T(8,128)S(1)}, u32[]{:S(2)}, u32[]{:S(2)}) collective-permute-start(f32[192,256]{1,0:T(8,128)S(1)} %get-tuple-element.85.refs_1_), channel_id=1, source_target_pairs={{0,8},{1,9},{2,10},{3,11},{4,12},{5,13},{6,14},{7,15},{8,0},{9,1},... | collective-permute-start | bytes 589832 | tf_op jit(solution)/shard_map/ppermute | solution.py:859
  37.2 9.5 %collective-permute-start.5 = (f32[192,256]{1,0:T(8,128)S(1)}, f32[192,256]{1,0:T(8,128)S(1)}, u32[]{:S(2)}, u32[]{:S(2)}) collective-permute-start(f32[192,256]{1,0:T(8,128)S(1)} %get-tuple-element.85.refs_1_), channel_id=1, source_target_pairs={{0,12},{1,13},{2,14},{3,15},{4,8},{5,9},{6,10},{7,11},{8,4},{9,5},... | collective-permute-start | bytes 589832 | tf_op jit(solution)/shard_map/ppermute | solution.py:859
  46.7 21.2 %copy-start.1 = (f32[8,512,256]{2,1,0:T(8,128)S(1)}, f32[8,512,256]{2,1,0:T(8,128)}, u32[]{:S(2)}) copy-start(f32[8,512,256]{2,1,0:T(8,128)} %refs_4_.3) | copy-start | bytes 12582916
  47.8 19.1 %collective-permute-start.8 = (f32[192,256]{1,0:T(8,128)S(1)}, f32[192,256]{1,0:T(8,128)S(1)}, u32[]{:S(2)}, u32[]{:S(2)}) collective-permute-start(f32[192,256]{1,0:T(8,128)S(1)} %get-tuple-element.102.refs_1_), channel_id=1, source_target_pairs={{0,16},{1,17},{2,18},{3,19},{4,20},{5,21},{6,22},{7,23},{8,24},{9,... | collective-permute-start | bytes 589832 | tf_op jit(solution)/shard_map/ppermute | solution.py:859
  57.5 0.9 copy-start.8
  57.5 1.1 copy-start.9
  75.3 13.5 %collective-permute-start.10 = (f32[96,256]{1,0:T(8,128)S(1)}, f32[96,256]{1,0:T(8,128)S(1)}, u32[]{:S(2)}, u32[]{:S(2)}) collective-permute-start(f32[96,256]{1,0:T(8,128)S(1)} %get-tuple-element.116.refs_1_), channel_id=1, source_target_pairs={{0,2},{1,3},{2,0},{3,1},{4,6},{5,7},{6,4},{7,5},{8,10},{9,11},{10,... | collective-permute-start | bytes 294920 | tf_op jit(solution)/shard_map/ppermute | solution.py:859
  77.5 11.3 %collective-permute-start.11 = (f32[96,256]{1,0:T(8,128)S(1)}, f32[96,256]{1,0:T(8,128)S(1)}, u32[]{:S(2)}, u32[]{:S(2)}) collective-permute-start(f32[96,256]{1,0:T(8,128)S(1)} %get-tuple-element.116.refs_1_), channel_id=1, source_target_pairs={{0,3},{1,2},{2,1},{3,0},{4,7},{5,6},{6,5},{7,4},{8,11},{9,10},{10,... | collective-permute-start | bytes 294920 | tf_op jit(solution)/shard_map/ppermute | solution.py:859
  77.5 11.3 %collective-permute-start.9 = (f32[96,256]{1,0:T(8,128)S(1)}, f32[96,256]{1,0:T(8,128)S(1)}, u32[]{:S(2)}, u32[]{:S(2)}) collective-permute-start(f32[96,256]{1,0:T(8,128)S(1)} %get-tuple-element.116.refs_1_), channel_id=1, source_target_pairs={{0,1},{1,0},{2,3},{3,2},{4,5},{5,4},{6,7},{7,6},{8,9},{9,8},{10,11... | collective-permute-start | bytes 294920 | tf_op jit(solution)/shard_map/ppermute | solution.py:859
  77.7 31.8 %collective-permute-start.16 = (f32[64,1024]{1,0:T(8,128)S(1)}, f32[64,1024]{1,0:T(8,128)S(1)}, u32[]{:S(2)}, u32[]{:S(2)}) collective-permute-start(f32[64,1024]{1,0:T(8,128)S(1)} %get-tuple-element.131), channel_id=1, source_target_pairs={{0,1},{1,2},{2,3},{3,4},{4,5},{5,6},{6,7},{7,8},{8,9},{9,10},{10,1... | collective-permute-start | bytes 786440 | tf_op jit(solution)/shard_map/ppermute | solution.py:853
  79.9 29.6 %collective-permute-start.17 = (f32[64,1024]{1,0:T(8,128)S(1)}, f32[64,1024]{1,0:T(8,128)S(1)}, u32[]{:S(2)}, u32[]{:S(2)}) collective-permute-start(f32[64,1024]{1,0:T(8,128)S(1)} %get-tuple-element.132), channel_id=1, source_target_pairs={{1,0},{2,1},{3,2},{4,3},{5,4},{6,5},{7,6},{8,7},{9,8},{10,9},{11,1... | collective-permute-start | bytes 786440 | tf_op jit(solution)/shard_map/ppermute | solution.py:854
  89.4 12.6 %collective-permute-start.12 = (f32[96,256]{1,0:T(8,128)S(1)}, f32[96,256]{1,0:T(8,128)S(1)}, u32[]{:S(2)}, u32[]{:S(2)}) collective-permute-start(f32[96,256]{1,0:T(8,128)S(1)} %get-tuple-element.123.refs_1_), channel_id=1, source_target_pairs={{0,4},{1,5},{2,6},{3,7},{4,0},{5,1},{6,2},{7,3},{8,12},{9,13},{10,... | collective-permute-start | bytes 294920 | tf_op jit(solution)/shard_map/ppermute | solution.py:859
  94.6 7.4 %collective-permute-start.13 = (f32[96,256]{1,0:T(8,128)S(1)}, f32[96,256]{1,0:T(8,128)S(1)}, u32[]{:S(2)}, u32[]{:S(2)}) collective-permute-start(f32[96,256]{1,0:T(8,128)S(1)} %get-tuple-element.123.refs_1_), channel_id=1, source_target_pairs={{0,8},{1,9},{2,10},{3,11},{4,12},{5,13},{6,14},{7,15},{8,0},{9,1},... | collective-permute-start | bytes 294920 | tf_op jit(solution)/shard_map/ppermute | solution.py:859
  96.2 5.8 %collective-permute-start.14 = (f32[96,256]{1,0:T(8,128)S(1)}, f32[96,256]{1,0:T(8,128)S(1)}, u32[]{:S(2)}, u32[]{:S(2)}) collective-permute-start(f32[96,256]{1,0:T(8,128)S(1)} %get-tuple-element.123.refs_1_), channel_id=1, source_target_pairs={{0,12},{1,13},{2,14},{3,15},{4,8},{5,9},{6,10},{7,11},{8,4},{9,5},... | collective-permute-start | bytes 294920 | tf_op jit(solution)/shard_map/ppermute | solution.py:859
  102.6 11.4 %collective-permute-start.15 = (f32[96,256]{1,0:T(8,128)S(1)}, f32[96,256]{1,0:T(8,128)S(1)}, u32[]{:S(2)}, u32[]{:S(2)}) collective-permute-start(f32[96,256]{1,0:T(8,128)S(1)} %get-tuple-element.137.refs_1_), channel_id=1, source_target_pairs={{0,16},{1,17},{2,18},{3,19},{4,20},{5,21},{6,22},{7,23},{8,24},{9,... | collective-permute-start | bytes 294920 | tf_op jit(solution)/shard_map/ppermute | solution.py:859
  123.2 1.9 %collective-permute-start.18 = (f32[64,256]{1,0:T(8,128)S(1)}, f32[64,256]{1,0:T(8,128)S(1)}, u32[]{:S(2)}, u32[]{:S(2)}) collective-permute-start(f32[64,256]{1,0:T(8,128)S(1)} %get-tuple-element.145), channel_id=1, source_target_pairs={{0,1},{1,0},{2,3},{3,2},{4,5},{5,4},{6,7},{7,6},{8,9},{9,8},{10,11... | collective-permute-start | bytes 196616 | tf_op jit(solution)/shard_map/ppermute | solution.py:859
  123.3 5.0 %collective-permute-start.19 = (f32[64,256]{1,0:T(8,128)S(1)}, f32[64,256]{1,0:T(8,128)S(1)}, u32[]{:S(2)}, u32[]{:S(2)}) collective-permute-start(f32[64,256]{1,0:T(8,128)S(1)} %get-tuple-element.145), channel_id=1, source_target_pairs={{0,2},{1,3},{2,0},{3,1},{4,6},{5,7},{6,4},{7,5},{8,10},{9,11},{10,... | collective-permute-start | bytes 196616 | tf_op jit(solution)/shard_map/ppermute | solution.py:859
  123.4 5.3 %collective-permute-start.20 = (f32[64,256]{1,0:T(8,128)S(1)}, f32[64,256]{1,0:T(8,128)S(1)}, u32[]{:S(2)}, u32[]{:S(2)}) collective-permute-start(f32[64,256]{1,0:T(8,128)S(1)} %get-tuple-element.145), channel_id=1, source_target_pairs={{0,3},{1,2},{2,1},{3,0},{4,7},{5,6},{6,5},{7,4},{8,11},{9,10},{10,... | collective-permute-start | bytes 196616 | tf_op jit(solution)/shard_map/ppermute | solution.py:859
  128.7 4.4 %collective-permute-start.21 = (f32[64,256]{1,0:T(8,128)S(1)}, f32[64,256]{1,0:T(8,128)S(1)}, u32[]{:S(2)}, u32[]{:S(2)}) collective-permute-start(f32[64,256]{1,0:T(8,128)S(1)} %add_add_fusion.1), channel_id=1, source_target_pairs={{0,4},{1,5},{2,6},{3,7},{4,0},{5,1},{6,2},{7,3},{8,12},{9,13},{10,... | collective-permute-start | bytes 196616 | tf_op jit(solution)/shard_map/ppermute | solution.py:859
  129.5 4.3 %collective-permute-start.22 = (f32[64,256]{1,0:T(8,128)S(1)}, f32[64,256]{1,0:T(8,128)S(1)}, u32[]{:S(2)}, u32[]{:S(2)}) collective-permute-start(f32[64,256]{1,0:T(8,128)S(1)} %add_add_fusion.1), channel_id=1, source_target_pairs={{0,8},{1,9},{2,10},{3,11},{4,12},{5,13},{6,14},{7,15},{8,0},{9,1},... | collective-permute-start | bytes 196616 | tf_op jit(solution)/shard_map/ppermute | solution.py:859
  131.4 5.2 %collective-permute-start.23 = (f32[64,256]{1,0:T(8,128)S(1)}, f32[64,256]{1,0:T(8,128)S(1)}, u32[]{:S(2)}, u32[]{:S(2)}) collective-permute-start(f32[64,256]{1,0:T(8,128)S(1)} %add_add_fusion.1), channel_id=1, source_target_pairs={{0,12},{1,13},{2,14},{3,15},{4,8},{5,9},{6,10},{7,11},{8,4},{9,5},... | collective-permute-start | bytes 196616 | tf_op jit(solution)/shard_map/ppermute | solution.py:859
  136.6 5.9 %collective-permute-start.24 = (f32[64,256]{1,0:T(8,128)S(1)}, f32[64,256]{1,0:T(8,128)S(1)}, u32[]{:S(2)}, u32[]{:S(2)}) collective-permute-start(f32[64,256]{1,0:T(8,128)S(1)} %add_add_fusion.refs_0_), channel_id=1, source_target_pairs={{0,16},{1,17},{2,18},{3,19},{4,20},{5,21},{6,22},{7,23},{8,24},{9,... | collective-permute-start | bytes 196616 | tf_op jit(solution)/shard_map/ppermute | solution.py:859

commit v3 on v2

--- a/solution.py
+++ b/solution.py
@@ -124,31 +124,27 @@
     return level[0]
 
 
-def leaf_weights(vector_ref, interp_ref, leaf_count, leaf_size, loads):
+def leaf_weights(vector_ref, interp_ref, leaf_count, leaf_size):
     found = []
     for j in range(leaf_count):
-        if loads is not None:
-            loads[j].wait()
         found.append(times(stacked(vector_ref[:, j * leaf_size : (j + 1) * leaf_size]), *split(interp_ref[j])))
     return found
 
 
-def front(device, points, vector, leaf_skeleton, node_skeleton, leaf_interp, transfer, node_gain, leaves, reach):
+def front(device, points, vector, leaf_skeleton, node_skeleton, leaf_count, leaves, reach):
     dim = points.shape[1]
-    leaf_count, leaf_size, skel_size = leaf_interp.shape
+    leaf_size, skel_size = points.shape[0] // leaf_count, leaf_skeleton.shape[1]
     classes = vector.shape[0]
     pair_count = leaf_count - 1
     width = reach * leaf_size
     local_levels = leaf_count.bit_length() - 1
 
     def body(
-        dev_ref, points_hbm, vector_hbm, leaf_ref, node_hbm, interp_hbm, transfer_hbm, gain_hbm,
-        pack_ref, local_ref, hi_ref, lo_ref, head_ref, tail_ref,
-        rows_ref, points_ref, vector_ref, interp_ref, transfer_ref, points_sem, vector_sem, interp_sem, transfer_sem,
-        node_ref, gain_ref, node_sem, gain_sem,
+        dev_ref, points_hbm, vector_hbm, leaf_ref, node_hbm,
+        pack_ref, hi_ref, lo_ref, head_ref, tail_ref,
+        rows_ref, points_ref, ends_ref, node_ref, points_sem, ends_sem, node_sem,
     ):
         load_nodes = pltpu.make_async_copy(node_hbm, node_ref, node_sem)
-        load_gains = pltpu.make_async_copy(gain_hbm, gain_ref, gain_sem)
         loads = [
             pltpu.make_async_copy(
                 points_hbm.at[pl.ds(j * leaf_size, leaf_size)], points_ref.at[pl.ds(j * leaf_size, leaf_size)],
@@ -156,16 +152,16 @@
             )
             for j in range(leaf_count)
         ]
-        load_vector = pltpu.make_async_copy(vector_hbm, vector_ref, vector_sem)
-        load_maps = pltpu.make_async_copy(transfer_hbm.at[pl.ds(0, local_levels)], transfer_ref, transfer_sem)
-        interp_loads = [
-            pltpu.make_async_copy(interp_hbm.at[j], interp_ref.at[j], interp_sem.at[j]) for j in range(leaf_count)
+        starts = (0, (leaf_count - reach) * leaf_size)
+        end_loads = [
+            pltpu.make_async_copy(vector_hbm.at[:, pl.ds(starts[i], width)], ends_ref.at[i], ends_sem.at[i])
+            for i in range(2)
         ]
-        for copy in [*loads, load_nodes, load_vector, *interp_loads, load_maps, load_gains]:
+        for copy in [load_nodes, *loads, *end_loads]:
             copy.start()
         device = dev_ref[0]
+        rows_ref[...] = jnp.zeros_like(rows_ref)
         load_nodes.wait()
-        rows_ref[...] = jnp.zeros_like(rows_ref)
         pair = 0
         for depth in range(1, local_levels + 1):
             count = leaf_count >> depth
@@ -179,6 +175,11 @@
             loads[j].wait()
             cat = scaled_cat(points_ref[j * leaf_size : (j + 1) * leaf_size, :])
             level.append(nn(one_hot(leaf_columns[:, j : j + 1], leaf_size), cat).astype(BF16))
+        for i, ref in enumerate((head_ref, tail_ref)):
+            end_loads[i].wait()
+            ref[:width, :] = points_ref[starts[i] : starts[i] + width, :]
+            for n in range(width // 128):
+                ref[width + n * classes : width + (n + 1) * classes, :] = ends_ref[i, :, n * 128 : (n + 1) * 128]
         pair = 0
         while len(level) > 1:
             above = []
@@ -192,54 +193,31 @@
                 pair += 1
             level = above
         whole = level[0]
-        pack_skel(pack_ref, classes, whole[:, :dim].astype(F32) + whole[:, dim:].astype(F32))
-        load_vector.wait()
-        for ref, start in ((head_ref, 0), (tail_ref, (leaf_count - reach) * leaf_size)):
-            ref[:width, :] = points_ref[start : start + width, :]
-            for i in range(width // 128):
-                ref[width + i * classes : width + (i + 1) * classes, :] = vector_ref[
-                    :, start + i * 128 : start + (i + 1) * 128
-                ]
-        weights = leaf_weights(vector_ref, interp_ref, leaf_count, leaf_size, interp_loads)
-        load_maps.wait()
-        load_gains.wait()
-        pack_ref[:classes] = climb_local(
-            device, weights, leaf_count, leaves, transfer_ref, gain_ref, local_ref
-        )
+        pack_skel(pack_ref, 0, whole[:, :dim].astype(F32) + whole[:, dim:].astype(F32))
 
     return call(
         body,
         (
-            struct((classes + skel_size // 2, skel_size)),
-            struct((2 * leaf_count - 2, classes, skel_size)),
+            struct((skel_size // 2, skel_size)),
             struct((pair_count, skel_size, skel_size), BF16),
             struct((pair_count, skel_size, skel_size), BF16),
             struct((width + width // 128 * classes, 128)),
             struct((width + width // 128 * classes, 128)),
         ),
         "front",
-        28,
-        in_specs=[SM, HBM, HBM, VM, HBM, HBM, HBM, HBM],
-        out_specs=(VM,) * 6,
+        20,
+        in_specs=[SM, HBM, HBM, VM, HBM],
+        out_specs=(VM,) * 5,
         scratch_shapes=[
             pltpu.VMEM((leaf_count, skel_size), jnp.int32),
             pltpu.VMEM(points.shape, F32),
-            pltpu.VMEM(vector.shape, F32),
-            pltpu.VMEM(leaf_interp.shape, F32),
-            pltpu.VMEM((local_levels,) + transfer.shape[1:], F32),
+            pltpu.VMEM((2, classes, width), F32),
+            pltpu.VMEM(node_skeleton.shape, jnp.int32),
             pltpu.SemaphoreType.DMA((leaf_count,)),
-            pltpu.SemaphoreType.DMA,
-            pltpu.SemaphoreType.DMA((leaf_count,)),
-            pltpu.SemaphoreType.DMA,
-            pltpu.VMEM(node_skeleton.shape, jnp.int32),
-            pltpu.VMEM(node_gain.shape, F32),
-            pltpu.SemaphoreType.DMA,
+            pltpu.SemaphoreType.DMA((2,)),
             pltpu.SemaphoreType.DMA,
         ],
-    )(
-        device, in_hbm(points), in_hbm(vector), leaf_skeleton, in_hbm(node_skeleton), in_hbm(leaf_interp),
-        in_hbm(transfer), in_hbm(node_gain),
-    )
+    )(device, in_hbm(points), in_hbm(vector), leaf_skeleton, in_hbm(node_skeleton))
 
 
 def upward(device, vector, gram, leaf_interp, transfer, node_gain, leaves):
@@ -248,7 +226,7 @@
     local_levels = leaf_count.bit_length() - 1
 
     def body(dev_ref, vector_ref, gram_ref, interp_ref, transfer_ref, gain_ref, pack_ref, local_ref):
-        weights = leaf_weights(vector_ref, interp_ref, leaf_count, leaf_size, None)
+        weights = leaf_weights(vector_ref, interp_ref, leaf_count, leaf_size)
         pack_ref[:classes] = climb_local(
             dev_ref[0], weights, leaf_count, leaves, transfer_ref, gain_ref, local_ref
         )
@@ -267,7 +245,8 @@
     )(device, vector, gram, leaf_interp, transfer, node_gain)
 
 
-def apply_tile(mask, cat, hi, lo, out_ref, place):
+def apply_tile(neighbour, cat, hi, lo, out_ref, place):
+    mask = jnp.where(neighbour >= 0, 1.0, 0.0)
     out_ref[place] = out_ref[place] + mask * times(cat, hi, lo)
 
 
@@ -280,7 +259,7 @@
 def near_products(pairs, mask_ref, vecs, tile_ref, out_ref, reach):
     added = []
     for e, (a, b, both) in enumerate(pairs):
-        mask = mask_ref[a, reach + b - a]
+        mask = jnp.where(mask_ref[a, reach + b - a] >= 0, 1.0, 0.0)
         hi, lo = tile_ref[0, e, 0], tile_ref[0, e, 1]
         added.append((b, mask * times(vecs[a], hi, lo)))
         if both is not None:
@@ -304,13 +283,16 @@
         @pl.when(pl.program_id(0) == 0)
         def _():
             out_ref[...] = jnp.zeros_like(out_ref) if base_ref is None else base_ref[...]
-            for j in used:
-                cat = scaled_cat(points_ref[j * leaf_size : (j + 1) * leaf_size, :])
+
+            @pl.loop(used[0], used[-1] + 1)
+            def _(j):
+                where = pl.ds(pl.multiple_of(j * leaf_size, leaf_size), leaf_size)
+                cat = scaled_cat(points_ref[where, :])
                 cats[j] = cat
                 wide, row = half_norms(cat)
                 wides[j] = wide
                 rows[j] = jnp.broadcast_to(row, (8, leaf_size))
-                vecs[j] = stacked(vector_ref[:, j * leaf_size : (j + 1) * leaf_size])
+                vecs[j] = stacked(vector_ref[:, where])
 
         pairs = near_pairs(pl.program_id(0) + first, leaf_count)
         for e, (a, b, _) in enumerate(pairs):
@@ -351,8 +333,9 @@
         def loads(t):
             return [pltpu.make_async_copy(tile_hbm.at[t, e], tile_ref.at[t, e], sems.at[t, e]) for e in range(3)]
 
-        for copy in loads(0):
-            copy.start()
+        for t in range(count):
+            for copy in loads(t):
+                copy.start()
         out_ref[...] = jnp.zeros_like(out_ref) if base_ref is None else base_ref[...]
         for j in range(first, min(first + count + 2, leaf_count)):
             vecs[j] = stacked(vector_ref[:, j * leaf_size : (j + 1) * leaf_size])
@@ -361,11 +344,6 @@
         def _(t):
             for copy in loads(t):
                 copy.wait()
-
-            @pl.when(t + 1 < count)
-            def _():
-                for copy in loads(t + 1):
-                    copy.start()
 
             near_products(near_pairs(first + t, leaf_count), mask_ref, vecs, tile_ref.at[pl.ds(t, 1)], out_ref, reach)
 
@@ -404,13 +382,13 @@
     border = edges(leaf_count, reach)
     count = border.shape[0]
 
-    def body(own_hbm, left_hbm, right_hbm, mask_ref, border_ref, tile_hbm, out_ref, tile_ref, halo_ref, own_ref, sems, out_sems):
+    def body(own_hbm, left_ref, right_ref, mask_ref, border_ref, tile_hbm, out_ref, tile_ref, own_ref, sems, out_sems):
+        halo_refs = (left_ref, right_ref)
         tail = pl.ds((leaf_count - reach) * leaf_size, width)
         loads = [
             pltpu.make_async_copy(src, dst, sems.at[i])
             for i, (src, dst) in enumerate(
                 [
-                    (left_hbm, halo_ref.at[0]), (right_hbm, halo_ref.at[1]),
                     (own_hbm.at[pl.ds(0, width)], own_ref.at[0]), (own_hbm.at[tail], own_ref.at[1]),
                 ]
             )
@@ -421,27 +399,29 @@
         for copy in loads:
             copy.wait()
 
-        def cat_of(ref, i, spot):
-            return scaled_cat(ref[i, pl.ds(pl.multiple_of(spot * leaf_size, leaf_size), leaf_size), :])
+        def cat_of(ref, spot):
+            return scaled_cat(ref[pl.ds(pl.multiple_of(spot * leaf_size, leaf_size), leaf_size), :])
 
         def rows_of(i, spot):
             firsts = [pl.multiple_of(width + (spot * lanes + n) * classes, classes) for n in range(lanes)]
-            return jnp.concatenate([halo_ref[i, pl.ds(f, classes), :] for f in firsts], axis=1)
+            return jnp.concatenate([halo_refs[i][pl.ds(f, classes), :] for f in firsts], axis=1)
 
         def store(t):
             return pltpu.make_async_copy(tile_ref.at[t], tile_hbm.at[t], out_sems.at[t])
 
-        @pl.loop(0, count)
-        def _(t):
-            side, h, j, own, slot = [border_ref[t, i] for i in range(5)]
-            cat_h, cat_j = cat_of(halo_ref, side, h), cat_of(own_ref, side, j)
-            tile = pair_tile(cat_h, cat_j, half_norms(cat_h)[0], half_norms(cat_j)[1])
-            tile_ref[t, 0], tile_ref[t, 1] = split(tile)
-            store(t).start()
-            apply_tile(
-                mask_ref[own, slot], stacked(rows_of(side, h)), tile_ref[t, 0], tile_ref[t, 1], out_ref,
-                side * reach + j,
-            )
+        @pl.loop(0, count // 2)
+        def _(step):
+            added = []
+            for side in range(2):
+                t = step + side * (count // 2)
+                h, j, own, slot = [border_ref[t, i] for i in range(1, 5)]
+                cat_h, cat_j = cat_of(halo_refs[side], h), cat_of(own_ref.at[side], j)
+                tile = pair_tile(cat_h, cat_j, half_norms(cat_h)[0], half_norms(cat_j)[1])
+                tile_ref[t, 0], tile_ref[t, 1] = split(tile)
+                added.append((side * reach + j, mask_ref[own, slot], stacked(rows_of(side, h)), t))
+            for place, mask, rows, t in added:
+                apply_tile(mask, rows, tile_ref[t, 0], tile_ref[t, 1], out_ref, place)
+                store(t).start()
 
         @pl.loop(0, count)
         def _(t):
@@ -453,16 +433,15 @@
         (pltpu.HBM(shape, BF16), struct((2 * reach, classes, leaf_size))),
         "edge_build",
         22,
-        in_specs=[HBM, HBM, HBM, SM, SM],
+        in_specs=[HBM, VM, VM, SM, SM],
         out_specs=(HBM, VM),
         scratch_shapes=[
             pltpu.VMEM(shape, BF16),
-            pltpu.VMEM((2,) + left.shape, F32),
             pltpu.VMEM((2, width, dim), F32),
-            pltpu.SemaphoreType.DMA((4,)),
+            pltpu.SemaphoreType.DMA((2,)),
             pltpu.SemaphoreType.DMA((count,)),
         ],
-    )(in_hbm(points), in_hbm(left), in_hbm(right), near_mask, border)
+    )(in_hbm(points), left, right, near_mask, border)
 
 
 def edge_apply(tiles, left_rows, right_rows, near_mask, leaf_count, reach):
@@ -473,26 +452,25 @@
         def load(t):
             return pltpu.make_async_copy(tile_hbm.at[t], tile_ref.at[t], sems.at[t])
 
-        for t in range(min(3, count)):
-            load(t).start()
+        for step in range(count // 2):
+            load(step).start()
+            load(step + count // 2).start()
         out_ref[...] = jnp.zeros_like(out_ref)
         for h in range(reach):
             where = slice(h * leaf_size, (h + 1) * leaf_size)
             vecs[0, h] = stacked(lv_ref[:, where])
             vecs[1, h] = stacked(rv_ref[:, where])
 
-        @pl.loop(0, count)
-        def _(t):
-            side, h, j, own, slot = [border_ref[t, i] for i in range(5)]
-            load(t).wait()
-
-            @pl.when(t + 3 < count)
-            def _():
-                load(t + 3).start()
-
-            apply_tile(
-                mask_ref[own, slot], vecs[side, h], tile_ref[t, 0], tile_ref[t, 1], out_ref, side * reach + j
-            )
+        @pl.loop(0, count // 2)
+        def _(step):
+            load(step).wait()
+            load(step + count // 2).wait()
+            for side in range(2):
+                t = step + side * (count // 2)
+                h, j, own, slot = [border_ref[t, i] for i in range(1, 5)]
+                apply_tile(
+                    mask_ref[own, slot], vecs[side, h], tile_ref[t, 0], tile_ref[t, 1], out_ref, side * reach + j
+                )
 
     return call(
         body,
@@ -751,22 +729,16 @@
 def first_step(gram, right_side, image, second):
     classes = right_side.shape[0]
 
-    def body(gram_in, b_ref, image_ref, second_ref, res_ref, res_image_ref, gram_ref, small_ref):
+    def body(gram_in, b_ref, image_ref, second_ref, res_ref, res_image_ref, gram_ref, alpha_ref, both_ref):
         packed = gram_in[classes:, :]
         both = jnp.concatenate([packed[:, : 2 * classes], packed[:, 2 * classes :]], axis=0)
         turned = both.T
         base = 0.5 * (both[:, :classes] + turned[:classes])
         curvature = 0.5 * (both[:, classes:] + turned[classes:])
-        square = (classes, classes)
-        unit = jnp.where(
-            lax.broadcasted_iota(jnp.int32, square, 0) == lax.broadcasted_iota(jnp.int32, square, 1), 1.0, 0.0
-        )
-        solved, inverse = eliminate(
-            [jnp.concatenate([curvature, base], axis=1), jnp.concatenate([base, unit], axis=1)]
-        )
+        (solved,) = eliminate([jnp.concatenate([curvature, base], axis=1)])
         alpha_t = solved.T[classes:]
-        small_ref[:classes] = jnp.concatenate([alpha_t, inverse[:, classes:]], axis=1)
-        small_ref[classes:] = both
+        alpha_ref[...] = alpha_t
+        both_ref[...] = both
         res = b_ref[...] - mixed(alpha_t, image_ref[...])
         res_image = image_ref[...] - mixed(alpha_t, second_ref[...])
         res_ref[...] = res
@@ -789,26 +761,45 @@
             struct(right_side.shape),
             struct(right_side.shape),
             struct((classes, 4 * classes)),
-            struct((2 * classes, 2 * classes)),
+            struct((classes, classes)),
+            struct((classes, 2 * classes)),
         ),
         "first_step",
         28,
     )(gram, right_side, image, second)
 
 
-def last_step(small, parts, right_side, image, res, res_image):
+def between(both, alpha_t, right_side):
+    classes = right_side.shape[0]
+
+    def body(both_ref, alpha_ref, b_ref, inverse_ref, moved_ref):
+        both = both_ref[...]
+        base = 0.5 * (both[:, :classes] + both.T[:classes])
+        square = (classes, classes)
+        unit = jnp.where(
+            lax.broadcasted_iota(jnp.int32, square, 0) == lax.broadcasted_iota(jnp.int32, square, 1), 1.0, 0.0
+        )
+        (inverse,) = eliminate([jnp.concatenate([base, unit], axis=1)])
+        inverse_ref[...] = inverse[:, classes:]
+        moved_ref[...] = mixed(alpha_ref[...], b_ref[...])
+
+    return call(body, (struct((classes, classes)), struct(right_side.shape)), "between", 16)(
+        both, alpha_t, right_side
+    )
+
+
+def last_step(both, inverse, moved, parts, right_side, image, res, res_image):
     classes = right_side.shape[0]
     count = len(parts)
 
-    def body(small_ref, *refs):
+    def body(both_ref, inverse_ref, moved_ref, *refs):
         base_ref, image_ref, res_ref, res_image_ref, sol_ref, out_ref = refs[count:]
         grams = [ref[...] for ref in refs[:count]]
         while len(grams) > 1:
             grams = [a + b for a, b in zip(grams[0::2], grams[1::2])]
         grams = grams[0]
-        alpha_t = small_ref[:classes, :classes]
-        inverse = small_ref[:classes, classes:]
-        image_gram = small_ref[classes:, classes:]
+        inverse = inverse_ref[...]
+        image_gram = both_ref[:, classes:]
         new_gram = grams[:, :classes]
         new_gram = 0.5 * (new_gram + grams[:, : 2 * classes].T[:classes])
         beta = exact_dot(inverse, new_gram)
@@ -825,12 +816,12 @@
         (solved,) = eliminate([jnp.concatenate([curvature, new_gram], axis=1)])
         alpha2_t = solved.T[classes:]
         direction = res_ref[...] + mixed(beta_t, base_ref[...])
-        moved = res_image_ref[...] + mixed(beta_t, image_ref[...])
-        sol_ref[...] = mixed(alpha_t, base_ref[...]) + mixed(alpha2_t, direction)
-        out_ref[...] = res_ref[...] - mixed(alpha2_t, moved)
+        sol_ref[...] = moved_ref[...] + mixed(alpha2_t, direction)
+        direction_image = res_image_ref[...] + mixed(beta_t, image_ref[...])
+        out_ref[...] = res_ref[...] - mixed(alpha2_t, direction_image)
 
     return call(body, (struct(right_side.shape), struct(right_side.shape)), "last_step", 28)(
-        small, *parts, right_side, image, res, res_image
+        both, inverse, moved, *parts, right_side, image, res, res_image
     )
 
 
@@ -861,7 +852,7 @@
         ]
 
     stages = [(bit, min(2, dev_levels - bit)) for bit in range(0, dev_levels, 2)]
-    near_mask = (neighbours >= 0).astype(F32)
+    near_mask = neighbours
 
     def climb(pack, with_skel, extra, covers):
         siblings, tiles, results = [], [], []
@@ -891,8 +882,8 @@
     steps = leaf_count - 1
     cuts = [0, -(-steps * 3 // 7), -(-steps * 5 // 7), steps]
 
-    pack, weights, *local_tiles, head, tail = front(
-        device, points, right_side, leaf_skeleton, node_skeleton, leaf_interp, transfer, node_gain, leaves, reach
+    own_skel, *local_tiles, head, tail = front(
+        device, points, right_side, leaf_skeleton, node_skeleton, leaf_count, leaves, reach
     )
     left, right = exchange(head, tail)
     near_tiles, total = [], [None]
@@ -900,8 +891,10 @@
     def build(part):
         def run(pack):
             (vector,) = after(pack, right_side)
+            own_points = points if part else in_hbm(points)
+            vector = vector if part else in_hbm(vector)
             tiles, total[0] = near_build(
-                points, vector, near_mask, total[0], cuts[part], cuts[part + 1] - cuts[part], leaf_count, reach
+                own_points, vector, near_mask, total[0], cuts[part], cuts[part + 1] - cuts[part], leaf_count, reach
             )
             near_tiles.append(tiles)
             return total[0],
@@ -909,11 +902,14 @@
         return run
 
     def build_last(pack):
-        build(2)(pack)
         left_pack, right_pack, _ = after(pack, left, right, total[0])
         return edge_build(points, left_pack, right_pack, near_mask, classes, leaf_count, reach)
 
-    siblings, device_tiles, _, results = climb(pack, True, False, [build(0), build(1), build_last])
+    build(0)(own_skel)
+    (vector,) = after(total[0], right_side)
+    local_transfer = lax.slice_in_dim(transfer, 0, local_levels, axis=0)
+    pack, weights = upward(device, vector, own_skel, leaf_interp, local_transfer, node_gain, leaves)
+    siblings, device_tiles, _, results = climb(pack, True, False, [build(1), build(2), build_last])
     near = total[0]
     edge_tiles, edge = results[2]
     image, head, tail, gram = downward(
@@ -921,7 +917,7 @@
         siblings, device_tiles, reach, leaves, True,
     )
 
-    pack, weights = upward(device, image, gram, leaf_interp, transfer, node_gain, leaves)
+    pack, weights = upward(device, image, gram, leaf_interp, local_transfer, node_gain, leaves)
     left_rows, right_rows = exchange(*after(pack, head, tail))
     total = [None]
 
@@ -945,15 +941,18 @@
         siblings, device_tiles, reach, leaves, False,
     )
 
-    res, res_image, grams, small = first_step(pack, right_side, image, second)
-    for bit, width in stages[:-1]:
+    res, res_image, grams, alpha_t, both = first_step(pack, right_side, image, second)
+    inverse, moved = between(both, alpha_t, right_side)
+    for stage, (bit, width) in enumerate(stages[:-1]):
         parts = group(grams, bit, 1 << width)
+        if stage == 0:
+            parts, (inverse, moved) = lax.optimization_barrier((parts, (inverse, moved)))
         while len(parts) > 1:
             parts = [a + b for a, b in zip(parts[0::2], parts[1::2])]
         grams = parts[0]
     bit, width = stages[-1]
     parts = group(grams, bit, 1 << width)
-    return last_step(small, parts, right_side, image, res, res_image)
+    return last_step(both, inverse, moved, parts, right_side, image, res, res_image)
 
 
 def solution(mesh):

time: 149 us -> 147 us (0.987)
  starting transfers between devices: 39.3 us -> 37.5 us
  waiting for transfers between devices: 13.6 us -> 15.2 us
    pallas_call x1 -> x2, Pallas kernels: 2.18 us -> 4.3 us  [upward(): call(body, (struct((classes + gram.shape[0], skel_size)), struct((2 * lea...]
    pallas_call x3, Pallas kernels: 18.9 us -> 16.8 us  [near_apply(): call(body, struct((leaf_count, classes, leaf_size)), 'near_apply', 20, in...]
    pallas_call x3, Pallas kernels: 23.3 us -> 25.4 us  [near_build(): call(body, (pltpu.HBM((count, 3, 2, leaf_size, leaf_size), BF16), struct(...]
    ppermute x21, starting transfers between devices: 32.3 us -> 30.4 us  [group(): lax.ppermute(pack, 'leaf', [(d, d ^ i << first_bit) for d in range(dev_co...]
    ppermute x21, waiting for transfers between devices: 13.6 us -> 15.2 us  [group(): lax.ppermute(pack, 'leaf', [(d, d ^ i << first_bit) for d in range(dev_co...]
    pallas_call x1 -> x2, Pallas kernels: 10.4 us -> 9.11 us  [the longest x1 6.45 us: front(): call(body, (struct((skel_size // 2, skel_size)), struct((pair_count, skel...]
  transfers between devices with their start and end apart: 25 -> 25, of which waited for: 7 -> 9; matrix products, arithmetic and copies ran while one was open for 0% -> 0% of each run, Pallas kernels for 39% -> 42%
where the time goes in v3:
time: 147 us
  Pallas kernels  91.2 us (62%)
  starting transfers between devices  37.5 us (26%)
  waiting for transfers between devices  15.2 us (10%)
  local copies, waits for them, and re-layouts  1.91 us (1%)
    ppermute x21, starting transfers between devices, group(): lax.ppermute(pack, 'leaf', [(d, d ^ i << first_bit) for d in range(dev_co...  30.4 us
    pallas_call x3, Pallas kernels, near_build(): call(body, (pltpu.HBM((count, 3, 2, leaf_size, leaf_size), BF16), struct(...  25.4 us
    pallas_call x3, Pallas kernels, near_apply(): call(body, struct((leaf_count, classes, leaf_size)), 'near_apply', 20, in...  16.8 us
    ppermute x21, waiting for transfers between devices, group(): lax.ppermute(pack, 'leaf', [(d, d ^ i << first_bit) for d in range(dev_co...  15.2 us
    pallas_call x2, Pallas kernels, downward(): call(body, tuple(out), 'downward', 30, in_specs=specs, out_specs=tuple([V...  9.14 us
    pallas_call x1, Pallas kernels, edge_build(): call(body, (pltpu.HBM(shape, BF16), struct((2 * reach, classes, leaf_size...  7.1 us
    pallas_call x1, Pallas kernels, front(): call(body, (struct((skel_size // 2, skel_size)), struct((pair_count, skel...  6.45 us
    pallas_call x1, Pallas kernels, last_step(): call(body, (struct(right_side.shape), struct(right_side.shape)), 'last_st...  5.82 us
  transfers between devices with their start and end apart: 25, of which 9 were waited for; matrix products, arithmetic and copies ran while one was open for 0% of the time, Pallas kernels for 42%

profile of v3, /device:TPU:0, one launch (start us, length us, event | category | flops | bytes accessed | tf_op | source)
XLA Modules:
  0.0 146.9 jit_solution(17760217318512909259)
XLA Ops:
  0.7 0.8 copy-done.9
  1.5 6.5 %front.1 = (f32[128,256]{1,0:T(8,128)S(1)}, bf16[7,256,256]{2,1,0:T(8,128)(2,1)S(1)}, bf16[7,256,256]{2,1,0:T(8,128)(2,1)S(1)}, f32[1536,128]{1,0:T(8,128)S(1)}, f32[1536,128]{1,0:T(8,128)S(1)}) custom-call(s32[1]{0:T(128)} %bitcast.dev_ref.refs_0_, f32[4096,128]{1,0:T(8,128)} %own_hbm.1, f32[64,4096]{1,0:T(8,128)} %refs_2_.1, s32[8,256]{1,0:T(8,128)S(1)} %copy-done.9, ...), custom_call_target="tpu_custom_call" | custom-call | tf_op jit(solution)/shard_map/front/pallas_call | solution.py:198
  8.0 2.4 %collective-permute-start.6 = (f32[1536,128]{1,0:T(8,128)S(1)}, f32[1536,128]{1,0:T(8,128)S(1)}, u32[]{:S(2)}, u32[]{:S(2)}) collective-permute-start(f32[1536,128]{1,0:T(8,128)S(1)} %get-tuple-element.105), channel_id=1, source_target_pairs={{0,1},{1,2},{2,3},{3,4},{4,5},{5,6},{6,7},{7,8},{8,9},{9,10},{10,1... | collective-permute-start | bytes 2359304 | tf_op jit(solution)/shard_map/ppermute | solution.py:844
  10.4 1.5 %collective-permute-start.7 = (f32[1536,128]{1,0:T(8,128)S(1)}, f32[1536,128]{1,0:T(8,128)S(1)}, u32[]{:S(2)}, u32[]{:S(2)}) collective-permute-start(f32[1536,128]{1,0:T(8,128)S(1)} %get-tuple-element.106), channel_id=1, source_target_pairs={{1,0},{2,1},{3,2},{4,3},{5,4},{6,5},{7,6},{8,7},{9,8},{10,9},{11,1... | collective-permute-start | bytes 2359304 | tf_op jit(solution)/shard_map/ppermute | solution.py:845
  11.9 0.7 copy-done.6
  12.6 11.0 %near_build.3 = (bf16[3,3,2,512,512]{4,3,2,1,0:T(8,128)(2,1)}, f32[8,64,512]{2,1,0:T(8,128)S(1)}) custom-call(f32[4096,128]{1,0:T(8,128)} %own_hbm.1, f32[64,4096]{1,0:T(8,128)} %refs_2_.1, s32[8,5]{1,0:T(8,128)S(1)} %copy-done.6), custom_call_target="tpu_custom_call" | custom-call | tf_op jit(solution)/shard_map/near_build/pallas_call | solution.py:305
  23.9 2.2 %upward.2 = (f32[192,256]{1,0:T(8,128)S(1)}, f32[14,64,256]{2,1,0:T(8,128)S(1)}) custom-call(s32[1]{0:T(128)} %bitcast.dev_ref.refs_0_, f32[64,4096]{1,0:T(8,128)S(1)} %copy-done, f32[128,256]{1,0:T(8,128)S(1)} %get-tuple-element.86.gram_ref, f32[8,512,256]{2,1,0:T(8,128)S(1)} %copy-done.1, f32[3,2,256,256]{3,2,1,0:T(8,128)S(1)} %slice.15.transfer_ref, ...), custom_call_target="tpu_custom_call" | custom-call | tf_op jit(solution)/shard_map/upward/pallas_call | solution.py:235
  26.0 3.2 %collective-permute-start = (f32[192,256]{1,0:T(8,128)S(1)}, f32[192,256]{1,0:T(8,128)S(1)}, u32[]{:S(2)}, u32[]{:S(2)}) collective-permute-start(f32[192,256]{1,0:T(8,128)S(1)} %get-tuple-element.93.refs_1_), channel_id=1, source_target_pairs={{0,1},{1,0},{2,3},{3,2},{4,5},{5,4},{6,7},{7,6},{8,9},{9,8},{10,11... | collective-permute-start | bytes 589832 | tf_op jit(solution)/shard_map/ppermute | solution.py:850
  29.3 1.7 %collective-permute-start.1 = (f32[192,256]{1,0:T(8,128)S(1)}, f32[192,256]{1,0:T(8,128)S(1)}, u32[]{:S(2)}, u32[]{:S(2)}) collective-permute-start(f32[192,256]{1,0:T(8,128)S(1)} %get-tuple-element.93.refs_1_), channel_id=1, source_target_pairs={{0,2},{1,3},{2,0},{3,1},{4,6},{5,7},{6,4},{7,5},{8,10},{9,11},{10,... | collective-permute-start | bytes 589832 | tf_op jit(solution)/shard_map/ppermute | solution.py:850
  31.0 7.2 %near_build.4 = (bf16[2,3,2,512,512]{4,3,2,1,0:T(8,128)(2,1)}, f32[8,64,512]{2,1,0:T(8,128)S(1)}) custom-call(f32[4096,128]{1,0:T(8,128)S(1)} %copy-done.2, f32[64,4096]{1,0:T(8,128)S(1)} %copy-done, s32[8,5]{1,0:T(8,128)S(1)} %copy-done.6, f32[8,64,512]{2,1,0:T(8,128)S(1)} %get-tuple-element.88.refs_0_), custom_call_target="tpu_custom_call" | custom-call | tf_op jit(solution)/shard_map/near_build/pallas_call | solution.py:305
  38.4 1.7 %collective-permute-done.2.refs_4_ = f32[192,256]{1,0:T(8,128)S(1)} collective-permute-done((f32[192,256]{1,0:T(8,128)S(1)}, f32[192,256]{1,0:T(8,128)S(1)}, u32[]{:S(2)}, u32[]{:S(2)}) %collective-permute-start.2) | collective-permute-done | bytes 196640 | tf_op jit(solution)/shard_map/ppermute | solution.py:850
  40.1 1.1 tree_stage.6
  41.2 2.8 %collective-permute-start.3 = (f32[192,256]{1,0:T(8,128)S(1)}, f32[192,256]{1,0:T(8,128)S(1)}, u32[]{:S(2)}, u32[]{:S(2)}) collective-permute-start(f32[192,256]{1,0:T(8,128)S(1)} %get-tuple-element.100.refs_1_), channel_id=1, source_target_pairs={{0,4},{1,5},{2,6},{3,7},{4,0},{5,1},{6,2},{7,3},{8,12},{9,13},{10,... | collective-permute-start | bytes 589832 | tf_op jit(solution)/shard_map/ppermute | solution.py:850
  44.0 1.6 %collective-permute-start.4 = (f32[192,256]{1,0:T(8,128)S(1)}, f32[192,256]{1,0:T(8,128)S(1)}, u32[]{:S(2)}, u32[]{:S(2)}) collective-permute-start(f32[192,256]{1,0:T(8,128)S(1)} %get-tuple-element.100.refs_1_), channel_id=1, source_target_pairs={{0,8},{1,9},{2,10},{3,11},{4,12},{5,13},{6,14},{7,15},{8,0},{9,1},... | collective-permute-start | bytes 589832 | tf_op jit(solution)/shard_map/ppermute | solution.py:850
  45.6 0.8 collective-permute-start.5
  46.4 7.1 %near_build.5 = (bf16[2,3,2,512,512]{4,3,2,1,0:T(8,128)(2,1)}, f32[8,64,512]{2,1,0:T(8,128)S(1)}) custom-call(f32[4096,128]{1,0:T(8,128)S(1)} %copy-done.2, f32[64,4096]{1,0:T(8,128)S(1)} %copy-done, s32[8,5]{1,0:T(8,128)S(1)} %copy-done.6, f32[8,64,512]{2,1,0:T(8,128)S(1)} %get-tuple-element.92.refs_0_), custom_call_target="tpu_custom_call" | custom-call | tf_op jit(solution)/shard_map/near_build/pallas_call | solution.py:305
  53.5 2.3 %collective-permute-done.5.refs_4_ = f32[192,256]{1,0:T(8,128)S(1)} collective-permute-done((f32[192,256]{1,0:T(8,128)S(1)}, f32[192,256]{1,0:T(8,128)S(1)}, u32[]{:S(2)}, u32[]{:S(2)}) %collective-permute-start.5) | collective-permute-done | bytes 196640 | tf_op jit(solution)/shard_map/ppermute | solution.py:850
  55.8 1.1 tree_stage.7
  56.9 2.8 %collective-permute-start.8 = (f32[192,256]{1,0:T(8,128)S(1)}, f32[192,256]{1,0:T(8,128)S(1)}, u32[]{:S(2)}, u32[]{:S(2)}) collective-permute-start(f32[192,256]{1,0:T(8,128)S(1)} %get-tuple-element.115.refs_1_), channel_id=1, source_target_pairs={{0,16},{1,17},{2,18},{3,19},{4,20},{5,21},{6,22},{7,23},{8,24},{9,... | collective-permute-start | bytes 589832 | tf_op jit(solution)/shard_map/ppermute | solution.py:850
  59.8 7.1 %edge_build.1 = (bf16[6,2,512,512]{3,2,1,0:T(8,128)(2,1)}, f32[4,64,512]{2,1,0:T(8,128)S(1)}) custom-call(f32[4096,128]{1,0:T(8,128)} %own_hbm.1, f32[1536,128]{1,0:T(8,128)S(1)} %collective-permute-done.6.left_ref, f32[1536,128]{1,0:T(8,128)S(1)} %collective-permute-done.7.right_ref, s32[8,5]{1,0:T(8,128)S(1)} %copy-done.6, s32[6,5]{1,0:T(8,128)S(1)} %copy-done.8), custom_call_target="tpu_custom_call" | custom-call | tf_op jit(solution)/shard_map/edge_build/pallas_call | solution.py:431
  66.9 1.5 %collective-permute-done.8.refs_2_ = f32[192,256]{1,0:T(8,128)S(1)} collective-permute-done((f32[192,256]{1,0:T(8,128)S(1)}, f32[192,256]{1,0:T(8,128)S(1)}, u32[]{:S(2)}, u32[]{:S(2)}) %collective-permute-start.8) | collective-permute-done | bytes 196640 | tf_op jit(solution)/shard_map/ppermute | solution.py:850
  68.4 0.9 tree_stage.8
  69.3 5.2 %downward.2 = (f32[64,4096]{1,0:T(8,128)S(1)}, f32[64,1024]{1,0:T(8,128)S(1)}, f32[64,1024]{1,0:T(8,128)S(1)}, f32[32,256]{1,0:T(8,128)S(1)}) custom-call(s32[1]{0:T(128)} %bitcast.dev_ref.refs_0_, f32[64,4096]{1,0:T(8,128)S(1)} %copy-done, f32[8,64,512]{2,1,0:T(8,128)S(1)} %get-tuple-element.99.refs_2_, f32[4,64,512]{2,1,0:T(8,128)S(1)} %get-tuple-element.109.refs_3_, ...), custom_call_target="tpu_custom_call" | custom-call | tf_op jit(solution)/shard_map/downward/pallas_call | solution.py:672
  74.5 2.1 %upward.3 = (f32[96,256]{1,0:T(8,128)S(1)}, f32[14,64,256]{2,1,0:T(8,128)S(1)}) custom-call(s32[1]{0:T(128)} %bitcast.dev_ref.refs_0_, f32[64,4096]{1,0:T(8,128)S(1)} %get-tuple-element.147.vector_ref.refs_1_.image_ref.refs_3_, f32[32,256]{1,0:T(8,128)S(1)} %get-tuple-element.125.gram_ref, f32[8,512,256]{2,1,0:T(8,128)S(1)} %copy-done.1, ...), custom_call_target="tpu_custom_call" | custom-call | tf_op jit(solution)/shard_map/upward/pallas_call | solution.py:235
  77.2 1.7 %collective-permute-start.9 = (f32[96,256]{1,0:T(8,128)S(1)}, f32[96,256]{1,0:T(8,128)S(1)}, u32[]{:S(2)}, u32[]{:S(2)}) collective-permute-start(f32[96,256]{1,0:T(8,128)S(1)} %get-tuple-element.129.refs_1_), channel_id=1, source_target_pairs={{0,1},{1,0},{2,3},{3,2},{4,5},{5,4},{6,7},{7,6},{8,9},{9,8},{10,11... | collective-permute-start | bytes 294920 | tf_op jit(solution)/shard_map/ppermute | solution.py:850
  78.9 1.9 %collective-permute-start.16 = (f32[64,1024]{1,0:T(8,128)S(1)}, f32[64,1024]{1,0:T(8,128)S(1)}, u32[]{:S(2)}, u32[]{:S(2)}) collective-permute-start(f32[64,1024]{1,0:T(8,128)S(1)} %get-tuple-element.144), channel_id=1, source_target_pairs={{0,1},{1,2},{2,3},{3,4},{4,5},{5,6},{6,7},{7,8},{8,9},{9,10},{10,1... | collective-permute-start | bytes 786440 | tf_op jit(solution)/shard_map/ppermute | solution.py:844
  80.8 1.3 collective-permute-start.17
  82.1 6.5 %near_apply.3.refs_0_ = f32[8,64,512]{2,1,0:T(8,128)S(1)} custom-call(bf16[3,3,2,512,512]{4,3,2,1,0:T(8,128)(2,1)} %get-tuple-element.127.tile_hbm, f32[64,4096]{1,0:T(8,128)S(1)} %get-tuple-element.147.vector_ref.refs_1_.image_ref.refs_3_, s32[8,5]{1,0:T(8,128)S(1)} %copy-done.7), custom_call_target="tpu_custom_call" | custom-call | tf_op jit(solution)/shard_map/near_apply/pallas_call | solution.py:350
  89.3 3.8 %collective-permute-start.12 = (f32[96,256]{1,0:T(8,128)S(1)}, f32[96,256]{1,0:T(8,128)S(1)}, u32[]{:S(2)}, u32[]{:S(2)}) collective-permute-start(f32[96,256]{1,0:T(8,128)S(1)} %get-tuple-element.136.refs_1_), channel_id=1, source_target_pairs={{0,4},{1,5},{2,6},{3,7},{4,0},{5,1},{6,2},{7,3},{8,12},{9,13},{10,... | collective-permute-start | bytes 294920 | tf_op jit(solution)/shard_map/ppermute | solution.py:850
  93.1 1.0 collective-permute-start.13
  94.1 1.4 collective-permute-start.14
  95.5 5.2 %near_apply.4.refs_0_ = f32[8,64,512]{2,1,0:T(8,128)S(1)} custom-call(bf16[2,3,2,512,512]{4,3,2,1,0:T(8,128)(2,1)} %get-tuple-element.134.tile_hbm, f32[64,4096]{1,0:T(8,128)S(1)} %get-tuple-element.147.vector_ref.refs_1_.image_ref.refs_3_, s32[8,5]{1,0:T(8,128)S(1)} %copy-done.7, f32[8,64,512]{2,1,0:T(8,128)S(1)} %near_apply.3.refs_0_), custom_call_target="tpu_custom_call" | custom-call | tf_op jit(solution)/shard_map/near_apply/pallas_call | solution.py:350
  100.7 0.6 tree_stage.10
  101.3 3.4 %collective-permute-start.15 = (f32[96,256]{1,0:T(8,128)S(1)}, f32[96,256]{1,0:T(8,128)S(1)}, u32[]{:S(2)}, u32[]{:S(2)}) collective-permute-start(f32[96,256]{1,0:T(8,128)S(1)} %get-tuple-element.150.refs_1_), channel_id=1, source_target_pairs={{0,16},{1,17},{2,18},{3,19},{4,20},{5,21},{6,22},{7,23},{8,24},{9,... | collective-permute-start | bytes 294920 | tf_op jit(solution)/shard_map/ppermute | solution.py:850
  104.7 5.1 %near_apply.5.refs_2_ = f32[8,64,512]{2,1,0:T(8,128)S(1)} custom-call(bf16[2,3,2,512,512]{4,3,2,1,0:T(8,128)(2,1)} %get-tuple-element.146.tile_hbm, f32[64,4096]{1,0:T(8,128)S(1)} %get-tuple-element.147.vector_ref.refs_1_.image_ref.refs_3_, s32[8,5]{1,0:T(8,128)S(1)} %copy-done.7, f32[8,64,512]{2,1,0:T(8,128)S(1)} %near_apply.4.refs_0_), custom_call_target="tpu_custom_call" | custom-call | tf_op jit(solution)/shard_map/near_apply/pallas_call | solution.py:350
  109.9 4.2 %edge_apply.1.refs_3_ = f32[4,64,512]{2,1,0:T(8,128)S(1)} custom-call(bf16[6,2,512,512]{3,2,1,0:T(8,128)(2,1)} %get-tuple-element.141.tile_hbm, f32[64,1024]{1,0:T(8,128)S(1)} %collective-permute-done.16.lv_ref, f32[64,1024]{1,0:T(8,128)S(1)} %collective-permute-done.17.rv_ref, s32[8,5]{1,0:T(8,128)S(1)} %copy-done.7, s32[6,5]{1,0:T(8,128)S(1)} %copy-done.8), custom_call_target="tpu_custom_call" | custom-call | tf_op jit(solution)/shard_map/edge_apply/pallas_call | solution.py:475
  114.2 3.9 %downward.3.second_ref = f32[64,4096]{1,0:T(8,128)S(1)} custom-call(s32[1]{0:T(128)} %bitcast.dev_ref.refs_0_, f32[64,4096]{1,0:T(8,128)S(1)} %get-tuple-element.147.vector_ref.refs_1_.image_ref.refs_3_, f32[8,64,512]{2,1,0:T(8,128)S(1)} %near_apply.5.refs_2_, f32[4,64,512]{2,1,0:T(8,128)S(1)} %edge_apply.1.refs_3_, f32[8,512,256]{2,1,0:T(8,128)S(1)} %copy-done.1, ...), custom_call_target="tpu_custom_call" | custom-call | tf_op jit(solution)/shard_map/downward/pallas_call | solution.py:672
  118.1 4.9 %first_step.1 = (f32[64,4096]{1,0:T(8,128)S(1)}, f32[64,4096]{1,0:T(8,128)S(1)}, f32[64,256]{1,0:T(8,128)S(1)}, f32[64,64]{1,0:T(8,128)S(1)}, f32[64,128]{1,0:T(8,128)S(1)}) custom-call(f32[96,256]{1,0:T(8,128)S(1)} %get-tuple-element.152.gram_in, f32[64,4096]{1,0:T(8,128)S(1)} %copy-done, ...), custom_call_target="tpu_custom_call" | custom-call | tf_op jit(solution)/shard_map/first_step/pallas_call | solution.py:758
  123.2 1.8 %collective-permute-start.20 = (f32[64,256]{1,0:T(8,128)S(1)}, f32[64,256]{1,0:T(8,128)S(1)}, u32[]{:S(2)}, u32[]{:S(2)}) collective-permute-start(f32[64,256]{1,0:T(8,128)S(1)} %get-tuple-element.164), channel_id=1, source_target_pairs={{0,3},{1,2},{2,1},{3,0},{4,7},{5,6},{6,5},{7,4},{8,11},{9,10},{10,... | collective-permute-start | bytes 196616 | tf_op jit(solution)/shard_map/ppermute | solution.py:850
  125.0 2.7 %between.1 = (f32[64,64]{1,0:T(8,128)S(1)}, f32[64,4096]{1,0:T(8,128)S(1)}) custom-call(f32[64,128]{1,0:T(8,128)S(1)} %get-tuple-element.157.both_ref, f32[64,64]{1,0:T(8,128)S(1)} %get-tuple-element.159.alpha_ref, f32[64,4096]{1,0:T(8,128)S(1)} %copy-done), custom_call_target="tpu_custom_call" | custom-call | tf_op jit(solution)/shard_map/between/pallas_call | solution.py:786
  128.5 1.0 collective-permute-start.21
  129.5 1.2 collective-permute-start.22
  130.7 1.4 collective-permute-start.23
  132.0 0.9 collective-permute-done.21
  132.9 0.8 collective-permute-done.22
  133.7 2.1 %collective-permute-done.23 = f32[64,256]{1,0:T(8,128)S(1)} collective-permute-done((f32[64,256]{1,0:T(8,128)S(1)}, f32[64,256]{1,0:T(8,128)S(1)}, u32[]{:S(2)}, u32[]{:S(2)}) %collective-permute-start.23) | collective-permute-done | bytes 65568 | tf_op jit(solution)/shard_map/ppermute | solution.py:850
  135.9 5.1 %collective-permute-done.24.refs_1_ = f32[64,256]{1,0:T(8,128)S(1)} collective-permute-done((f32[64,256]{1,0:T(8,128)S(1)}, f32[64,256]{1,0:T(8,128)S(1)}, u32[]{:S(2)}, u32[]{:S(2)}) %collective-permute-start.24) | collective-permute-done | bytes 65568 | tf_op jit(solution)/shard_map/ppermute | solution.py:850
  141.1 5.8 %last_step.1 = (f32[64,4096]{1,0:T(8,128)}, f32[64,4096]{1,0:T(8,128)}) custom-call(f32[64,128]{1,0:T(8,128)S(1)} %get-tuple-element.157.both_ref, f32[64,64]{1,0:T(8,128)S(1)} %get-tuple-element.162.inverse_ref, f32[64,4096]{1,0:T(8,128)S(1)} %get-tuple-element.163.moved_ref, f32[64,256]{1,0:T(8,128)S(1)} %add_add_fusion.refs_0_, ...), custom_call_target="tpu_custom_call" | custom-call | tf_op jit(solution)/shard_map/last_step/pallas_call | solution.py:823
  (49 shorter events, 2.7 us)
Async XLA Ops:
  0.6 23.0 %copy-start.4 = (f32[7,2,256,256]{3,2,1,0:T(8,128)S(1)}, f32[7,2,256,256]{3,2,1,0:T(8,128)}, u32[]{:S(2)}) copy-start(f32[7,2,256,256]{3,2,1,0:T(8,128)} %refs_5_.13) | copy-start | bytes 11010052
  0.6 0.8 copy-start.9
  1.5 22.3 %copy-start = (f32[64,4096]{1,0:T(8,128)S(1)}, f32[64,4096]{1,0:T(8,128)}, u32[]{:S(2)}) copy-start(f32[64,4096]{1,0:T(8,128)} %refs_2_.1) | copy-start | bytes 3145732
  1.5 22.3 %copy-start.1 = (f32[8,512,256]{2,1,0:T(8,128)S(1)}, f32[8,512,256]{2,1,0:T(8,128)}, u32[]{:S(2)}) copy-start(f32[8,512,256]{2,1,0:T(8,128)} %refs_4_.3) | copy-start | bytes 12582916
  1.5 22.3 %copy-start.3 = (f32[510,256]{1,0:T(8,128)S(1)}, f32[510,256]{1,0:T(8,128)}, u32[]{:S(2)}) copy-start(f32[510,256]{1,0:T(8,128)} %refs_9_.3) | copy-start | bytes 1566724
  8.0 51.8 %collective-permute-start.6 = (f32[1536,128]{1,0:T(8,128)S(1)}, f32[1536,128]{1,0:T(8,128)S(1)}, u32[]{:S(2)}, u32[]{:S(2)}) collective-permute-start(f32[1536,128]{1,0:T(8,128)S(1)} %get-tuple-element.105), channel_id=1, source_target_pairs={{0,1},{1,2},{2,3},{3,4},{4,5},{5,6},{6,7},{7,8},{8,9},{9,10},{10,1... | collective-permute-start | bytes 2359304 | tf_op jit(solution)/shard_map/ppermute | solution.py:844
  10.4 49.3 %collective-permute-start.7 = (f32[1536,128]{1,0:T(8,128)S(1)}, f32[1536,128]{1,0:T(8,128)S(1)}, u32[]{:S(2)}, u32[]{:S(2)}) collective-permute-start(f32[1536,128]{1,0:T(8,128)S(1)} %get-tuple-element.106), channel_id=1, source_target_pairs={{1,0},{2,1},{3,2},{4,3},{5,4},{6,5},{7,6},{8,7},{9,8},{10,9},{11,1... | collective-permute-start | bytes 2359304 | tf_op jit(solution)/shard_map/ppermute | solution.py:845
  11.9 0.7 copy-start.6
  23.8 7.1 %copy-start.2 = (f32[4096,128]{1,0:T(8,128)S(1)}, f32[4096,128]{1,0:T(8,128)}, u32[]{:S(2)}) copy-start(f32[4096,128]{1,0:T(8,128)} %own_hbm.1) | copy-start | bytes 6291460
  26.0 14.0 %copy-start.5 = (s32[254,256]{1,0:T(8,128)S(1)}, s32[254,256]{1,0:T(8,128)}, u32[]{:S(2)}) copy-start(s32[254,256]{1,0:T(8,128)} %refs_5_.9) | copy-start | bytes 780292
  26.0 12.3 %collective-permute-start = (f32[192,256]{1,0:T(8,128)S(1)}, f32[192,256]{1,0:T(8,128)S(1)}, u32[]{:S(2)}, u32[]{:S(2)}) collective-permute-start(f32[192,256]{1,0:T(8,128)S(1)} %get-tuple-element.93.refs_1_), channel_id=1, source_target_pairs={{0,1},{1,0},{2,3},{3,2},{4,5},{5,4},{6,7},{7,6},{8,9},{9,8},{10,11... | collective-permute-start | bytes 589832 | tf_op jit(solution)/shard_map/ppermute | solution.py:850
  29.3 9.1 %collective-permute-start.1 = (f32[192,256]{1,0:T(8,128)S(1)}, f32[192,256]{1,0:T(8,128)S(1)}, u32[]{:S(2)}, u32[]{:S(2)}) collective-permute-start(f32[192,256]{1,0:T(8,128)S(1)} %get-tuple-element.93.refs_1_), channel_id=1, source_target_pairs={{0,2},{1,3},{2,0},{3,1},{4,6},{5,7},{6,4},{7,5},{8,10},{9,11},{10,... | collective-permute-start | bytes 589832 | tf_op jit(solution)/shard_map/ppermute | solution.py:850
  30.9 9.1 %collective-permute-start.2 = (f32[192,256]{1,0:T(8,128)S(1)}, f32[192,256]{1,0:T(8,128)S(1)}, u32[]{:S(2)}, u32[]{:S(2)}) collective-permute-start(f32[192,256]{1,0:T(8,128)S(1)} %get-tuple-element.93.refs_1_), channel_id=1, source_target_pairs={{0,3},{1,2},{2,1},{3,0},{4,7},{5,6},{6,5},{7,4},{8,11},{9,10},{10,... | collective-permute-start | bytes 589832 | tf_op jit(solution)/shard_map/ppermute | solution.py:850
  41.2 18.6 %copy-start.8 = (s32[6,5]{1,0:T(8,128)S(1)}, s32[6,5]{1,0:T(8,128)}, u32[]{:S(2)}) copy-start(s32[6,5]{1,0:T(8,128)} %constant.6.clone.border_ref) | copy-start | bytes 364
  41.2 12.3 %collective-permute-start.3 = (f32[192,256]{1,0:T(8,128)S(1)}, f32[192,256]{1,0:T(8,128)S(1)}, u32[]{:S(2)}, u32[]{:S(2)}) collective-permute-start(f32[192,256]{1,0:T(8,128)S(1)} %get-tuple-element.100.refs_1_), channel_id=1, source_target_pairs={{0,4},{1,5},{2,6},{3,7},{4,0},{5,1},{6,2},{7,3},{8,12},{9,13},{10,... | collective-permute-start | bytes 589832 | tf_op jit(solution)/shard_map/ppermute | solution.py:850
  44.0 9.5 %collective-permute-start.4 = (f32[192,256]{1,0:T(8,128)S(1)}, f32[192,256]{1,0:T(8,128)S(1)}, u32[]{:S(2)}, u32[]{:S(2)}) collective-permute-start(f32[192,256]{1,0:T(8,128)S(1)} %get-tuple-element.100.refs_1_), channel_id=1, source_target_pairs={{0,8},{1,9},{2,10},{3,11},{4,12},{5,13},{6,14},{7,15},{8,0},{9,1},... | collective-permute-start | bytes 589832 | tf_op jit(solution)/shard_map/ppermute | solution.py:850
  45.6 10.2 %collective-permute-start.5 = (f32[192,256]{1,0:T(8,128)S(1)}, f32[192,256]{1,0:T(8,128)S(1)}, u32[]{:S(2)}, u32[]{:S(2)}) collective-permute-start(f32[192,256]{1,0:T(8,128)S(1)} %get-tuple-element.100.refs_1_), channel_id=1, source_target_pairs={{0,12},{1,13},{2,14},{3,15},{4,8},{5,9},{6,10},{7,11},{8,4},{9,5},... | collective-permute-start | bytes 589832 | tf_op jit(solution)/shard_map/ppermute | solution.py:850
  56.9 11.5 %collective-permute-start.8 = (f32[192,256]{1,0:T(8,128)S(1)}, f32[192,256]{1,0:T(8,128)S(1)}, u32[]{:S(2)}, u32[]{:S(2)}) collective-permute-start(f32[192,256]{1,0:T(8,128)S(1)} %get-tuple-element.115.refs_1_), channel_id=1, source_target_pairs={{0,16},{1,17},{2,18},{3,19},{4,20},{5,21},{6,22},{7,23},{8,24},{9,... | collective-permute-start | bytes 589832 | tf_op jit(solution)/shard_map/ppermute | solution.py:850
  74.5 7.6 %copy-start.7 = (s32[8,5]{1,0:T(8,128)S(1)}, s32[8,5]{1,0:T(8,128)}, u32[]{:S(2)}) copy-start(s32[8,5]{1,0:T(8,128)} %mask_ref.15) | copy-start | bytes 484
  76.7 11.9 %collective-permute-start.10 = (f32[96,256]{1,0:T(8,128)S(1)}, f32[96,256]{1,0:T(8,128)S(1)}, u32[]{:S(2)}, u32[]{:S(2)}) collective-permute-start(f32[96,256]{1,0:T(8,128)S(1)} %get-tuple-element.129.refs_1_), channel_id=1, source_target_pairs={{0,2},{1,3},{2,0},{3,1},{4,6},{5,7},{6,4},{7,5},{8,10},{9,11},{10,... | collective-permute-start | bytes 294920 | tf_op jit(solution)/shard_map/ppermute | solution.py:850
  76.8 11.8 %collective-permute-start.11 = (f32[96,256]{1,0:T(8,128)S(1)}, f32[96,256]{1,0:T(8,128)S(1)}, u32[]{:S(2)}, u32[]{:S(2)}) collective-permute-start(f32[96,256]{1,0:T(8,128)S(1)} %get-tuple-element.129.refs_1_), channel_id=1, source_target_pairs={{0,3},{1,2},{2,1},{3,0},{4,7},{5,6},{6,5},{7,4},{8,11},{9,10},{10,... | collective-permute-start | bytes 294920 | tf_op jit(solution)/shard_map/ppermute | solution.py:850
  77.2 11.4 %collective-permute-start.9 = (f32[96,256]{1,0:T(8,128)S(1)}, f32[96,256]{1,0:T(8,128)S(1)}, u32[]{:S(2)}, u32[]{:S(2)}) collective-permute-start(f32[96,256]{1,0:T(8,128)S(1)} %get-tuple-element.129.refs_1_), channel_id=1, source_target_pairs={{0,1},{1,0},{2,3},{3,2},{4,5},{5,4},{6,7},{7,6},{8,9},{9,8},{10,11... | collective-permute-start | bytes 294920 | tf_op jit(solution)/shard_map/ppermute | solution.py:850
  78.9 30.9 %collective-permute-start.16 = (f32[64,1024]{1,0:T(8,128)S(1)}, f32[64,1024]{1,0:T(8,128)S(1)}, u32[]{:S(2)}, u32[]{:S(2)}) collective-permute-start(f32[64,1024]{1,0:T(8,128)S(1)} %get-tuple-element.144), channel_id=1, source_target_pairs={{0,1},{1,2},{2,3},{3,4},{4,5},{5,6},{6,7},{7,8},{8,9},{9,10},{10,1... | collective-permute-start | bytes 786440 | tf_op jit(solution)/shard_map/ppermute | solution.py:844
  80.8 29.0 %collective-permute-start.17 = (f32[64,1024]{1,0:T(8,128)S(1)}, f32[64,1024]{1,0:T(8,128)S(1)}, u32[]{:S(2)}, u32[]{:S(2)}) collective-permute-start(f32[64,1024]{1,0:T(8,128)S(1)} %get-tuple-element.145), channel_id=1, source_target_pairs={{1,0},{2,1},{3,2},{4,3},{5,4},{6,5},{7,6},{8,7},{9,8},{10,9},{11,1... | collective-permute-start | bytes 786440 | tf_op jit(solution)/shard_map/ppermute | solution.py:845
  89.3 11.4 %collective-permute-start.12 = (f32[96,256]{1,0:T(8,128)S(1)}, f32[96,256]{1,0:T(8,128)S(1)}, u32[]{:S(2)}, u32[]{:S(2)}) collective-permute-start(f32[96,256]{1,0:T(8,128)S(1)} %get-tuple-element.136.refs_1_), channel_id=1, source_target_pairs={{0,4},{1,5},{2,6},{3,7},{4,0},{5,1},{6,2},{7,3},{8,12},{9,13},{10,... | collective-permute-start | bytes 294920 | tf_op jit(solution)/shard_map/ppermute | solution.py:850
  93.1 7.6 %collective-permute-start.13 = (f32[96,256]{1,0:T(8,128)S(1)}, f32[96,256]{1,0:T(8,128)S(1)}, u32[]{:S(2)}, u32[]{:S(2)}) collective-permute-start(f32[96,256]{1,0:T(8,128)S(1)} %get-tuple-element.136.refs_1_), channel_id=1, source_target_pairs={{0,8},{1,9},{2,10},{3,11},{4,12},{5,13},{6,14},{7,15},{8,0},{9,1},... | collective-permute-start | bytes 294920 | tf_op jit(solution)/shard_map/ppermute | solution.py:850
  94.1 6.6 %collective-permute-start.14 = (f32[96,256]{1,0:T(8,128)S(1)}, f32[96,256]{1,0:T(8,128)S(1)}, u32[]{:S(2)}, u32[]{:S(2)}) collective-permute-start(f32[96,256]{1,0:T(8,128)S(1)} %get-tuple-element.136.refs_1_), channel_id=1, source_target_pairs={{0,12},{1,13},{2,14},{3,15},{4,8},{5,9},{6,10},{7,11},{8,4},{9,5},... | collective-permute-start | bytes 294920 | tf_op jit(solution)/shard_map/ppermute | solution.py:850
  101.3 12.9 %collective-permute-start.15 = (f32[96,256]{1,0:T(8,128)S(1)}, f32[96,256]{1,0:T(8,128)S(1)}, u32[]{:S(2)}, u32[]{:S(2)}) collective-permute-start(f32[96,256]{1,0:T(8,128)S(1)} %get-tuple-element.150.refs_1_), channel_id=1, source_target_pairs={{0,16},{1,17},{2,18},{3,19},{4,20},{5,21},{6,22},{7,23},{8,24},{9,... | collective-permute-start | bytes 294920 | tf_op jit(solution)/shard_map/ppermute | solution.py:850
  123.0 4.6 %collective-permute-start.18 = (f32[64,256]{1,0:T(8,128)S(1)}, f32[64,256]{1,0:T(8,128)S(1)}, u32[]{:S(2)}, u32[]{:S(2)}) collective-permute-start(f32[64,256]{1,0:T(8,128)S(1)} %get-tuple-element.164), channel_id=1, source_target_pairs={{0,1},{1,0},{2,3},{3,2},{4,5},{5,4},{6,7},{7,6},{8,9},{9,8},{10,11... | collective-permute-start | bytes 196616 | tf_op jit(solution)/shard_map/ppermute | solution.py:850
  123.1 5.0 %collective-permute-start.19 = (f32[64,256]{1,0:T(8,128)S(1)}, f32[64,256]{1,0:T(8,128)S(1)}, u32[]{:S(2)}, u32[]{:S(2)}) collective-permute-start(f32[64,256]{1,0:T(8,128)S(1)} %get-tuple-element.164), channel_id=1, source_target_pairs={{0,2},{1,3},{2,0},{3,1},{4,6},{5,7},{6,4},{7,5},{8,10},{9,11},{10,... | collective-permute-start | bytes 196616 | tf_op jit(solution)/shard_map/ppermute | solution.py:850
  123.2 5.3 %collective-permute-start.20 = (f32[64,256]{1,0:T(8,128)S(1)}, f32[64,256]{1,0:T(8,128)S(1)}, u32[]{:S(2)}, u32[]{:S(2)}) collective-permute-start(f32[64,256]{1,0:T(8,128)S(1)} %get-tuple-element.164), channel_id=1, source_target_pairs={{0,3},{1,2},{2,1},{3,0},{4,7},{5,6},{6,5},{7,4},{8,11},{9,10},{10,... | collective-permute-start | bytes 196616 | tf_op jit(solution)/shard_map/ppermute | solution.py:850
  128.5 4.4 %collective-permute-start.21 = (f32[64,256]{1,0:T(8,128)S(1)}, f32[64,256]{1,0:T(8,128)S(1)}, u32[]{:S(2)}, u32[]{:S(2)}) collective-permute-start(f32[64,256]{1,0:T(8,128)S(1)} %add_add_fusion.1), channel_id=1, source_target_pairs={{0,4},{1,5},{2,6},{3,7},{4,0},{5,1},{6,2},{7,3},{8,12},{9,13},{10,... | collective-permute-start | bytes 196616 | tf_op jit(solution)/shard_map/ppermute | solution.py:850
  129.5 4.3 %collective-permute-start.22 = (f32[64,256]{1,0:T(8,128)S(1)}, f32[64,256]{1,0:T(8,128)S(1)}, u32[]{:S(2)}, u32[]{:S(2)}) collective-permute-start(f32[64,256]{1,0:T(8,128)S(1)} %add_add_fusion.1), channel_id=1, source_target_pairs={{0,8},{1,9},{2,10},{3,11},{4,12},{5,13},{6,14},{7,15},{8,0},{9,1},... | collective-permute-start | bytes 196616 | tf_op jit(solution)/shard_map/ppermute | solution.py:850
  130.7 5.2 %collective-permute-start.23 = (f32[64,256]{1,0:T(8,128)S(1)}, f32[64,256]{1,0:T(8,128)S(1)}, u32[]{:S(2)}, u32[]{:S(2)}) collective-permute-start(f32[64,256]{1,0:T(8,128)S(1)} %add_add_fusion.1), channel_id=1, source_target_pairs={{0,12},{1,13},{2,14},{3,15},{4,8},{5,9},{6,10},{7,11},{8,4},{9,5},... | collective-permute-start | bytes 196616 | tf_op jit(solution)/shard_map/ppermute | solution.py:850
  135.8 5.2 %collective-permute-start.24 = (f32[64,256]{1,0:T(8,128)S(1)}, f32[64,256]{1,0:T(8,128)S(1)}, u32[]{:S(2)}, u32[]{:S(2)}) collective-permute-start(f32[64,256]{1,0:T(8,128)S(1)} %add_add_fusion.refs_0_), channel_id=1, source_target_pairs={{0,16},{1,17},{2,18},{3,19},{4,20},{5,21},{6,22},{7,23},{8,24},{9,... | collective-permute-start | bytes 196616 | tf_op jit(solution)/shard_map/ppermute | solution.py:850
